TPU v7x, 32 devices: a whole 2x2x4 slice. The times are simulated.
32 devices in a mesh: dp: 4 (over x, core), mp: 8 (over z, y).
Axes of the slice: x: 2, y: 2, z: 4, core: 2. Of those that a mesh axis runs over, the one named last changes fastest.
Arguments:
- tokens: bfloat16 [25088, 512], P(('dp', 'mp')), may hold values from -6 to 6
- cotangent: bfloat16 [25088, 512], P(('dp', 'mp')), may hold values from -6 to 6
- image_counts: int32 [4], replicated, may hold values from 1 to 32, 96 in all
- params: float32 [8, 394324], P('mp', 'dp'), may hold values from -4 to 4, as said below
- moment_one: float32 [8, 394324], P('mp', 'dp'), may hold values from -96 to 96
- moment_two: float32 [8, 394324], P('mp', 'dp'), may hold values from 0 to 40, as said below
Outputs:
- output: bfloat16 [25088, 512], P(('dp', 'mp'))
- input_grad: bfloat16 [25088, 512], P(('dp', 'mp'))
- param_grad: float32 [8, 394324], P('mp', 'dp')
- new_params: float32 [8, 394324], P('mp', 'dp')
- revised_first_mean: float32 [8, 394324], P('mp', 'dp')
- new_moment_two: float32 [8, 394324], P('mp', 'dp')
Inputs may be any that keep to these rules, and one draw needn't show every extreme that they name: `image_counts`: the live images of a group are its first slots; the counts add up to three quarters of all slots, rounded down, and one group is full. `params`: laid out as its meaning says. `moment_two`: Positive, laid out as params.
All inputs are finite; a program needn't handle non-finite values.
Results may differ from a plain program's by a relative error of at most 0.022.
Values may be sent and summed in bfloat16 or wider, within the bound.
A program may use at most 192 MiB of HBM per device.

v0:
```python
import math

import jax
import jax.numpy as jnp
from jax import lax
from jax.sharding import PartitionSpec as P

C = 512
FF = 2048
HD = 32
WIN = 7
MAP = 14
SHIFT = 3


norm_eps = 1e-05
mask_fill = -100.0
learn_rate = 0.05
beta_one = 0.9
second_decay_rate = 0.999
adam_eps = 1e-08
weight_decay = 0.05
adam_step = 2.0
small_labels = ["norm1_gain", "norm1_bias", "proj_bias", "norm2_gain", "norm2_bias", "fc2_bias"]


def combine_rule(spec, left, right):
    return jnp.einsum(spec, left, right, preferred_element_type=jnp.float32)


def contract_rows(left, right):
    return lax.dot_general(
        left, right, (((0,), (0,)), ((), ())), preferred_element_type=jnp.float32
    )


def contract_cols(left, right):
    return lax.dot_general(
        left, right, (((1,), (1,)), ((), ())), preferred_element_type=jnp.float32
    )


def segment_shapes(width_rank, hidden_rank):
    span = 2 * WIN - 1
    return [
        ("qkv_weight", (C, 3 * width_rank)),
        ("proj_weight", (width_rank, C)),
        ("fc1_weight", (C, hidden_rank)),
        ("fc2_weight", (hidden_rank, C)),
        ("norm1_gain", (width_rank,)),
        ("norm1_bias", (width_rank,)),
        ("query_bias", (width_rank,)),
        ("value_bias", (width_rank,)),
        ("proj_bias", (width_rank,)),
        ("norm2_gain", (width_rank,)),
        ("norm2_bias", (width_rank,)),
        ("fc1_bias", (hidden_rank,)),
        ("fc2_bias", (width_rank,)),
        ("table", (span * span, width_rank // HD)),
    ]


def unpack(flat, width_rank, hidden_rank):
    groups = flat.shape[0]
    owner_pieces = {}
    offset = 0
    for label, shape in segment_shapes(width_rank, hidden_rank):
        amount = math.prod(shape)
        owner_pieces[label] = flat[:, offset : offset + amount].reshape((groups,) + shape)
        offset = offset + amount
    return owner_pieces


def pack(owner_pieces, width_rank, hidden_rank, length):
    groups = owner_pieces["qkv_weight"].shape[0]
    parts = [
        owner_pieces[label].reshape(groups, -1)
        for label, shape in segment_shapes(width_rank, hidden_rank)
    ]
    used = sum((part.shape[1] for part in parts))
    parts.append(jnp.zeros((groups, length - used), jnp.float32))
    return jnp.concatenate(parts, axis=1)


def window_tables():
    side = MAP // WIN
    span = 2 * WIN - 1
    inner = jnp.arange(WIN * WIN, dtype=jnp.int32)
    row_in = inner // WIN
    col_in = inner % WIN
    offset_index = (row_in[:, None] - row_in[None, :] + WIN - 1) * span + (
        col_in[:, None] - col_in[None, :] + WIN - 1
    )
    one_hot = (
        offset_index.reshape(-1)[:, None] == jnp.arange(span * span, dtype=jnp.int32)[None, :]
    ).astype(jnp.float32)
    window_ids = jnp.arange(side * side, dtype=jnp.int32)
    row_coord = (window_ids // side)[:, None] * WIN + row_in[None, :]
    col_coord = (window_ids % side)[:, None] * WIN + col_in[None, :]

    def region(coord):
        return (coord >= MAP - WIN).astype(jnp.int32) + (coord >= MAP - SHIFT).astype(jnp.int32)

    region_ids = region(row_coord) * 3 + region(col_coord)
    mask = jnp.where(region_ids[:, :, None] == region_ids[:, None, :], 0.0, mask_fill).astype(
        jnp.float32
    )
    return (one_hot, mask)


def to_windows(raster):
    width = raster.shape[-1]
    side = MAP // WIN
    grid = raster.reshape(-1, MAP, MAP, width)
    grid = jnp.roll(grid, (-SHIFT, -SHIFT), (1, 2))
    grid = grid.reshape(-1, side, WIN, side, WIN, width).transpose(0, 1, 3, 2, 4, 5)
    return grid.reshape(-1, side * side, WIN * WIN, width)


def from_windows(blocks):
    width = blocks.shape[-1]
    side = MAP // WIN
    grid = blocks.reshape(-1, side, side, WIN, WIN, width).transpose(0, 1, 3, 2, 4, 5)
    grid = grid.reshape(-1, MAP, MAP, width)
    grid = jnp.roll(grid, (SHIFT, SHIFT), (1, 2))
    return grid.reshape(-1, width)


def norm_stats(values):
    center = jnp.mean(values, axis=1, keepdims=True)
    spread = jnp.mean(jnp.square(values - center), axis=1, keepdims=True)
    return (center, lax.rsqrt(spread + norm_eps))


def norm_back(scaled, unit, scale):
    return scale * (
        scaled
        - jnp.mean(scaled, axis=1, keepdims=True)
        - unit * jnp.mean(scaled * unit, axis=1, keepdims=True)
    )


def gelu(values):
    return values * (0.5 * (1.0 + lax.erf(values * (1.0 / math.sqrt(2.0)))))


def gelu_derivative(values):
    cdf = 0.5 * (1.0 + lax.erf(values * (1.0 / math.sqrt(2.0))))
    density = jnp.exp(-0.5 * values * values) * (1.0 / math.sqrt(2.0 * math.pi))
    return cdf + values * density


def qkv_finish(raw, query_bias, value_bias):
    shift = jnp.stack([query_bias, jnp.zeros_like(query_bias), value_bias], axis=1)
    factor = jnp.array([HD ** (-0.5), 1.0, 1.0], jnp.float32)[None, None, :, None]
    return ((raw + shift[None]) * factor).astype(jnp.bfloat16)


def window_scores(blocks, table, one_hot, mask):
    heads = table.shape[1]
    size = WIN * WIN
    bias = (
        jnp.dot(one_hot, table, precision=lax.Precision.HIGHEST)
        .reshape(size, size, heads)
        .transpose(2, 0, 1)
    )
    scores = combine_rule("nwphd,nwqhd->nwhpq", blocks[:, :, :, :, 0, :], blocks[:, :, :, :, 1, :])
    return scores + bias[None, None] + mask[None, :, None]


def attend_forward(projected, table, one_hot, mask):
    heads = table.shape[1]
    blocks = to_windows(projected)
    count, wins = (blocks.shape[0], blocks.shape[1])
    blocks = blocks.reshape(count, wins, WIN * WIN, heads, 3, HD)
    scores = window_scores(blocks, table, one_hot, mask)
    top = jnp.max(scores, axis=-1, keepdims=True)
    log_total = top + jnp.log(jnp.sum(jnp.exp(scores - top), axis=-1, keepdims=True))
    soft = jnp.exp(scores - log_total).astype(jnp.bfloat16)
    mixed = combine_rule("nwhpq,nwqhd->nwphd", soft, blocks[:, :, :, :, 2, :]).astype(jnp.bfloat16)
    return (from_windows(mixed.reshape(count, wins, WIN * WIN, heads * HD)), log_total)


def attend_backward(projected, grad_mixed, table, log_total, one_hot, mask):
    heads = table.shape[1]
    size = WIN * WIN
    blocks = to_windows(projected)
    count, wins = (blocks.shape[0], blocks.shape[1])
    blocks = blocks.reshape(count, wins, size, heads, 3, HD)
    scores = window_scores(blocks, table, one_hot, mask)
    soft = jnp.exp(scores - log_total)
    incoming = to_windows(grad_mixed).reshape(count, wins, size, heads, HD)
    grad_value = combine_rule("nwhpq,nwphd->nwqhd", soft.astype(jnp.bfloat16), incoming)
    grad_soft = combine_rule("nwphd,nwqhd->nwhpq", incoming, blocks[:, :, :, :, 2, :])
    inner = jnp.sum(soft * grad_soft, axis=-1, keepdims=True)
    grad_scores = soft * (grad_soft - inner)
    grad_bias = jnp.sum(grad_scores, axis=(0, 1)).transpose(1, 2, 0).reshape(size * size, heads)
    grad_table = jnp.dot(one_hot.T, grad_bias, precision=lax.Precision.HIGHEST)
    rounded = grad_scores.astype(jnp.bfloat16)
    grad_query = combine_rule("nwhpq,nwqhd->nwphd", rounded, blocks[:, :, :, :, 1, :]) * HD ** (
        -0.5
    )
    grad_key = combine_rule("nwhpq,nwphd->nwqhd", rounded, blocks[:, :, :, :, 0, :])
    stacked = jnp.stack([grad_query, grad_key, grad_value], axis=4).reshape(
        count, wins, size, heads * 3 * HD
    )
    return (from_windows(stacked), grad_table)


def head_block(tokens, cotangent, live, live_all, owner_pieces, rank, one_hot, mask):
    ranks = lax.axis_size("mp")
    width_rank = owner_pieces["proj_weight"].shape[1]
    heads = width_rank // HD
    rows = tokens.shape[0]

    def linear_entries_arg(label):
        return owner_pieces[label][0].astype(jnp.float32)

    live_col = live[:, None]
    smalls = jnp.stack([owner_pieces[label][0] for label in small_labels])
    whole, cot_all, smalls_all = (
        lax.all_gather(tokens, "mp", axis=0, tiled=True),
        lax.all_gather(cotangent, "mp", axis=0, tiled=True),
        lax.all_gather(smalls, "mp", axis=1, tiled=True),
    )
    full = smalls_all.astype(jnp.float32)
    inputs_all = whole.astype(jnp.float32)
    center1, scale1 = norm_stats(inputs_all)
    unit1 = (inputs_all - center1) * scale1
    normed1 = (unit1 * full[0] + full[1]).astype(jnp.bfloat16)
    group_rows = whole.shape[0]
    raw = jnp.dot(
        normed1, owner_pieces["qkv_weight"][0], preferred_element_type=jnp.float32
    ).reshape(group_rows, heads, 3, HD)
    projected = qkv_finish(
        raw,
        linear_entries_arg("query_bias").reshape(heads, HD),
        linear_entries_arg("value_bias").reshape(heads, HD),
    )
    projected = projected.reshape(group_rows, heads * 3 * HD)
    table = owner_pieces["table"][0].astype(jnp.float32)
    mixed, log_total = attend_forward(projected, table, one_hot, mask)
    partial_value = jnp.dot(
        mixed, owner_pieces["proj_weight"][0], preferred_element_type=jnp.float32
    )
    attended = (
        lax.psum_scatter(
            partial_value.astype(jnp.bfloat16), "mp", scatter_dimension=0, tiled=True
        ).astype(jnp.float32)
        + full[2]
    )
    inputs = tokens.astype(jnp.float32)
    residual = inputs + attended
    center2, scale2 = norm_stats(residual)
    unit2 = (residual - center2) * scale2
    normed2 = (unit2 * full[3] + full[4]).astype(jnp.bfloat16)
    normed2_all = lax.all_gather(normed2, "mp", axis=0, tiled=True)
    hidden_before_gelu = jnp.dot(
        normed2_all, owner_pieces["fc1_weight"][0], preferred_element_type=jnp.float32
    ) + linear_entries_arg("fc1_bias")
    nonlinear_token_list = gelu(hidden_before_gelu).astype(jnp.bfloat16)
    feed_part = jnp.dot(
        nonlinear_token_list, owner_pieces["fc2_weight"][0], preferred_element_type=jnp.float32
    )
    perceptron_result = (
        lax.psum_scatter(
            feed_part.astype(jnp.bfloat16), "mp", scatter_dimension=0, tiled=True
        ).astype(jnp.float32)
        + full[5]
    )
    output = (live_col * (residual + perceptron_result)).astype(jnp.bfloat16)
    grad_out = live_col * cotangent.astype(jnp.float32)
    parameter_gradients = {}
    grad_all = cot_all * live_all[:, None].astype(jnp.bfloat16)
    parameter_gradients["fc2_weight"] = contract_rows(nonlinear_token_list, grad_all)[None]
    gradient_before_gelu = contract_cols(grad_all, owner_pieces["fc2_weight"][0]) * gelu_derivative(
        hidden_before_gelu
    )
    parameter_gradients["fc1_bias"] = jnp.sum(gradient_before_gelu, axis=0)[None]
    preact_rounded = gradient_before_gelu.astype(jnp.bfloat16)
    parameter_gradients["fc1_weight"] = contract_rows(normed2_all, preact_rounded)[None]
    grad_norm2 = lax.psum_scatter(
        contract_cols(preact_rounded, owner_pieces["fc1_weight"][0]).astype(jnp.bfloat16),
        "mp",
        scatter_dimension=0,
        tiled=True,
    ).astype(jnp.float32)
    grad_residual = grad_out + norm_back(grad_norm2 * full[3], unit2, scale2)
    residual_rounded = grad_residual.astype(jnp.bfloat16)
    rounded_all = lax.all_gather(residual_rounded, "mp", axis=0, tiled=True)
    parameter_gradients["proj_weight"] = contract_rows(mixed, rounded_all)[None]
    grad_mixed = contract_cols(rounded_all, owner_pieces["proj_weight"][0]).astype(jnp.bfloat16)
    grad_projected, grad_table = attend_backward(
        projected, grad_mixed, table, log_total, one_hot, mask
    )
    split = grad_projected.reshape(group_rows, heads, 3, HD)
    parameter_gradients["query_bias"] = jnp.sum(split[:, :, 0, :], axis=0).reshape(1, width_rank)
    parameter_gradients["value_bias"] = jnp.sum(split[:, :, 2, :], axis=0).reshape(1, width_rank)
    parameter_gradients["table"] = grad_table[None]
    projected_rounded = grad_projected.astype(jnp.bfloat16)
    parameter_gradients["qkv_weight"] = contract_rows(normed1, projected_rounded)[None]
    norm1_part = contract_cols(projected_rounded, owner_pieces["qkv_weight"][0])
    grad_norm1 = lax.psum_scatter(
        norm1_part.astype(jnp.bfloat16), "mp", scatter_dimension=0, tiled=True
    ).astype(jnp.float32)
    unit1_own = lax.dynamic_slice_in_dim(unit1, rank * rows, rows, 0)
    scale1_own = lax.dynamic_slice_in_dim(scale1, rank * rows, rows, 0)
    grad_input = (grad_residual + norm_back(grad_norm1 * full[0], unit1_own, scale1_own)).astype(
        jnp.bfloat16
    )
    small_terms = jnp.stack(
        [
            jnp.sum(grad_norm1 * unit1_own, axis=0),
            jnp.sum(grad_norm1, axis=0),
            jnp.sum(grad_residual, axis=0),
            jnp.sum(grad_norm2 * unit2, axis=0),
            jnp.sum(grad_norm2, axis=0),
            jnp.sum(grad_out, axis=0),
        ]
    ).reshape(len(small_labels), ranks, width_rank)
    small_sums = lax.psum_scatter(small_terms, "mp", scatter_dimension=1, tiled=True)
    for index, label in enumerate(small_labels):
        parameter_gradients[label] = small_sums[index]
    return (output, grad_input, parameter_gradients)


def local(tokens, cotangent, image_counts, params, moment_one, moment_two):
    ranks = lax.axis_size("mp")
    rank = lax.axis_index("mp")
    group = lax.axis_index("dp")
    width_rank = C // ranks
    hidden_rank = FF // ranks
    pixels = MAP * MAP
    rows = tokens.shape[0]
    shard_length = params.shape[1]
    one_hot, mask = window_tables()
    owned = lax.all_gather(params.astype(jnp.bfloat16), "dp", axis=1, tiled=True)
    limit = jnp.sum(
        jnp.where(jnp.arange(image_counts.shape[0], dtype=jnp.int32) == group, image_counts, 0)
    )
    images = rank * (rows // pixels) + jnp.arange(rows, dtype=jnp.int32) // pixels
    live = (images < limit).astype(jnp.float32)
    owner_pieces = unpack(owned, width_rank, hidden_rank)
    live_all = (jnp.arange(rows * ranks, dtype=jnp.int32) // pixels < limit).astype(jnp.float32)
    output, grad_input, parameter_gradients = head_block(
        tokens, cotangent, live, live_all, owner_pieces, rank, one_hot, mask
    )
    flat = pack(parameter_gradients, width_rank, hidden_rank, owned.shape[1])
    grad_shard = lax.psum_scatter(flat, "dp", scatter_dimension=1, tiled=True)
    weights_rank = (4 * C * C + 2 * C * FF) // ranks
    position = group * shard_length + jnp.arange(shard_length, dtype=jnp.int32)[None, :]
    decays = (position < weights_rank).astype(jnp.float32)
    new_one = beta_one * moment_one + (1.0 - beta_one) * grad_shard
    new_two = second_decay_rate * moment_two + (1.0 - second_decay_rate) * grad_shard * grad_shard
    corrected_one = new_one / (1.0 - beta_one**adam_step)
    corrected_two = new_two / (1.0 - second_decay_rate**adam_step)
    new_params = params - learn_rate * (
        corrected_one / (jnp.sqrt(corrected_two) + adam_eps) + weight_decay * decays * params
    )
    return (output, grad_input, grad_shard, new_params, new_one, new_two)


def solution(mesh):
    return jax.shard_map(
        local,
        mesh=mesh,
        in_specs=(
            P(("dp", "mp"), None),
            P(("dp", "mp"), None),
            P(),
            P("mp", "dp"),
            P("mp", "dp"),
            P("mp", "dp"),
        ),
        out_specs=(
            P(("dp", "mp"), None),
            P(("dp", "mp"), None),
            P("mp", "dp"),
            P("mp", "dp"),
            P("mp", "dp"),
            P("mp", "dp"),
        ),
        check_vma=False,
    )
```

profile of v0, /device:TPU:0, one launch (start us, length us, event | category | flops | bytes accessed | tf_op | source)
XLA Modules:
  0.0 1342.3 jit_solution(6521785367379511616)
XLA Ops:
  8.1 2.0 convert_reduce_fusion.3
  12.2 2.1 dynamic-update-slice
  16.2 36.5 %all-reduce.6.cloned.1.call-done = bf16[394324]{0:T(1024)(128)(2,1)} async-done(((bf16[394324]{0:T(1024)(128)(2,1)}), bf16[394324]{0:T(1024)(128)(2,1)}) %all-reduce.6.cloned.1.call-update) | async-done | bytes 788664
  52.7 8.4 reshape.473
  61.5 27.7 %all-gather = bf16[8,64,6]{1,2,0:T(8,128)(2,1)S(1)} all-gather(bf16[1,64,6]{1,2,0:T(8,128)(2,1)S(1)} %bitcast.187), channel_id=1, replica_groups=mesh['dp'=4,'mp'=8] {'mp'}, dimensions={0}, use_global_device_ids=true | all-gather | bytes 6912 | tf_op jit(solution)/shard_map/all_gather | solution.py:224
  93.6 27.4 %all-gather.6.cloned.1.call-done = bf16[6272,512]{1,0:T(8,128)(2,1)} async-done(((bf16[784,512]{1,0:T(8,128)(2,1)}), bf16[6272,512]{1,0:T(8,128)(2,1)}) %all-gather.6.cloned.1.call-update) | async-done | bytes 6422544 | tf_op jit(solution)/shard_map/all_gather | solution.py:222
  121.0 3.9 convert_reduce_fusion
  125.7 2.9 fusion.2
  128.7 6.0 fusion.4
  134.7 12.6 copy.83
  147.3 21.8 %reshape_reshape.20 = bf16[32,14,14,192]{3,2,1,0:T(8,128)(2,1)} reshape(bf16[6272,2,3,32]{3,2,1,0:T(4,128)(2,1)} %copy.83) | data formatting | bytes 4816896 | tf_op jit(solution)/shard_map/reshape;reshape | solution.py:114
  177.3 11.2 reshape_reshape.21
  188.5 25.3 %fusion.105 = (bf16[32,4,49,2,1,32]{5,4,3,0,2,1:T(2,128)(2,1)}, bf16[32,4,49,2,1,32]{5,4,3,0,2,1:T(2,128)(2,1)}, bf16[32,4,49,2,1,32]{5,4,3,0,2,1:T(2,128)(2,1)}) fusion(bf16[32,4,49,2,3,32]{5,4,3,0,2,1:T(4,128)(2,1)} %reshape_reshape.21), kind=kLoop, calls=%fused_computation.208 | loop fusion | bytes 4816896 | tf_op jit(solution)/shard_map/slice | solution.py:167
  213.8 12.7 copy.124
  226.6 14.0 %copy.123 = bf16[32,4,49,2,1,32]{2,5,3,1,0,4:T(8,128)(2,1)} copy(bf16[32,4,49,2,1,32]{5,4,3,0,2,1:T(2,128)(2,1)} %get-tuple-element.29) | data formatting | bytes 1605632
  240.6 13.9 %copy.125 = bf16[32,4,49,2,1,32]{2,5,3,1,0,4:T(8,128)(2,1)} copy(bf16[32,4,49,2,1,32]{5,4,3,0,2,1:T(2,128)(2,1)} %get-tuple-element.30) | data formatting | bytes 1605632
  254.5 3.8 fusion.14
  258.3 2.6 exponential_reduce_fusion
  261.6 3.3 convert_bitcast_fusion
  265.0 7.8 copy.92
  272.8 2.6 reshape_reshape.22
  280.5 5.4 convolution_convert_fusion.3
  286.2 117.8 %reduce-scatter.7.cloned.1.call-done = bf16[784,512]{1,0:T(8,128)(2,1)} async-done(((bf16[6272,512]{1,0:T(8,128)(2,1)}), bf16[784,512]{1,0:T(8,128)(2,1)}) %reduce-scatter.7.cloned.1.call-update) | async-done | bytes 802832 | tf_op jit(solution)/shard_map/reduce_scatter | solution.py:247
  410.8 3.0 slice_reduce_fusion.2
  414.8 93.3 %all-gather.8.cloned.1.call-done = bf16[6272,512]{1,0:T(8,128)(2,1)} async-done(((bf16[784,512]{1,0:T(8,128)(2,1)}), bf16[6272,512]{1,0:T(8,128)(2,1)}) %all-gather.8.cloned.1.call-update) | async-done | bytes 6422544 | tf_op jit(solution)/shard_map/all_gather | solution.py:257
  508.2 6.6 multiply_convert_fusion
  514.8 93.9 %all-gather.10.cloned.1.call-done = bf16[6272,512]{1,0:T(8,128)(2,1)} async-done(((bf16[784,512]{1,0:T(8,128)(2,1)}), bf16[6272,512]{1,0:T(8,128)(2,1)}) %all-gather.10.cloned.1.call-update) | async-done | bytes 6422544 | tf_op jit(solution)/shard_map/all_gather | solution.py:223
  608.7 8.1 fusion.109
  616.8 4.5 convolution_convert_fusion.1
  621.4 6.5 convolution_convert_fusion.2
  629.0 110.4 %reduce-scatter.11.cloned.1.call-done = bf16[784,512]{1,0:T(8,128)(2,1)} async-done(((bf16[6272,512]{1,0:T(8,128)(2,1)}), bf16[784,512]{1,0:T(8,128)(2,1)}) %reduce-scatter.11.cloned.1.call-update) | async-done | bytes 802832 | tf_op jit(solution)/shard_map/reduce_scatter | solution.py:282
  739.4 2.7 fusion.53
  742.2 119.9 %reduce-scatter.9.cloned.1.call-done = bf16[784,512]{1,0:T(8,128)(2,1)} async-done(((bf16[6272,512]{1,0:T(8,128)(2,1)}), bf16[784,512]{1,0:T(8,128)(2,1)}) %reduce-scatter.9.cloned.1.call-update) | async-done | bytes 802832 | tf_op jit(solution)/shard_map/reduce_scatter | solution.py:266
  862.1 3.6 fusion.103
  869.3 9.1 fusion
  878.4 4.9 fusion.61
  884.7 5.1 fusion.64
  893.8 73.7 %all-gather.12.cloned.1.call-done = bf16[6272,512]{1,0:T(8,128)(2,1)} async-done(((bf16[784,512]{1,0:T(8,128)(2,1)}), bf16[6272,512]{1,0:T(8,128)(2,1)}) %all-gather.12.cloned.1.call-update) | async-done | bytes 6422544 | tf_op jit(solution)/shard_map/all_gather | solution.py:290
  967.5 4.9 convolution_convert_fusion.4
  976.7 2.9 reshape_reshape.23
  979.6 8.8 copy.98
  988.4 7.9 convolution_bitcast_fusion
  996.3 3.2 multiply_reduce_fusion
  999.6 2.8 fusion.102
  1002.3 4.0 convolution_bitcast_fusion.1
  1006.3 3.2 multiply_bitcast_fusion
  1009.5 10.6 pad_maximum_fusion
  1020.1 23.6 %copy.103 = f32[32,4,49,2,3,32]{5,4,3,0,2,1:T(4,128)} copy(f32[32,4,49,2,3,32]{2,5,3,1,0,4:T(8,128)} %pad_maximum_fusion) | data formatting | bytes 9633792 | tf_op jit(solution)/shard_map/stack | solution.py:204
  1043.6 26.7 %reshape_reshape.24 = f32[32,2,2,7,7,192]{5,0,4,3,2,1:T(8,128)} reshape(f32[32,4,49,2,3,32]{5,4,3,0,2,1:T(4,128)} %copy.103) | data formatting | bytes 9633792 | tf_op jit(solution)/shard_map/reshape;reshape | solution.py:123
  1070.3 3.4 copy.104
  1075.0 3.7 fusion.9
  1084.7 3.7 copy.105
  1088.3 5.1 convert_element_type.224
  1093.5 4.6 convolution_convert_fusion
  1098.0 8.6 fusion.43
  1108.2 9.5 copy.107
  1117.8 24.8 %reshape_reshape.25 = f32[6272,2,3,32]{3,2,1,0:T(4,128)} reshape(f32[32,14,14,192]{3,2,1,0:T(8,128)} %copy.107) | data formatting | bytes 9633792 | tf_op jit(solution)/shard_map/reshape;reshape | solution.py:296
  1142.6 25.9 %slice_reduce_fusion = (f32[2,32]{1,0:T(2,128)S(1)}, f32[2,32]{1,0:T(2,128)S(1)}) fusion(f32[6272,2,3,32]{3,2,1,0:T(4,128)} %reshape_reshape.25), kind=kLoop, calls=%fused_computation.27 | loop fusion | flops 802688 | bytes 3211776 | tf_op jit(solution)/shard_map/reduce_sum | solution.py:298
  1172.3 63.5 %reduce-scatter.13.cloned.1.call-done = bf16[784,512]{1,0:T(8,128)(2,1)} async-done(((bf16[6272,512]{1,0:T(8,128)(2,1)}), bf16[784,512]{1,0:T(8,128)(2,1)}) %reduce-scatter.13.cloned.1.call-update) | async-done | bytes 802832 | tf_op jit(solution)/shard_map/reduce_scatter | solution.py:303
  1235.8 2.3 fusion.54
  1238.4 35.4 %all-reduce.1 = f32[6,8,64]{2,1,0:T(8,128)S(1)} all-reduce(f32[6,8,64]{2,1,0:T(8,128)S(1)} %constant_dynamic-update-slice_fusion), channel_id=6, replica_groups=mesh['dp'=4,'mp'=8] {'mp'}, use_global_device_ids=true, to_apply=%region_22.23.clone | all-reduce | flops 3072 | bytes 24576
  1289.7 2.8 fusion.47
  1292.4 37.1 %all-reduce.8.cloned.1.call-done = f32[1,394324]{1,0:T(1,128)} async-done(((f32[1,394324]{1,0:T(1,128)}), f32[1,394324]{1,0:T(1,128)}) %all-reduce.8.cloned.1.call-update) | async-done | bytes 1577312
  1329.6 4.9 multiply_subtract_fusion
  (258 shorter events, 73.0 us)
Async XLA Ops:
  8.0 44.7 %all-reduce.6.cloned.1.call-start = ((), (), s32[]{:S(2)}) async-start(), calls=%async_computation.12 | async-start | bytes 1581056
  15.2 105.8 %all-gather.6.cloned.1.call-start = ((), (), s32[]{:S(2)}) async-start(), calls=%async_computation.4 | async-start | bytes 7225344 | tf_op jit(solution)/shard_map/all_gather | solution.py:222
  15.8 388.3 %reduce-scatter.7.cloned.1.call-start = ((), (), s32[]{:S(2)}) async-start(), calls=%async_computation.5 | async-start | bytes 7225344 | tf_op jit(solution)/shard_map/reduce_scatter | solution.py:247
  16.1 75.5 %copy-start.39 = (s32[49,49]{1,0:T(8,128)}, s32[49,49]{1,0:T(8,128)S(1)}, u32[]{:S(2)}) copy-start(s32[49,49]{1,0:T(8,128)S(1)} %add_add_fusion.2) | copy-start | bytes 28816
  61.0 63.9 %copy-start.15 = (bf16[1,394324]{1,0:T(2,128)(2,1)}, bf16[1,394324]{1,0:T(2,128)(2,1)S(1)}, u32[]{:S(2)}) copy-start(bf16[1,394324]{1,0:T(2,128)(2,1)S(1)} %reshape.473) | copy-start | bytes 2365948
  90.5 170.5 %copy-start.22 = (f32[2,49,49]{1,2,0:T(8,128)}, f32[2,49,49]{1,2,0:T(8,128)S(1)}, u32[]{:S(2)}) copy-start(f32[2,49,49]{1,2,0:T(8,128)S(1)} %copy.90) | copy-start | bytes 57628
  92.9 35.7 %copy-start.25 = (bf16[512,192]{1,0:T(8,128)(2,1)}, bf16[512,192]{1,0:T(8,128)(2,1)S(1)}, u32[]{:S(2)}) copy-start(bf16[512,192]{1,0:T(8,128)(2,1)S(1)} %squeeze_reshape.19) | copy-start | bytes 589828
  93.6 35.0 %copy-start.43 = (f32[1,512]{1,0:T(1,128)}, f32[1,512]{1,0:T(1,128)S(1)}, u32[]{:S(2)}) copy-start(f32[1,512]{1,0:T(1,128)S(1)} %get-tuple-element.50) | copy-start | bytes 6148
  93.6 35.0 %copy-start.52 = (f32[1,512]{1,0:T(1,128)}, f32[1,512]{1,0:T(1,128)S(1)}, u32[]{:S(2)}) copy-start(f32[1,512]{1,0:T(1,128)S(1)} %get-tuple-element.49) | copy-start | bytes 6148
  121.0 4.7 copy-start.1
  124.9 3.8 copy-start.57
  125.7 9.0 copy-start.33
  128.6 6.1 copy-start.36
  226.6 27.9 %copy-start.6 = (bf16[32,4,49,2,1,32]{2,5,3,1,0,4:T(8,128)(2,1)}, bf16[32,4,49,2,1,32]{2,5,3,1,0,4:T(8,128)(2,1)S(1)}, u32[]{:S(2)}) copy-start(bf16[32,4,49,2,1,32]{2,5,3,1,0,4:T(8,128)(2,1)S(1)} %copy.124) | copy-start | bytes 2408452
  258.3 3.3 copy-start.9
  285.9 118.2 %copy-start.2 = (bf16[784,512]{1,0:T(8,128)(2,1)S(1)}, bf16[784,512]{1,0:T(8,128)(2,1)}, u32[]{:S(2)}) copy-start(bf16[784,512]{1,0:T(8,128)(2,1)} %param.7) | copy-start | bytes 2408452
  285.9 118.2 %copy-start.41 = (f32[1,512]{1,0:T(1,128)S(1)}, f32[1,512]{1,0:T(1,128)}, u32[]{:S(2)}) copy-start(f32[1,512]{1,0:T(1,128)} %get-tuple-element.48) | copy-start | bytes 6148
  285.9 121.4 %copy-start.42 = (f32[1,512]{1,0:T(1,128)S(1)}, f32[1,512]{1,0:T(1,128)}, u32[]{:S(2)}) copy-start(f32[1,512]{1,0:T(1,128)} %get-tuple-element.47) | copy-start | bytes 6148
  285.9 121.4 %copy-start.51 = (f32[1,512]{1,0:T(1,128)S(1)}, f32[1,512]{1,0:T(1,128)}, u32[]{:S(2)}) copy-start(f32[1,512]{1,0:T(1,128)} %get-tuple-element.46) | copy-start | bytes 6148
  285.9 123.5 %copy-start.55 = (s32[4]{0:T(128)S(1)}, s32[4]{0:T(128)}, u32[]{:S(2)}) copy-start(s32[4]{0:T(128)} %param.9) | copy-start | bytes 52
  285.9 124.8 %copy-start.16 = (bf16[1,394324]{1,0:T(2,128)(2,1)S(1)}, bf16[1,394324]{1,0:T(2,128)(2,1)}, u32[]{:S(2)}) copy-start(bf16[1,394324]{1,0:T(2,128)(2,1)} %copy-done.15) | copy-start | bytes 2365948
  285.9 222.2 %all-gather.8.cloned.1.call-start = ((), (), s32[]{:S(2)}) async-start(), calls=%async_computation.6 | async-start | bytes 7225344 | tf_op jit(solution)/shard_map/all_gather | solution.py:257
  404.1 3.2 copy-start.5
  408.7 200.0 %all-gather.10.cloned.1.call-start = ((), (), s32[]{:S(2)}) async-start(), calls=%async_computation.8 | async-start | bytes 7225344 | tf_op jit(solution)/shard_map/all_gather | solution.py:223
  409.4 330.0 %reduce-scatter.11.cloned.1.call-start = ((), (), s32[]{:S(2)}) async-start(), calls=%async_computation.9 | async-start | bytes 7225344 | tf_op jit(solution)/shard_map/reduce_scatter | solution.py:282
  414.7 100.0 %copy-start.28 = (bf16[512,256]{1,0:T(8,128)(2,1)}, bf16[512,256]{1,0:T(8,128)(2,1)S(1)}, u32[]{:S(2)}) copy-start(bf16[512,256]{1,0:T(8,128)(2,1)S(1)} %squeeze_reshape.22) | copy-start | bytes 786436
  608.7 8.1 copy-start.29
  621.3 240.8 %reduce-scatter.9.cloned.1.call-start = ((), (), s32[]{:S(2)}) async-start(), calls=%async_computation.7 | async-start | bytes 7225344 | tf_op jit(solution)/shard_map/reduce_scatter | solution.py:266
  627.9 234.2 %copy-start.50 = (f32[1,512]{1,0:T(1,128)S(1)}, f32[1,512]{1,0:T(1,128)}, u32[]{:S(2)}) copy-start(f32[1,512]{1,0:T(1,128)} %get-tuple-element.45) | copy-start | bytes 6148
  627.9 339.6 %all-gather.12.cloned.1.call-start = ((), (), s32[]{:S(2)}) async-start(), calls=%async_computation.10 | async-start | bytes 7225344 | tf_op jit(solution)/shard_map/all_gather | solution.py:290
  862.1 5.9 copy-start.40
  862.1 6.6 copy-start.56
  862.1 7.2 copy-start.34
  862.1 7.2 copy-start.37
  867.9 367.9 %reduce-scatter.13.cloned.1.call-start = ((), (), s32[]{:S(2)}) async-start(), calls=%async_computation.11 | async-start | bytes 7225344 | tf_op jit(solution)/shard_map/reduce_scatter | solution.py:303
  878.4 6.2 copy-start.17
  884.7 82.8 %copy-start.30 = (bf16[64,512]{1,0:T(8,128)(2,1)S(1)}, bf16[64,512]{1,0:T(8,128)(2,1)}, u32[]{:S(2)}) copy-start(bf16[64,512]{1,0:T(8,128)(2,1)} %squeeze_reshape.21) | copy-start | bytes 196612
  979.5 8.8 copy-start.19
  979.5 8.8 copy-start.23
  979.5 16.8 %slice-start = ((s8[7340032]{0:T(1024)(128)(4,1)}), s8[3145728]{0:T(1024)(128)(4,1)S(1)}, s32[]{:S(2)}) async-start(s8[7340032]{0:T(1024)(128)(4,1)} %bitcast.149), calls=%async_computation.14 | async-start | bytes 6291456
  988.4 7.9 slice-start.1
  988.4 7.9 copy-start.10
  988.4 7.9 copy-start.11
  1002.3 4.0 copy-start.8
  1006.3 3.2 copy-start.12
  1074.5 4.2 slice-start.2
  1075.0 4.9 slice-start.3
  1075.0 5.3 copy-start.4
  1088.3 5.1 copy-start.26
  1093.4 4.6 copy-start.35
  1093.4 4.6 copy-start.38
  1093.4 4.6 copy-start.44
  1093.4 4.6 copy-start.53
  1117.7 211.8 %all-reduce.8.cloned.1.call-start = ((), (), s32[]{:S(2)}) async-start(), calls=%async_computation.13 | async-start | bytes 3154944
  1142.6 26.1 %copy-start.31 = (f32[1,1,64,512]{3,1,2,0:T(1,128)S(1)}, f32[1,1,64,512]{3,1,2,0:T(1,128)}, u32[]{:S(2)}) copy-start(f32[1,1,64,512]{3,1,2,0:T(1,128)} %copy.126) | copy-start | bytes 393220
  1168.6 69.8 %copy-start.48 = (f32[1,8,64]{2,1,0:T(8,128)S(1)}, f32[1,8,64]{2,1,0:T(8,128)}, u32[]{:S(2)}) copy-start(f32[1,8,64]{2,1,0:T(8,128)} %stack.47) | copy-start | bytes 6148
  1168.6 69.8 %copy-start.46 = (f32[1,8,64]{2,1,0:T(8,128)S(1)}, f32[1,8,64]{2,1,0:T(8,128)}, u32[]{:S(2)}) copy-start(f32[1,8,64]{2,1,0:T(8,128)} %stack.48) | copy-start | bytes 6148
  1168.6 69.8 %copy-start.47 = (f32[1,8,64]{2,1,0:T(8,128)S(1)}, f32[1,8,64]{2,1,0:T(8,128)}, u32[]{:S(2)}) copy-start(f32[1,8,64]{2,1,0:T(8,128)} %stack.49) | copy-start | bytes 6148
  1168.6 69.8 %copy-start.45 = (f32[1,8,64]{2,1,0:T(8,128)S(1)}, f32[1,8,64]{2,1,0:T(8,128)}, u32[]{:S(2)}) copy-start(f32[1,8,64]{2,1,0:T(8,128)} %stack.50) | copy-start | bytes 6148
  1168.6 114.9 %copy-start.54 = (f32[256]{0:T(256)S(1)}, f32[256]{0:T(256)}, u32[]{:S(2)}) copy-start(f32[256]{0:T(256)} %get-tuple-element.59) | copy-start | bytes 3076
  1168.6 121.1 %copy-start.14 = (f32[784,512]{1,0:T(8,128)S(1)}, f32[784,512]{1,0:T(8,128)}, u32[]{:S(2)}) copy-start(f32[784,512]{1,0:T(8,128)} %copy-done.13) | copy-start | bytes 4816900
  1235.8 53.9 %copy-start.20 = (bf16[784,512]{1,0:T(8,128)(2,1)S(1)}, bf16[784,512]{1,0:T(8,128)(2,1)}, u32[]{:S(2)}) copy-start(bf16[784,512]{1,0:T(8,128)(2,1)} %reduce-scatter.13.cloned.1.call-done) | copy-start | bytes 2408452
  1238.2 91.4 %copy-start.27 = (f32[1,98581]{1,0:T(1,128)S(1)}, f32[1,98581]{1,0:T(1,128)}, u32[]{:S(2)}) copy-start(f32[1,98581]{1,0:T(1,128)} %param.10) | copy-start | bytes 1182976
  1238.2 91.4 %copy-start.32 = (f32[1,98581]{1,0:T(1,128)S(1)}, f32[1,98581]{1,0:T(1,128)}, u32[]{:S(2)}) copy-start(f32[1,98581]{1,0:T(1,128)} %param.11) | copy-start | bytes 1182976
  (8 other events, 13.4 us)
Sparse Core Ops, SparseCore 0:
  15.3 37.3 all-reduce.5
  1289.0 40.4 all-reduce.7
Sparse Core Ops, SparseCore 1:
  17.8 103.1 all-gather.5
  286.0 118.0 reduce-scatter.6
  408.7 99.4 all-gather.7
  510.4 98.3 all-gather.9
  621.4 118.0 reduce-scatter.10
  743.1 119.0 reduce-scatter.8
  868.0 99.4 all-gather.11
  1117.8 117.9 reduce-scatter.12
where the time goes:
time: 1350 us; the launch traced here: 1340 us
  waiting for transfers between devices  775 us (57%)
  local copies, waits for them, and re-layouts  297 us (22%)
  matrix products  94.6 us (7%)
  other arithmetic  92.8 us (7%)
  blocking collectives  63.1 us (5%)
  between operations  18.4 us (1%)
    reduce_scatter x1, waiting for transfers between devices, head_block(): lax.psum_scatter(feed_part.astype(jnp.bfloat16), 'mp', scatter_dimension=...  120 us
    reduce_scatter x1, waiting for transfers between devices, head_block(): lax.psum_scatter(partial_value.astype(jnp.bfloat16), 'mp', scatter_dimens...  118 us
    reduce_scatter x1, waiting for transfers between devices, head_block(): lax.psum_scatter(contract_cols(preact_rounded, owner_pieces['fc1_weight']...  110 us
    all_gather x1, waiting for transfers between devices, head_block(): lax.all_gather(cotangent, 'mp', axis=0, tiled=True)  93.9 us
    all_gather x1, waiting for transfers between devices, head_block(): normed2_all = lax.all_gather(normed2, 'mp', axis=0, tiled=True)  93.3 us
    unnamed x154, local copies, waits for them, and re-layouts  79.7 us
    unnamed x12, waiting for transfers between devices  75 us
    all_gather x1, waiting for transfers between devices, head_block(): rounded_all = lax.all_gather(residual_rounded, 'mp', axis=0, tiled=True)  73.7 us
  transfers between devices with their start and end apart: 10, of which 10 were waited for; matrix products, arithmetic and copies ran while one was open for 9% of the time, Pallas kernels for 0%

commit v1 on v0

v1 whole, which is shorter than its diff:
```python
import functools
import math

import jax
import jax.numpy as jnp
import numpy as np
from jax import lax
from jax.experimental import pallas as pl
from jax.experimental.pallas import tpu as pltpu
from jax.sharding import PartitionSpec as P

C = 512
FF = 2048
HD = 32
WIN = 7
MAP = 14
SHIFT = 3
PIX = MAP * MAP
HEADS = C // HD
SEG = 64
GH = 4
NG = HEADS // GH
SIDE = MAP // WIN
NW = SIDE * SIDE
SPAN = 2 * WIN - 1

norm_eps = 1e-05
mask_fill = -100.0
learn_rate = 0.05
beta_one = 0.9
second_decay_rate = 0.999
adam_eps = 1e-08
weight_decay = 0.05
adam_step = 2.0
f32 = jnp.float32
bf16 = jnp.bfloat16


def mm(a, b):
    return lax.dot_general(a, b, (((1,), (0,)), ((), ())), preferred_element_type=f32)


def mm_t(a, b):
    return lax.dot_general(a, b, (((1,), (1,)), ((), ())), preferred_element_type=f32)


def mm_r(a, b):
    return lax.dot_general(a, b, (((0,), (0,)), ((), ())), preferred_element_type=f32)


def norm_stats(values):
    center = jnp.mean(values, axis=1, keepdims=True)
    spread = jnp.mean(jnp.square(values - center), axis=1, keepdims=True)
    return center, lax.rsqrt(spread + norm_eps)


def norm_back(scaled, unit, scale):
    return scale * (
        scaled
        - jnp.mean(scaled, axis=1, keepdims=True)
        - unit * jnp.mean(scaled * unit, axis=1, keepdims=True)
    )


def phi_parts(v):
    z = jnp.abs(v) * (1.0 / math.sqrt(2.0))
    t = 1.0 / (1.0 + 0.3275911 * z)
    poly = t * (
        0.254829592
        + t * (-0.284496736 + t * (1.421413741 + t * (-1.453152027 + t * 1.061405429)))
    )
    e = jnp.exp(-0.5 * v * v)
    tail = 0.5 * poly * e
    return jnp.where(v >= 0, 1.0 - tail, tail), e


def window_sites():
    w = np.arange(NW)[:, None]
    p = np.arange(WIN * WIN)[None, :]
    row = (w // SIDE) * WIN + p // WIN
    col = (w % SIDE) * WIN + p % WIN
    token = ((row + SHIFT) % MAP) * MAP + (col + SHIFT) % MAP

    def region(c):
        return (c >= MAP - WIN).astype(np.int32) + (c >= MAP - SHIFT).astype(np.int32)

    ids = region(row) * 3 + region(col)
    return token, ids


def image_frames(images):
    starts = [PIX * i // 16 * 16 for i in range(images)]
    offsets = [PIX * i - s for i, s in enumerate(starts)]
    length = -(-(PIX + max(offsets)) // 16) * 16
    return starts, offsets, length


def placement(images):
    token, _ = window_sites()
    starts, offsets, length = image_frames(images)
    sel = np.zeros((images, NW * SEG, length), np.float32)
    for i in range(images):
        for w in range(NW):
            sel[i, w * SEG + np.arange(WIN * WIN), token[w] + offsets[i]] = 1.0
    return sel


def score_bias(table):
    size = WIN * WIN
    p = np.arange(size)
    a, b = p // WIN, p % WIN
    off = (a[None, :] - a[:, None] + WIN - 1) * SPAN + b[None, :] - b[:, None] + WIN - 1
    one_hot = np.zeros((size, size, SPAN * SPAN), np.float32)
    one_hot[np.arange(size)[:, None], np.arange(size)[None, :], off] = 1.0
    _, ids = window_sites()
    full_mask = np.full((NW, SEG, SEG), 0.0, np.float32)
    full_mask[:, size:, :] = -1e30
    full_mask[:, :size, :size] = np.where(ids[:, :, None] == ids[:, None, :], 0.0, mask_fill)
    onehot = jnp.asarray(one_hot.reshape(size * size, -1), bf16)
    bias = jnp.dot(table.T.astype(bf16), onehot.T, preferred_element_type=f32)
    bias = bias.reshape(NG, GH, size, size)
    bias = jnp.pad(bias, ((0, 0), (0, 0), (0, SEG - size), (0, SEG - size)))
    bias = bias.transpose(0, 2, 1, 3)
    out = bias[None] + jnp.asarray(full_mask)[:, None, :, None, :]
    return out.reshape(NW * NG, SEG, GH * SEG)


def table_back(acc):
    size = WIN * WIN
    p = np.arange(size)
    a, b = p // WIN, p % WIN
    off = (a[None, :] - a[:, None] + WIN - 1) * SPAN + b[None, :] - b[:, None] + WIN - 1
    one_hot = np.zeros((size * size, SPAN * SPAN), np.float32)
    one_hot[np.arange(size * size), off.reshape(-1)] = 1.0
    acc = acc.reshape(NG, SEG, GH, SEG)[:, :size, :, :size].transpose(0, 2, 1, 3).reshape(HEADS, size * size)
    hi = acc.astype(bf16)
    lo = (acc - hi.astype(f32)).astype(bf16)
    oh = jnp.asarray(one_hot, bf16)
    return (
        jnp.dot(hi, oh, preferred_element_type=f32) + jnp.dot(lo, oh, preferred_element_type=f32)
    ).T


def lane_head_mask():
    return lax.broadcasted_iota(jnp.int32, (SEG, GH * HD), 1) // HD


def block_diag(part, head_of_lane):
    zero = jnp.zeros_like(part)
    return jnp.concatenate([jnp.where(head_of_lane == h, part, zero) for h in range(GH)], axis=0)


def diag_pick(full, head_of_lane):
    out = full[:SEG]
    for h in range(1, GH):
        out = jnp.where(head_of_lane == h, full[h * SEG : (h + 1) * SEG], out)
    return out


def compute_kernel(
    images, rows, block, length,
    nlive, x, cot, wqkv, wproj, w1, w2, vecs, b1, bias, sel,
    out, gin, gqkv_w, gproj_w, g1_w, g2_w, gvec, gb1, acc,
    ln1, qkv, wq, probs, mixw, mixed, ln2, act, gpre, gresb, gres, gmix, gwin,
):
    blocks = rows // block
    frame = image_frames(images)[0]
    head_of_lane = lane_head_mask()

    def vec(i):
        return vecs[i : i + 1, :]

    gvec[...] = jnp.zeros_like(gvec)
    gb1[...] = jnp.zeros_like(gb1)
    acc[...] = jnp.zeros_like(acc)
    mixed[...] = jnp.zeros_like(mixed)

    def norm_rows(t, _):
        sl = pl.ds(pl.multiple_of(t * block, 16), block)
        xin = x[sl, :].astype(f32)
        center, scale = norm_stats(xin)
        normed = ((xin - center) * scale * vec(0) + vec(1)).astype(bf16)
        ln1[sl, :] = normed
        qkv[sl, 0:C] = ((mm_t(normed, wqkv[0:C, :]) + vec(2)) * HD ** (-0.5)).astype(bf16)
        qkv[sl, C : 2 * C] = mm_t(normed, wqkv[C : 2 * C, :]).astype(bf16)
        qkv[sl, 2 * C : 3 * C] = (mm_t(normed, wqkv[2 * C : 3 * C, :]) + vec(3)).astype(bf16)
        return 0

    lax.fori_loop(0, blocks, norm_rows, 0)

    for i in range(images):
        fr = pl.ds(frame[i], length)
        wq[i] = mm(sel[i], qkv[fr, :]).astype(bf16)

        def window(w, _):
            ws = pl.ds(pl.multiple_of(w * SEG, SEG), SEG)
            for g in range(NG):
                q = wq[i, ws, g * 128 : (g + 1) * 128]
                k = wq[i, ws, C + g * 128 : C + (g + 1) * 128]
                v = wq[i, ws, 2 * C + g * 128 : 2 * C + (g + 1) * 128]
                st = mm_t(k, block_diag(q, head_of_lane)) + bias[w * NG + g]
                e = jnp.exp(st - jnp.max(st, axis=0, keepdims=True))
                pt = (e * (1.0 / jnp.sum(e, axis=0, keepdims=True))).astype(bf16)
                probs[i, w * NG + g] = pt
                mixw[ws, g * 128 : (g + 1) * 128] = diag_pick(mm_r(pt, v), head_of_lane).astype(bf16)
            return 0

        lax.fori_loop(0, NW, window, 0)
        mixed[fr, :] = (mixed[fr, :].astype(f32) + mm_r(sel[i], mixw[...])).astype(bf16)

    def middle(t, _):
        sl = pl.ds(pl.multiple_of(t * block, 16), block)
        xin = x[sl, :].astype(f32)
        res = xin + (mm(mixed[sl, :], wproj[...]) + vec(4))
        center, scale = norm_stats(res)
        unit = (res - center) * scale
        normed = (unit * vec(5) + vec(6)).astype(bf16)
        ln2[sl, :] = normed
        live = (
            lax.broadcasted_iota(jnp.int32, (block, 1), 0) + t * block < nlive[0]
        ).astype(f32)
        gout = live * cot[sl, :].astype(f32)
        goutb = gout.astype(bf16)
        feed = jnp.zeros((block, C), f32)
        gln = jnp.zeros((block, C), f32)
        for j in range(4):
            js = slice(j * 512, (j + 1) * 512)
            pre = mm(normed, w1[:, js]) + b1[:, js]
            phi, e = phi_parts(pre)
            av = (pre * phi).astype(bf16)
            act[sl, js] = av
            feed = feed + mm(av, w2[js, :])
            gp = mm_t(goutb, w2[js, :]) * (phi + pre * (e * (1.0 / math.sqrt(2.0 * math.pi))))
            gb1[:, js] += jnp.sum(gp, axis=0, keepdims=True)
            gpb = gp.astype(bf16)
            gpre[sl, js] = gpb
            gln = gln + mm_t(gpb, w1[:, js])
        out[sl, :] = (live * (res + feed + vec(7))).astype(bf16)
        gr = gout + norm_back(gln * vec(5), unit, scale)
        gres[sl, :] = gr
        grb = gr.astype(bf16)
        gresb[sl, :] = grb
        gmix[sl, :] = mm_t(grb, wproj[...]).astype(bf16)
        gvec[4:5, :] += jnp.sum(gr, axis=0, keepdims=True)
        gvec[5:6, :] += jnp.sum(gln * unit, axis=0, keepdims=True)
        gvec[6:7, :] += jnp.sum(gln, axis=0, keepdims=True)
        gvec[7:8, :] += jnp.sum(gout, axis=0, keepdims=True)
        return 0

    lax.fori_loop(0, blocks, middle, 0)

    def masked_cot():
        live = (lax.broadcasted_iota(jnp.int32, (rows, 1), 0) < nlive[0]).astype(bf16)
        return cot[...] * live

    gout_all = masked_cot()

    def ff_grads(j, _):
        js = pl.ds(pl.multiple_of(j * 256, 256), 256)
        g2_w[:, js] = mm_r(gout_all, act[:, js]).astype(g2_w.dtype)
        g1_w[:, js] = mm_r(ln2[...], gpre[:, js]).astype(g1_w.dtype)
        return 0

    lax.fori_loop(0, FF // 256, ff_grads, 0)
    gproj_w[...] = mm_r(mixed[...], gresb[...]).astype(gproj_w.dtype)

    qkv[...] = jnp.zeros_like(qkv)
    for i in range(images):
        fr = pl.ds(frame[i], length)
        mixw[...] = mm(sel[i], gmix[fr, :]).astype(bf16)

        def window(w, _):
            ws = pl.ds(pl.multiple_of(w * SEG, SEG), SEG)
            for g in range(NG):
                q = wq[i, ws, g * 128 : (g + 1) * 128]
                k = wq[i, ws, C + g * 128 : C + (g + 1) * 128]
                v = wq[i, ws, 2 * C + g * 128 : 2 * C + (g + 1) * 128]
                pt = probs[i, w * NG + g]
                dod = block_diag(mixw[ws, g * 128 : (g + 1) * 128], head_of_lane)
                gv = mm(pt, dod)
                dpt = mm_t(v, dod)
                ptf = pt.astype(f32)
                prod = ptf * dpt
                dst = prod - ptf * jnp.sum(prod, axis=0, keepdims=True)
                acc[g] += dst
                dsb = dst.astype(bf16)
                gk = mm(dsb, block_diag(q, head_of_lane))
                gq = diag_pick(mm_r(dsb, k), head_of_lane) * HD ** (-0.5)
                gl = slice(g * 128, (g + 1) * 128)
                gvec[2:3, gl] += jnp.sum(gq, axis=0, keepdims=True)
                gvec[3:4, gl] += jnp.sum(gv, axis=0, keepdims=True)
                gwin[ws, g * 128 : (g + 1) * 128] = gq.astype(bf16)
                gwin[ws, C + g * 128 : C + (g + 1) * 128] = gk.astype(bf16)
                gwin[ws, 2 * C + g * 128 : 2 * C + (g + 1) * 128] = gv.astype(bf16)
            return 0

        lax.fori_loop(0, NW, window, 0)
        qkv[fr, :] = (qkv[fr, :].astype(f32) + mm_r(sel[i], gwin[...])).astype(bf16)

    def last(t, _):
        sl = pl.ds(pl.multiple_of(t * block, 16), block)
        gln = mm(qkv[sl, :], wqkv[...])
        xin = x[sl, :].astype(f32)
        center, scale = norm_stats(xin)
        unit = (xin - center) * scale
        gvec[0:1, :] += jnp.sum(gln * unit, axis=0, keepdims=True)
        gvec[1:2, :] += jnp.sum(gln, axis=0, keepdims=True)
        gin[sl, :] = (gres[sl, :] + norm_back(gln * vec(0), unit, scale)).astype(bf16)
        return 0

    lax.fori_loop(0, blocks, last, 0)

    def qkv_grads(j, _):
        js = pl.ds(pl.multiple_of(j * 256, 256), 256)
        gqkv_w[js, :] = mm_r(qkv[:, js], ln1[...]).astype(gqkv_w.dtype)
        return 0

    lax.fori_loop(0, 3 * C // 256, qkv_grads, 0)


def block_size(rows):
    for cand in (112, 80, 64, 48, 32, 16):
        if rows % cand == 0:
            return cand
    return rows


def block_compute(x, cot, nlive, wqkv, wproj, w1, w2, vecs, b1, bias, interpret=False):
    tokens = x.shape[0]
    images = tokens // PIX
    rows = -(-tokens // 16) * 16
    if rows != tokens:
        x = jnp.pad(x, ((0, rows - tokens), (0, 0)))
        cot = jnp.pad(cot, ((0, rows - tokens), (0, 0)))
    block = block_size(rows)
    starts, _, length = image_frames(images)
    assert starts[-1] + length <= rows
    sel = jnp.asarray(placement(images), bf16)
    vmem = pl.BlockSpec(memory_space=pltpu.VMEM)
    smem = pl.BlockSpec(memory_space=pltpu.SMEM)
    s = jax.ShapeDtypeStruct
    outs = pl.pallas_call(
        functools.partial(compute_kernel, images, rows, block, length),
        out_shape=(
            s((rows, C), bf16),
            s((rows, C), bf16),
            s((3 * C, C), bf16),
            s((C, C), bf16),
            s((C, FF), bf16),
            s((C, FF), bf16),
            s((8, C), f32),
            s((1, FF), f32),
            s((NG, SEG, GH * SEG), f32),
        ),
        in_specs=[smem] + [vmem] * 10,
        out_specs=(vmem,) * 9,
        scratch_shapes=[
            pltpu.VMEM((rows, C), bf16),
            pltpu.VMEM((rows, 3 * C), bf16),
            pltpu.VMEM((images, NW * SEG, 3 * C), bf16),
            pltpu.VMEM((images, NW * NG, SEG, GH * SEG), bf16),
            pltpu.VMEM((NW * SEG, C), bf16),
            pltpu.VMEM((rows, C), bf16),
            pltpu.VMEM((rows, C), bf16),
            pltpu.VMEM((rows, FF), bf16),
            pltpu.VMEM((rows, FF), bf16),
            pltpu.VMEM((rows, C), bf16),
            pltpu.VMEM((rows, C), f32),
            pltpu.VMEM((rows, C), bf16),
            pltpu.VMEM((NW * SEG, 3 * C), bf16),
        ],
        compiler_params=pltpu.CompilerParams(vmem_limit_bytes=60 * 1024 * 1024),
        interpret=interpret,
    )(nlive, x, cot, wqkv, wproj, w1, w2, vecs, b1, bias, sel)
    return (outs[0][:tokens], outs[1][:tokens]) + outs[2:]


VEC_LABELS = [
    "norm1_gain",
    "norm1_bias",
    "query_bias",
    "value_bias",
    "proj_bias",
    "norm2_gain",
    "norm2_bias",
    "fc2_bias",
]


def segment_shapes(width_rank, hidden_rank):
    return [
        ("qkv_weight", (C, 3 * width_rank)),
        ("proj_weight", (width_rank, C)),
        ("fc1_weight", (C, hidden_rank)),
        ("fc2_weight", (hidden_rank, C)),
        ("norm1_gain", (width_rank,)),
        ("norm1_bias", (width_rank,)),
        ("query_bias", (width_rank,)),
        ("value_bias", (width_rank,)),
        ("proj_bias", (width_rank,)),
        ("norm2_gain", (width_rank,)),
        ("norm2_bias", (width_rank,)),
        ("fc1_bias", (hidden_rank,)),
        ("fc2_bias", (width_rank,)),
        ("table", (SPAN * SPAN, width_rank // HD)),
    ]


def unpack(flat, width_rank, hidden_rank):
    pieces = {}
    offset = 0
    for label, shape in segment_shapes(width_rank, hidden_rank):
        amount = math.prod(shape)
        pieces[label] = flat[:, offset : offset + amount].reshape((flat.shape[0],) + shape)
        offset = offset + amount
    return pieces


def local(tokens, cotangent, image_counts, params, moment_one, moment_two):
    ranks = lax.axis_size("mp")
    rank = lax.axis_index("mp")
    group = lax.axis_index("dp")
    width = C // ranks
    hidden = FF // ranks
    heads = width // HD
    rows = tokens.shape[0]
    shard_length = params.shape[1]
    length = shard_length * lax.axis_size("dp")
    owned = lax.all_gather(params.astype(bf16), "mp", axis=0, tiled=True)
    owned = lax.all_gather(owned, "dp", axis=1, tiled=True)
    op = unpack(owned, width, hidden)
    wqkv = op["qkv_weight"].reshape(ranks, C, heads, 3, HD).transpose(3, 0, 2, 4, 1).reshape(3 * C, C)
    wproj = op["proj_weight"].reshape(C, C)
    w1 = op["fc1_weight"].transpose(1, 0, 2).reshape(C, FF)
    w2 = op["fc2_weight"].reshape(FF, C)
    vecs = jnp.stack([op[n].reshape(C) for n in VEC_LABELS]).astype(f32)
    b1 = op["fc1_bias"].reshape(1, FF).astype(f32)
    bias = score_bias(op["table"].transpose(1, 0, 2).reshape(-1, HEADS))
    limit = jnp.sum(
        jnp.where(jnp.arange(image_counts.shape[0], dtype=jnp.int32) == group, image_counts, 0)
    )
    nlive = jnp.clip(limit * PIX - rank * rows, 0, rows).reshape(1)
    output, grad_input, gqkv, gproj, g1, g2, gvec, gb1, acc = block_compute(
        tokens, cotangent, nlive, wqkv, wproj, w1, w2, vecs, b1, bias
    )
    gtable = table_back(acc)
    gvec = gvec.reshape(8, ranks, width)
    pieces = [
        gqkv.reshape(3, ranks, heads, HD, C).transpose(1, 4, 2, 0, 3).reshape(ranks, -1),
        gproj.reshape(ranks, -1),
        g1.reshape(C, ranks, hidden).transpose(1, 0, 2).reshape(ranks, -1),
        g2.T.reshape(ranks, -1),
    ]
    pieces += [gvec[i].astype(bf16) for i in range(7)]
    pieces += [gb1.reshape(ranks, hidden).astype(bf16), gvec[7].astype(bf16)]
    pieces += [gtable.reshape(-1, ranks, heads).transpose(1, 0, 2).reshape(ranks, -1).astype(bf16)]
    used = sum(p.shape[1] for p in pieces)
    pieces.append(jnp.zeros((ranks, length - used), bf16))
    flat = jnp.concatenate(pieces, axis=1)
    flat = lax.psum_scatter(flat, "mp", scatter_dimension=0, tiled=True)
    grad_shard = lax.psum_scatter(flat, "dp", scatter_dimension=1, tiled=True).astype(f32)
    weights_rank = (4 * C * C + 2 * C * FF) // ranks
    position = group * shard_length + jnp.arange(shard_length, dtype=jnp.int32)[None, :]
    decays = (position < weights_rank).astype(jnp.float32)
    new_one = beta_one * moment_one + (1.0 - beta_one) * grad_shard
    new_two = second_decay_rate * moment_two + (1.0 - second_decay_rate) * grad_shard * grad_shard
    corrected_one = new_one / (1.0 - beta_one**adam_step)
    corrected_two = new_two / (1.0 - second_decay_rate**adam_step)
    new_params = params - learn_rate * (
        corrected_one / (jnp.sqrt(corrected_two) + adam_eps) + weight_decay * decays * params
    )
    return (output, grad_input, grad_shard, new_params, new_one, new_two)


def solution(mesh):
    return jax.shard_map(
        local,
        mesh=mesh,
        in_specs=(
            P(("dp", "mp"), None),
            P(("dp", "mp"), None),
            P(),
            P("mp", "dp"),
            P("mp", "dp"),
            P("mp", "dp"),
        ),
        out_specs=(
            P(("dp", "mp"), None),
            P(("dp", "mp"), None),
            P("mp", "dp"),
            P("mp", "dp"),
            P("mp", "dp"),
            P("mp", "dp"),
        ),
        check_vma=False,
    )
```

time: 1350 us -> 643 us (0.48)
  waiting for transfers between devices: 775 us -> 361 us
  local copies, waits for them, and re-layouts: 297 us -> 159 us
  matrix products: 94.6 us -> 1.36 us
  Pallas kernels: 0 us -> 83.6 us
  other arithmetic: 92.8 us -> 10.3 us
  blocking collectives: 63.1 us -> 0 us
    reduce_scatter x4 -> x0, waiting for transfers between devices: 412 us -> none  [the longest x1 120 us: head_block(): lax.psum_scatter(feed_part.astype(jnp.bfloat16), 'mp', scatter_dimension=...]
    all_gather x4 -> x2, waiting for transfers between devices: 288 us -> 108 us  [the longest x1 64.4 us: local(): owned = lax.all_gather(params.astype(bf16), 'mp', axis=0, tiled=True)]
    unnamed x12 -> x6, waiting for transfers between devices: 75 us -> 253 us
    another operation x27 -> x13, local copies, waits for them, and re-layouts: 129 us -> 20.9 us  [the longest x1 15.3 us: local(): op['qkv_weight'].reshape(ranks, C, heads, 3, HD).transpose(3, 0, 2, 4, 1)]
    dot_general x20 -> x3, matrix products: 94.6 us -> 1.36 us  [the longest x1 0.81 us: score_bias(): bias = jnp.dot(table.T.astype(bf16), onehot.T, preferred_element_type=f32)]
    pallas_call x0 -> x1, Pallas kernels: none -> 83.6 us  [block_compute(): pl.pallas_call(functools.partial(compute_kernel, images, rows, block, len...]
    reduce_sum x10 -> x0, other arithmetic: 49.9 us -> none  [the longest x1 25.9 us: head_block(): jnp.sum(split[:, :, 2, :], axis=0).reshape(1, width_rank)]
    unnamed x1 -> x0, blocking collectives: 35.4 us -> none
  transfers between devices with their start and end apart: 10 -> 4, of which waited for: 10 -> 4; matrix products, arithmetic and copies ran while one was open for 9% -> 0% of each run, Pallas kernels for 0% -> 0%
where the time goes in v1:
time: 643 us; the launch traced here: 631 us
  waiting for transfers between devices  361 us (56%)
  local copies, waits for them, and re-layouts  159 us (25%)
  Pallas kernels  83.6 us (13%)
  between operations  15.5 us (2%)
  other arithmetic  10.3 us (2%)
    unnamed x6, waiting for transfers between devices  253 us
    unnamed x47, local copies, waits for them, and re-layouts  84.1 us
    pallas_call x1, Pallas kernels, block_compute(): pl.pallas_call(functools.partial(compute_kernel, images, rows, block, len...  83.6 us
    all_gather x1, waiting for transfers between devices, local(): owned = lax.all_gather(params.astype(bf16), 'mp', axis=0, tiled=True)  64.4 us
    all_gather x1, waiting for transfers between devices, local(): owned = lax.all_gather(owned, 'dp', axis=1, tiled=True)  44 us
    reshape x2, local copies, waits for them, and re-layouts, local(): gqkv.reshape(3, ranks, heads, HD, C).transpose(1, 4, 2, 0, 3)  15.5 us
    another operation x1, local copies, waits for them, and re-layouts, local(): op['qkv_weight'].reshape(ranks, C, heads, 3, HD).transpose(3, 0, 2, 4, 1)  15.3 us
  transfers between devices with their start and end apart: 4, of which 4 were waited for; matrix products, arithmetic and copies ran while one was open for 0% of the time, Pallas kernels for 0%

profile of v1, /device:TPU:0, one launch (start us, length us, event | category | flops | bytes accessed | tf_op | source)
XLA Modules:
  0.0 630.7 jit_solution(10433924828808079886)
XLA Ops:
  7.2 2.0 convert_bitcast_fusion
  9.3 64.4 %all-gather.5.cloned.1.call-done = bf16[8,1,98581]{2,1,0:T(2,128)(2,1)} async-done(((bf16[1,1,98581]{2,1,0:T(2,128)(2,1)}), bf16[8,1,98581]{2,1,0:T(2,128)(2,1)}) %all-gather.5.cloned.1.call-update) | async-done | bytes 1577312 | tf_op jit(solution)/shard_map/all_gather | solution.py:429
  73.7 3.2 copy.84
  77.0 0.6 fusion.8
  78.3 44.0 %all-gather.7.cloned.1.call-done = bf16[4,98581,8]{1,2,0:T(8,128)(2,1)} async-done(((bf16[1,98581,8]{1,2,0:T(8,128)(2,1)}), bf16[4,98581,8]{1,2,0:T(8,128)(2,1)}) %all-gather.7.cloned.1.call-update) | async-done | bytes 6309200 | tf_op jit(solution)/shard_map/all_gather | solution.py:430
  122.3 7.9 %copy.86 = bf16[4,98581,8]{1,0,2:T(4,128)(2,1)} copy(bf16[4,98581,8]{1,2,0:T(8,128)(2,1)} %all-gather.7.cloned.1.call-done) | data formatting | bytes 12618368 | tf_op jit(solution)/shard_map/all_gather | solution.py:430
  130.1 12.2 %reshape.160 = bf16[3154592]{0:T(1024)(128)(2,1)} reshape(bf16[8,4,98581]{2,1,0:T(4,128)(2,1)} %bitcast.73) | data formatting | bytes 12618368
  142.4 13.7 %reshape.161 = bf16[8,394324]{1,0:T(8,128)(2,1)} reshape(bf16[3154592]{0:T(1024)(128)(2,1)} %reshape.160) | data formatting | bytes 12618368
  156.0 3.6 bitcast_bitcast_fusion
  159.9 1.3 slice.108
  161.1 1.6 fusion.11
  162.7 0.6 copy.77
  164.1 0.6 convert_element_type.80.vecs
  164.7 0.1 copy.63
  164.8 0.1 reshape.129
  165.0 0.1 copy.64
  165.1 1.0 reshape_reshape.10.wproj
  166.1 3.9 reshape_reshape.11.w2
  170.1 2.0 copy.76
  172.1 3.4 reshape.162
  175.5 0.8 convolution_bitcast_fusion
  176.3 0.6 broadcast_add_fusion
  176.9 2.1 add.60.bias
  179.0 15.3 %reshape_reshape.9 = bf16[8,512,2,3,32]{4,3,2,1,0:T(4,128)(2,1)} reshape(bf16[786432]{0:T(1024)(128)(2,1)} %reshape.162) | data formatting | bytes 3145728 | tf_op jit(solution)/shard_map/reshape;reshape | solution.py:432
  194.3 11.8 %copy.62 = bf16[3,8,2,32,512]{4,3,2,1,0:T(8,128)(2,1)} copy(bf16[3,8,2,32,512]{3,0,2,4,1:T(4,128)(2,1)} %bitcast.71) | data formatting | bytes 3145728 | tf_op jit(solution)/shard_map/transpose | solution.py:432
  206.1 83.6 %shard_map.145 = (bf16[784,512]{1,0:T(8,128)(2,1)}, bf16[784,512]{1,0:T(8,128)(2,1)}, bf16[1536,512]{1,0:T(8,128)(2,1)}, bf16[512,512]{1,0:T(8,128)(2,1)}, bf16[...) custom-call(s32[1]{0:T(128)} %bitcast.nlive, ...), custom_call_target="tpu_custom_call" | custom-call | tf_op jit(solution)/shard_map/pallas_call | solution.py:342
  289.7 0.7 convert_reduce_fusion
  290.4 0.7 convert.11
  291.9 1.3 reshape.133
  293.2 1.2 reshape.137
  294.4 0.2 reshape.138
  294.6 0.3 fusion.6
  294.9 0.3 fusion.1
  295.2 0.2 copy.69
  295.4 0.1 convert_element_type.100
  295.6 2.3 copy.78
  297.9 3.9 copy.67
  301.8 3.9 reshape.136
  305.7 12.3 %copy.66 = bf16[3,8,2,32,512]{3,0,2,4,1:T(4,128)(2,1)} copy(bf16[3,8,2,32,512]{4,3,2,1,0:T(8,128)(2,1)} %bitcast.82) | data formatting | bytes 3145728 | tf_op jit(solution)/shard_map/reshape | solution.py:449
  318.0 14.3 %reshape.164 = bf16[786432]{0:T(1024)(128)(2,1)} reshape(bf16[8,512,2,3,32]{4,3,2,1,0:T(4,128)(2,1)} %bitcast.72) | data formatting | bytes 3145728
  332.3 3.2 reshape.132
  335.5 2.7 constant_dynamic-update-slice_fusion.3
  338.2 0.9 constant_dynamic-update-slice_fusion.2
  339.0 1.5 constant_dynamic-update-slice_fusion.1
  340.5 0.8 copy-done
  341.4 1.4 constant_dynamic-update-slice_fusion
  342.8 1.3 dynamic-update-slice.4
  344.1 1.4 dynamic-update-slice.5
  345.6 1.3 dynamic-update-slice.6
  346.9 1.4 dynamic-update-slice.7
  348.3 1.3 dynamic-update-slice.8
  349.6 1.4 dynamic-update-slice.9
  351.0 1.3 dynamic-update-slice.10
  352.3 1.4 dynamic-update-slice.11
  353.7 1.4 dynamic-update-slice.12
  355.2 1.3 dynamic-update-slice.13
  356.5 1.4 dynamic-update-slice.14
  357.9 0.6 copy-done.9
  358.5 0.6 dynamic-slice
  359.1 211.5 %all-reduce.6.cloned.1.call-done = bf16[8,394324]{1,0:T(8,128)(2,1)} async-done(((bf16[8,394324]{1,0:T(8,128)(2,1)}), bf16[8,394324]{1,0:T(8,128)(2,1)}) %all-reduce.6.cloned.1.call-update) | async-done | bytes 6309200
  570.6 6.0 constant_dynamic-slice_fusion
  576.6 0.6 dynamic-slice.2
  577.9 41.2 %all-reduce.8.cloned.1.call-done = bf16[1,394324]{1,0:T(2,128)(2,1)} async-done(((bf16[1,394324]{1,0:T(2,128)(2,1)}), bf16[1,394324]{1,0:T(2,128)(2,1)}) %all-reduce.8.cloned.1.call-update) | async-done | bytes 788664
  619.1 4.9 multiply_subtract_fusion
  (56 shorter events, 2.1 us)
Async XLA Ops:
  7.2 66.5 %all-gather.5.cloned.1.call-start = ((), (), s32[]{:S(2)}) async-start(), calls=%async_computation | async-start | bytes 3552768 | tf_op jit(solution)/shard_map/all_gather | solution.py:429
  9.3 67.7 %copy-start.7 = (s32[4]{0:T(128)S(1)}, s32[4]{0:T(128)}, u32[]{:S(2)}) copy-start(s32[4]{0:T(128)} %param.12) | copy-start | bytes 52
  9.3 113.0 %all-gather.7.cloned.1.call-start = ((), (), s32[]{:S(2)}) async-start(), calls=%async_computation.1 | async-start | bytes 7895040 | tf_op jit(solution)/shard_map/all_gather | solution.py:430
  76.9 493.6 %all-reduce.6.cloned.1.call-start = ((), (), s32[]{:S(2)}) async-start(), calls=%async_computation.2 | async-start | bytes 12619776
  172.1 3.4 copy-start.3
  172.1 4.3 copy-start.6
  291.2 3.5 copy-start.1
  339.0 2.3 copy-start
  357.8 0.7 copy-start.9
  357.8 261.2 %all-reduce.8.cloned.1.call-start = ((), (), s32[]{:S(2)}) async-start(), calls=%async_computation.3 | async-start | bytes 3154944
  570.6 6.0 copy-start.8
  570.6 48.5 %copy-start.2 = (f32[1,98581]{1,0:T(1,128)S(1)}, f32[1,98581]{1,0:T(1,128)}, u32[]{:S(2)}) copy-start(f32[1,98581]{1,0:T(1,128)} %param.13) | copy-start | bytes 1182976
  570.6 48.5 %copy-start.4 = (f32[1,98581]{1,0:T(1,128)S(1)}, f32[1,98581]{1,0:T(1,128)}, u32[]{:S(2)}) copy-start(f32[1,98581]{1,0:T(1,128)} %param.14) | copy-start | bytes 1182976
  570.6 48.5 %copy-start.5 = (f32[1,98581]{1,0:T(1,128)S(1)}, f32[1,98581]{1,0:T(1,128)}, u32[]{:S(2)}) copy-start(f32[1,98581]{1,0:T(1,128)} %param.15) | copy-start | bytes 1182976
Sparse Core Ops, SparseCore 0:
  10.8 62.9 all-gather.4
  77.1 45.1 all-gather.6
  358.0 212.5 all-reduce.5
  576.7 42.2 all-reduce.7

commit v2 on v1

--- a/solution.py
+++ b/solution.py
@@ -374,6 +374,969 @@
     )(nlive, x, cot, wqkv, wproj, w1, w2, vecs, b1, bias, sel)
     return (outs[0][:tokens], outs[1][:tokens]) + outs[2:]
 
+LINES = 4
+MPS = 8
+DPS = 4
+QROWS = 384
+QUART = QROWS * 256
+FLAT = 776
+MESH = pl.DeviceIdType.MESH
+
+
+def base_of(p):
+    return (p // WIN) * SPAN + p % WIN
+
+
+def iota(shape, dim):
+    return lax.broadcasted_iota(jnp.int32, shape, dim)
+
+
+def as_bf(mask):
+    return jnp.where(mask, 1.0, 0.0).astype(bf16)
+
+
+def spread_queries():
+    row = iota((GH * 256, GH * SEG), 0)
+    lane = iota((GH * 256, GH * SEG), 1)
+    q = lane % SEG
+    return as_bf((row // 256 == lane // SEG) & (row % 256 == base_of(q)) & (q < WIN * WIN))
+
+
+def key_rows(reverse):
+    k = iota((SEG, 8 * WIN), 0)
+    row = iota((SEG, 8 * WIN), 1)
+    b = WIN - 1 - k % WIN if reverse else k % WIN
+    return as_bf((row == (k // WIN) * 8 + b) & (k < WIN * WIN))
+
+
+def table_lanes():
+    row = iota((384, 512), 0)
+    lane = iota((384, 512), 1)
+    return as_bf((row == 2 * (lane % 256) + lane // 256) & (lane % 256 < SPAN * SPAN))
+
+
+def split_mm(op, exact, value):
+    hi = value.astype(bf16)
+    lo = (value - hi.astype(f32)).astype(bf16)
+    return op(exact, hi) + op(exact, lo)
+
+
+def split_mm_left(op, value, exact):
+    hi = value.astype(bf16)
+    lo = (value - hi.astype(f32)).astype(bf16)
+    return op(hi, exact) + op(lo, exact)
+
+
+def turn_rows(part):
+    return pltpu.roll(part, 0, 1, stride=1, stride_axis=0)
+
+
+def gather_smalls(sm, vecs, b1, tabs, bias, mask):
+    lane = iota((16, 128), 1)
+    low = lane < 64
+    for g in range(4):
+        first, second = sm[2 * g].astype(f32), sm[2 * g + 1].astype(f32)
+        turned = [pltpu.roll(first, 64, 1), pltpu.roll(second, 64, 1)]
+        los = jnp.where(low, first, turned[1])
+        his = jnp.where(low, turned[0], second)
+        gl = slice(g * 128, (g + 1) * 128)
+        for i, src, row in (
+            (0, los, 0), (1, his, 0), (2, los, 1), (3, his, 1), (4, los, 2), (5, his, 2), (6, los, 3), (7, his, 5),
+        ):
+            vecs[i : i + 1, gl] = src[row : row + 1]
+        for k in range(2):
+            r = 2 * g + k
+            full = (first, second)[k]
+            rot = turned[k]
+            b1[:, r * 256 : r * 256 + 128] = jnp.where(low[:1], rot[3:4], rot[4:5])
+            b1[:, r * 256 + 128 : r * 256 + 256] = jnp.where(low[:1], rot[4:5], rot[5:6])
+            for j in range(3):
+                tabs[r : r + 1, j * 128 : (j + 1) * 128] = full[6 + j : 7 + j]
+    tab = mm(tabs[...].astype(bf16), table_lanes())
+    spread = spread_queries()
+    keys = key_rows(False)
+    for g in range(NG):
+        parts = []
+        for h in range(GH):
+            r, i = divmod(g * GH + h, 2)
+            t = jnp.broadcast_to(tab[r : r + 1, i * 256 : (i + 1) * 256], (8, 256))
+            rows = [
+                turn_rows(pltpu.roll(t, (SPAN * a - 84) % 256, 1)) for a in range(WIN)
+            ]
+            parts.append(jnp.concatenate(rows, axis=0))
+        line = jnp.concatenate(parts, axis=1).astype(bf16)
+        placed = mm(line, spread).astype(bf16)
+        bt = mm(keys, placed)
+        for w in range(NW):
+            bias[w * NG + g] = bt + mask[w]
+
+
+def scatter_smalls(gvec, gb1, acc, gsm, tabs):
+    lane = iota((1, 128), 1)
+    low = lane < 64
+    spread = spread_queries()
+    keys = key_rows(True)
+    tabs[...] = jnp.zeros_like(tabs)
+    for g in range(NG):
+        z = split_mm(mm_r, keys, acc[g])
+        y = split_mm_left(mm_t, z, spread)
+        for h in range(GH):
+            r, i = divmod(g * GH + h, 2)
+            total = jnp.zeros((8, 256), f32)
+            for a in range(WIN):
+                part = y[8 * a : 8 * a + 8, h * 256 : (h + 1) * 256]
+                total = total + turn_rows(pltpu.roll(part, (78 - SPAN * a) % 256, 1))
+            tabs[r : r + 1, i * 256 : (i + 1) * 256] = jnp.sum(total, axis=0, keepdims=True)
+    flat = split_mm_left(mm_t, tabs[...], table_lanes())
+
+    def half(i, r):
+        g, k = divmod(r, 2)
+        v = gvec[i : i + 1, g * 128 : (g + 1) * 128]
+        turned = pltpu.roll(v, 64, 1)
+        return (v, turned) if k == 0 else (turned, v)
+
+    zero = jnp.zeros((1, 128), f32)
+    for r in range(MPS):
+        fb0 = gb1[:, r * 256 : r * 256 + 128]
+        fb1 = gb1[:, r * 256 + 128 : r * 256 + 256]
+        t0, t1 = pltpu.roll(fb0, 64, 1), pltpu.roll(fb1, 64, 1)
+        rows = [
+            jnp.where(low, half(0, r)[0], half(1, r)[1]),
+            jnp.where(low, half(2, r)[0], half(3, r)[1]),
+            jnp.where(low, half(4, r)[0], half(5, r)[1]),
+            jnp.where(low, half(6, r)[0], t0),
+            jnp.where(low, t0, t1),
+            jnp.where(low, t1, half(7, r)[1]),
+        ]
+        for j, row in enumerate(rows):
+            gsm[r, j : j + 1, :] = row
+        for j in range(3):
+            gsm[r, 6 + j : 7 + j, :] = flat[r : r + 1, j * 128 : (j + 1) * 128]
+        for j in range(9, 16):
+            gsm[r, j : j + 1, :] = zero
+
+
+def slot(m, d):
+    return m * DPS + d
+
+
+def w_qkv(wb, kind, quad, half):
+    return jnp.concatenate(
+        [wb[slot(4 * quad + r, 0), half * 192 + kind * 64 : half * 192 + kind * 64 + 64, :] for r in range(4)], axis=0
+    )
+
+
+def w_proj(wb, quad, half):
+    return jnp.concatenate([wb[slot(4 * quad + r, 1), half * 64 : half * 64 + 64, :] for r in range(4)], axis=0)
+
+
+def w_one(wb, r, half):
+    return wb[slot(r, 1), 128:384, :] if half == 0 else wb[slot(r, 2), 0:256, :]
+
+
+def w_two(wb, r, half):
+    return jnp.concatenate(
+        [
+            wb[slot(r, 2), 256 + half * 64 : 256 + half * 64 + 64, :],
+            wb[slot(r, 3), half * 192 : half * 192 + 192, :],
+        ],
+        axis=0,
+    )
+
+
+HALVES = (slice(0, 256), slice(256, 512))
+
+
+def mega_compute(images, rows, block, length, live_rows, x, cot, wb, vecs, b1, bias, sel, out, gin, gb, gvec, gb1, acc, sc):
+    blocks = rows // block
+    frame = image_frames(images)[0]
+    head_of_lane = lane_head_mask()
+    ln1, qkv, wq, probs, mixw, mixed, ln2, act, gpre, gresb, gres, gmix, gwin, goutb = sc
+
+    def vec(i):
+        return vecs[i : i + 1, :]
+
+    gvec[...] = jnp.zeros_like(gvec)
+    gb1[...] = jnp.zeros_like(gb1)
+    acc[...] = jnp.zeros_like(acc)
+    mixed[...] = jnp.zeros_like(mixed)
+
+    def norm_rows(t, _):
+        sl = pl.ds(pl.multiple_of(t * block, 16), block)
+        xin = x[sl, :].astype(f32)
+        center, scale = norm_stats(xin)
+        normed = ((xin - center) * scale * vec(0) + vec(1)).astype(bf16)
+        ln1[sl, :] = normed
+        for kind in range(3):
+            for quad in range(2):
+                cols = slice(kind * C + quad * 256, kind * C + quad * 256 + 256)
+                val = mm_t(normed[:, HALVES[0]], w_qkv(wb, kind, quad, 0)) + mm_t(
+                    normed[:, HALVES[1]], w_qkv(wb, kind, quad, 1)
+                )
+                qs = slice(quad * 256, quad * 256 + 256)
+                if kind == 0:
+                    val = (val + vecs[2:3, qs]) * HD ** (-0.5)
+                if kind == 2:
+                    val = val + vecs[3:4, qs]
+                qkv[sl, cols] = val.astype(bf16)
+        return 0
+
+    lax.fori_loop(0, blocks, norm_rows, 0)
+
+    for i in range(images):
+        fr = pl.ds(frame[i], length)
+        wq[i] = mm(sel[i], qkv[fr, :]).astype(bf16)
+
+        def window(w, _):
+            ws = pl.ds(pl.multiple_of(w * SEG, SEG), SEG)
+            for g in range(NG):
+                q = wq[i, ws, g * 128 : (g + 1) * 128]
+                k = wq[i, ws, C + g * 128 : C + (g + 1) * 128]
+                v = wq[i, ws, 2 * C + g * 128 : 2 * C + (g + 1) * 128]
+                st = mm_t(k, block_diag(q, head_of_lane)) + bias[w * NG + g]
+                e = jnp.exp(st - jnp.max(st, axis=0, keepdims=True))
+                pt = (e * (1.0 / jnp.sum(e, axis=0, keepdims=True))).astype(bf16)
+                probs[i, w * NG + g] = pt
+                mixw[ws, g * 128 : (g + 1) * 128] = diag_pick(mm_r(pt, v), head_of_lane).astype(bf16)
+            return 0
+
+        lax.fori_loop(0, NW, window, 0)
+        mixed[fr, :] = (mixed[fr, :].astype(f32) + mm_r(sel[i], mixw[...])).astype(bf16)
+
+    def middle(t, _):
+        sl = pl.ds(pl.multiple_of(t * block, 16), block)
+        xin = x[sl, :].astype(f32)
+        att = [
+            mm(mixed[sl, HALVES[0]], w_proj(wb, 0, h)) + mm(mixed[sl, HALVES[1]], w_proj(wb, 1, h)) for h in range(2)
+        ]
+        res = xin + (jnp.concatenate(att, axis=1) + vec(4))
+        center, scale = norm_stats(res)
+        unit = (res - center) * scale
+        normed = (unit * vec(5) + vec(6)).astype(bf16)
+        ln2[sl, :] = normed
+        live = (iota((block, 1), 0) + t * block < live_rows).astype(f32)
+        gout = live * cot[sl, :].astype(f32)
+        gob = gout.astype(bf16)
+        goutb[sl, :] = gob
+        feed = [jnp.zeros((block, 256), f32)] * 2
+        gln = [jnp.zeros((block, 256), f32)] * 2
+        for r in range(MPS):
+            js = slice(r * 256, (r + 1) * 256)
+            pre = mm(normed[:, HALVES[0]], w_one(wb, r, 0)) + mm(normed[:, HALVES[1]], w_one(wb, r, 1)) + b1[:, js]
+            phi, e = phi_parts(pre)
+            av = (pre * phi).astype(bf16)
+            act[sl, js] = av
+            feed = [feed[h] + mm(av, w_two(wb, r, h)) for h in range(2)]
+            ga = mm_t(gob[:, HALVES[0]], w_two(wb, r, 0)) + mm_t(gob[:, HALVES[1]], w_two(wb, r, 1))
+            gp = ga * (phi + pre * (e * (1.0 / math.sqrt(2.0 * math.pi))))
+            gb1[:, js] += jnp.sum(gp, axis=0, keepdims=True)
+            gpb = gp.astype(bf16)
+            gpre[sl, js] = gpb
+            gln = [gln[h] + mm_t(gpb, w_one(wb, r, h)) for h in range(2)]
+        feed = jnp.concatenate(feed, axis=1)
+        gln = jnp.concatenate(gln, axis=1)
+        out[sl, :] = (live * (res + feed + vec(7))).astype(bf16)
+        gr = gout + norm_back(gln * vec(5), unit, scale)
+        gres[sl, :] = gr
+        grb = gr.astype(bf16)
+        gresb[sl, :] = grb
+        for quad in range(2):
+            gmix[sl, HALVES[quad]] = (
+                mm_t(grb[:, HALVES[0]], w_proj(wb, quad, 0)) + mm_t(grb[:, HALVES[1]], w_proj(wb, quad, 1))
+            ).astype(bf16)
+        gvec[4:5, :] += jnp.sum(gr, axis=0, keepdims=True)
+        gvec[5:6, :] += jnp.sum(gln * unit, axis=0, keepdims=True)
+        gvec[6:7, :] += jnp.sum(gln, axis=0, keepdims=True)
+        gvec[7:8, :] += jnp.sum(gout, axis=0, keepdims=True)
+        return 0
+
+    lax.fori_loop(0, blocks, middle, 0)
+
+    def ff_grads(r, _):
+        js = pl.ds(pl.multiple_of(r * 256, 256), 256)
+        two = mm_r(act[:, js], goutb[...]).astype(bf16)
+        for h in range(2):
+            gb[slot(r, 2), 256 + h * 64 : 256 + h * 64 + 64, :] = two[0:64, HALVES[h]]
+            gb[slot(r, 3), h * 192 : h * 192 + 192, :] = two[64:256, HALVES[h]]
+        one = mm_r(ln2[...], gpre[:, js]).astype(bf16)
+        gb[slot(r, 1), 128:384, :] = one[0:256]
+        gb[slot(r, 2), 0:256, :] = one[256:512]
+        return 0
+
+    lax.fori_loop(0, MPS, ff_grads, 0)
+    gproj = mm_r(mixed[...], gresb[...]).astype(bf16)
+    for r in range(MPS):
+        for h in range(2):
+            gb[slot(r, 1), h * 64 : h * 64 + 64, :] = gproj[r * 64 : r * 64 + 64, HALVES[h]]
+
+    qkv[...] = jnp.zeros_like(qkv)
+    for i in range(images):
+        fr = pl.ds(frame[i], length)
+        mixw[...] = mm(sel[i], gmix[fr, :]).astype(bf16)
+
+        def window(w, _):
+            ws = pl.ds(pl.multiple_of(w * SEG, SEG), SEG)
+            for g in range(NG):
+                q = wq[i, ws, g * 128 : (g + 1) * 128]
+                k = wq[i, ws, C + g * 128 : C + (g + 1) * 128]
+                v = wq[i, ws, 2 * C + g * 128 : 2 * C + (g + 1) * 128]
+                pt = probs[i, w * NG + g]
+                dod = block_diag(mixw[ws, g * 128 : (g + 1) * 128], head_of_lane)
+                gv = mm(pt, dod)
+                dpt = mm_t(v, dod)
+                ptf = pt.astype(f32)
+                prod = ptf * dpt
+                dst = prod - ptf * jnp.sum(prod, axis=0, keepdims=True)
+                acc[g] += dst
+                dsb = dst.astype(bf16)
+                gk = mm(dsb, block_diag(q, head_of_lane))
+                gq = diag_pick(mm_r(dsb, k), head_of_lane) * HD ** (-0.5)
+                gl = slice(g * 128, (g + 1) * 128)
+                gvec[2:3, gl] += jnp.sum(gq, axis=0, keepdims=True)
+                gvec[3:4, gl] += jnp.sum(gv, axis=0, keepdims=True)
+                gwin[ws, g * 128 : (g + 1) * 128] = gq.astype(bf16)
+                gwin[ws, C + g * 128 : C + (g + 1) * 128] = gk.astype(bf16)
+                gwin[ws, 2 * C + g * 128 : 2 * C + (g + 1) * 128] = gv.astype(bf16)
+            return 0
+
+        lax.fori_loop(0, NW, window, 0)
+        qkv[fr, :] = (qkv[fr, :].astype(f32) + mm_r(sel[i], gwin[...])).astype(bf16)
+
+    def last(t, _):
+        sl = pl.ds(pl.multiple_of(t * block, 16), block)
+        gln = [jnp.zeros((block, 256), f32)] * 2
+        for kind in range(3):
+            for quad in range(2):
+                part = qkv[sl, kind * C + quad * 256 : kind * C + quad * 256 + 256]
+                gln = [gln[h] + mm(part, w_qkv(wb, kind, quad, h)) for h in range(2)]
+        gln = jnp.concatenate(gln, axis=1)
+        xin = x[sl, :].astype(f32)
+        center, scale = norm_stats(xin)
+        unit = (xin - center) * scale
+        gvec[0:1, :] += jnp.sum(gln * unit, axis=0, keepdims=True)
+        gvec[1:2, :] += jnp.sum(gln, axis=0, keepdims=True)
+        gin[sl, :] = (gres[sl, :] + norm_back(gln * vec(0), unit, scale)).astype(bf16)
+        return 0
+
+    lax.fori_loop(0, blocks, last, 0)
+
+    for kind in range(3):
+        for quad in range(2):
+            cols = slice(kind * C + quad * 256, kind * C + quad * 256 + 256)
+            part = mm_r(qkv[:, cols], ln1[...]).astype(bf16)
+            for r in range(4):
+                for h in range(2):
+                    gb[slot(4 * quad + r, 0), h * 192 + kind * 64 : h * 192 + kind * 64 + 64, :] = part[
+                        r * 64 : r * 64 + 64, HALVES[h]
+                    ]
+
+
+def mega_scratch(images, rows):
+    return [
+        pltpu.VMEM((rows, C), bf16),
+        pltpu.VMEM((rows, 3 * C), bf16),
+        pltpu.VMEM((images, NW * SEG, 3 * C), bf16),
+        pltpu.VMEM((images, NW * NG, SEG, GH * SEG), bf16),
+        pltpu.VMEM((NW * SEG, C), bf16),
+        pltpu.VMEM((rows, C), bf16),
+        pltpu.VMEM((rows, C), bf16),
+        pltpu.VMEM((rows, FF), bf16),
+        pltpu.VMEM((rows, FF), bf16),
+        pltpu.VMEM((rows, C), bf16),
+        pltpu.VMEM((rows, C), f32),
+        pltpu.VMEM((rows, C), bf16),
+        pltpu.VMEM((NW * SEG, 3 * C), bf16),
+        pltpu.VMEM((rows, C), bf16),
+    ]
+
+
+def score_masks():
+    _, ids = window_sites()
+    size = WIN * WIN
+    full = np.zeros((NW, SEG, SEG), np.float32)
+    full[:, size:, :] = -1e30
+    full[:, :size, :size] = np.where(ids[:, :, None] == ids[:, None, :], 0.0, mask_fill)
+    return np.tile(full, (1, 1, GH))
+
+
+def place():
+    d, m = lax.axis_index("dp"), lax.axis_index("mp")
+    return d, m, d // 2, d % 2, m // 2, m % 2
+
+
+def twin(a, j):
+    if j == 0:
+        return a
+    if j == 1:
+        return a + 1 - 2 * (a % 2)
+    if j == 2:
+        return (a + 2) % LINES
+    return LINES - 1 - a
+
+
+def remote(src, dst, send, recv, dev):
+    return pltpu.make_async_remote_copy(
+        src_ref=src, dst_ref=dst, send_sem=send, recv_sem=recv, device_id=dev, device_id_type=MESH
+    )
+
+
+def peers():
+    d, m, *_ = place()
+    return [{"dp": (d + k) % DPS, "mp": m} for k in range(1, DPS)] + [
+        {"dp": d, "mp": (m + k) % MPS} for k in range(1, MPS)
+    ]
+
+
+def greet():
+    barrier = pltpu.get_barrier_semaphore()
+    group = peers()
+    for dev in group:
+        pl.semaphore_signal(barrier, inc=1, device_id=dev, device_id_type=MESH)
+    pl.semaphore_wait(barrier, len(group))
+
+
+OFFSET = 277
+
+
+def flatten_params(pf, fl, roll, head, head_sem, wide, wb, sm):
+    d, m, *_ = place()
+    lane = iota((FLAT, 128), 1)
+    roll[0:8, :] = jnp.zeros((8, 128), f32)
+    fl[FLAT : FLAT + 16, :] = jnp.zeros((16, 128), f32)
+    for k in range(DPS):
+
+        @pl.when(d == k)
+        def _(k=k):
+            lanes, down = OFFSET * k % 128, OFFSET * k // 128
+            if k == 0:
+                fl[0:FLAT, :] = pf[...]
+            else:
+                roll[8 : 8 + FLAT, :] = pltpu.roll(pf[...], lanes, 1)
+                fl[down : down + FLAT, :] = jnp.where(
+                    lane >= lanes, roll[8 : 8 + FLAT, :], roll[7 : 7 + FLAT, :]
+                )
+
+    over = remote(fl.at[768:784], head.at[0], head_sem.at[0], head_sem.at[1], {"dp": (d + 1) % DPS, "mp": m})
+
+    @pl.when(d < DPS - 1)
+    def _():
+        over.start()
+
+    @pl.when(d > 0)
+    def _():
+        over.wait_recv()
+        pos = iota((8, 128), 0) * 128 + iota((8, 128), 1)
+        fl[0:8, :] = jnp.where(pos < OFFSET * d, head[0, 0:8, :], fl[0:8, :])
+
+    def cut(start, size, step):
+        return fl[pl.ds(start, size, stride=step), :]
+
+    @pl.when(d == 0)
+    def _():
+        low = iota((256, 128), 1) < 64
+        one, two = pltpu.roll(cut(1, 256, 3), 64, 1), pltpu.roll(cut(2, 256, 3), 64, 1)
+        wide[pl.ds(0, 256, stride=2), :] = cut(0, 256, 3)
+        wide[pl.ds(C, 256, stride=2), :] = cut(1, 256, 3)
+        wide[pl.ds(1, 256, stride=2), :] = jnp.where(low, one, two)
+        wide[pl.ds(C + 1, 256, stride=2), :] = two
+        turned = jnp.concatenate([wide[0:C, :].T, wide[C : 2 * C, :].T], axis=0).astype(bf16)
+        s = slot(m, 0)
+        for half in range(2):
+            for kind in range(3):
+                for i in range(2):
+                    to = half * 192 + kind * 64 + i * 32
+                    frm = i * 96 + kind * 32
+                    wb[s, to : to + 32, :] = turned[frm : frm + 32, HALVES[half]]
+
+    @pl.when(d == 1)
+    def _():
+        s = slot(m, 1)
+        for j in range(2):
+            js = slice(j * 128, (j + 1) * 128)
+            for half in range(2):
+                wb[s, half * 64 : half * 64 + 64, js] = cut(2 * half + j, 64, 4).astype(bf16)
+            wb[s, 128:384, js] = cut(256 + j, 256, 2).astype(bf16)
+
+    @pl.when(d == 2)
+    def _():
+        s = slot(m, 2)
+        for j in range(2):
+            js = slice(j * 128, (j + 1) * 128)
+            wb[s, 0:256, js] = cut(j, 256, 2).astype(bf16)
+            for half in range(2):
+                at = 256 + half * 64
+                wb[s, at : at + 64, js] = cut(512 + 2 * half + j, 64, 4).astype(bf16)
+
+    @pl.when(d == 3)
+    def _():
+        s = slot(m, 3)
+        for j in range(2):
+            js = slice(j * 128, (j + 1) * 128)
+            for half in range(2):
+                wb[s, half * 192 : half * 192 + 192, js] = cut(2 * half + j, 192, 4).astype(bf16)
+        sm[m] = fl[768:784, :].astype(bf16)
+
+    @pl.when(d < DPS - 1)
+    def _():
+        over.wait_send()
+
+
+def smalls_out(sm, ssem, rsem):
+    d, m, *_ = place()
+
+    def over_dp(k):
+        return remote(sm.at[m], sm.at[m], ssem.at[k], rsem.at[m], {"dp": k, "mp": m})
+
+    def over_mp(k):
+        return remote(sm.at[m], sm.at[m], ssem.at[3 + k], rsem.at[m], {"dp": d, "mp": (m + k) % MPS})
+
+    @pl.when(d == DPS - 1)
+    def _():
+        for k in range(DPS - 1):
+            over_dp(k).start()
+
+    @pl.when(d < DPS - 1)
+    def _():
+        over_dp(0).wait_recv()
+
+    for k in range(1, MPS):
+        over_mp(k).start()
+
+    def finish():
+        for k in range(1, MPS):
+            src = (m + k) % MPS
+            remote(sm.at[src], sm.at[src], ssem.at[0], rsem.at[src], {"dp": d, "mp": src}).wait_recv()
+
+    def drain():
+        @pl.when(d == DPS - 1)
+        def _():
+            for k in range(DPS - 1):
+                over_dp(k).wait_send()
+
+        for k in range(1, MPS):
+            over_mp(k).wait_send()
+
+    return finish, drain
+
+
+RIGHT, LEFT, SIDE_Y, SIDE_X, CORE = range(5)
+
+
+def blocks_out(wb, ssem, rsem):
+    d, m, x, c, a, b = place()
+    dev = {
+        RIGHT: {"dp": d, "mp": (m + 2) % MPS},
+        LEFT: {"dp": d, "mp": (m + MPS - 2) % MPS},
+        SIDE_Y: {"dp": d, "mp": m + 1 - 2 * b},
+        SIDE_X: {"dp": (d + 2) % DPS, "mp": m},
+        CORE: {"dp": d + 1 - 2 * c, "mp": m},
+    }
+    d_far = (d + 2) % DPS
+    d_twin = d + 1 - 2 * c
+    sends = []
+
+    def copy(s, way):
+        return remote(wb.at[s], wb.at[s], ssem.at[s, way], rsem.at[s], dev[way])
+
+    def go(s, way, cond=None):
+        sends.append((s, way, cond))
+        if cond is None:
+            copy(s, way).start()
+        else:
+            pl.when(cond)(lambda: copy(s, way).start())
+
+    def arrive(s):
+        copy(s, CORE).wait_recv()
+
+    def line_step(j):
+        far = twin(a, j)
+        s = slot(2 * far + b, d)
+        if j == 0:
+            go(s, RIGHT, a < LINES - 1)
+            go(s, LEFT, a > 0)
+        else:
+            arrive(s)
+            go(s, RIGHT, (far < a) & (a < LINES - 1))
+            go(s, LEFT, (far > a) & (a > 0))
+        go(s, SIDE_X)
+        go(s, SIDE_Y)
+        go(s, CORE)
+
+    def y_step(j):
+        s = slot(2 * twin(a, j) + 1 - b, d)
+        arrive(s)
+        go(s, SIDE_X)
+        go(s, CORE)
+
+    def x_step(j, same):
+        row = 2 * twin(a, j) + (b if same else 1 - b)
+        s = slot(row, d_far)
+        arrive(s)
+        go(s, CORE)
+
+    def core_step(row, dd):
+        arrive(slot(row, dd))
+
+    def drain():
+        for s, way, cond in sends:
+            if cond is None:
+                copy(s, way).wait_send()
+            else:
+                pl.when(cond)(lambda: copy(s, way).wait_send())
+
+    steps = [
+        lambda: line_step(0),
+        lambda: line_step(1),
+        lambda: y_step(0),
+        lambda: x_step(0, True),
+        lambda: line_step(2),
+        lambda: y_step(1),
+        lambda: x_step(1, True),
+        lambda: line_step(3),
+        lambda: x_step(0, False),
+        lambda: y_step(2),
+        lambda: x_step(2, True),
+        lambda: y_step(3),
+        lambda: x_step(1, False),
+        lambda: x_step(3, True),
+        lambda: x_step(2, False),
+        lambda: x_step(3, False),
+    ]
+    for row in range(MPS):
+        for dd in (d_twin, (d_twin + 2) % DPS):
+            steps.append(functools.partial(core_step, row, dd))
+    return steps, drain
+
+
+def blocks_in(gb, rc, rx, ry, rz, total, s_core, r_core, s_x, r_x, s_y, r_y, s_z, r_z):
+    d, m, x, c, a, b = place()
+    d_far = (d + 2) % DPS
+    d_twin = d + 1 - 2 * c
+    to_core = {"dp": d_twin, "mp": m}
+    to_x = {"dp": d_far, "mp": m}
+    to_y = {"dp": d, "mp": m + 1 - 2 * b}
+    to_left = {"dp": d, "mp": (m + MPS - 2) % MPS}
+    to_right = {"dp": d, "mp": (m + 2) % MPS}
+
+    def by_core(j, row):
+        dd = (d_twin + 2) % DPS if j == 0 else d_twin
+        k = j * MPS + row
+        return remote(gb.at[slot(row, dd)], rc.at[k], s_core.at[k], r_core.at[k], to_core)
+
+    def by_x(row):
+        return remote(gb.at[slot(row, d_far)], rx.at[row], s_x.at[row], r_x.at[row], to_x)
+
+    def by_y(t):
+        return remote(gb.at[slot(2 * t + 1 - b, d)], ry.at[t], s_y.at[t], r_y.at[t], to_y)
+
+    def by_z(t, side, dev):
+        return remote(gb.at[slot(2 * t + b, d)], rz.at[t, side], s_z.at[t], r_z.at[t, side], dev)
+
+    def add(s, got):
+        gb[s] = (gb[s].astype(f32) + got[...].astype(f32)).astype(bf16)
+
+    def start_core():
+        for j in range(2):
+            lax.fori_loop(0, MPS, lambda row, _: (by_core(j, row).start(), 0)[1], 0)
+
+    def over_x(row, _):
+        by_core(0, row).wait_recv()
+        add(slot(row, d_far), rc.at[row])
+        by_x(row).start()
+        return 0
+
+    def keep(row, _):
+        by_core(1, row).wait_recv()
+        add(slot(row, d), rc.at[MPS + row])
+        return 0
+
+    def over_y(t, _):
+        row = 2 * t + 1 - b
+        by_x(row).wait_recv()
+        add(slot(row, d), rx.at[row])
+        by_y(t).start()
+        return 0
+
+    def own_y(t, _):
+        row = 2 * t + b
+        by_x(row).wait_recv()
+        add(slot(row, d), rx.at[row])
+        by_y(t).wait_recv()
+        add(slot(row, d), ry.at[t])
+        return 0
+
+    def along_z(t):
+        s = slot(2 * t + b, d)
+
+        @pl.when((t < a) & (a < LINES - 1))
+        def _():
+            by_z(t, 1, to_left).wait_recv()
+            add(s, rz.at[t, 1])
+
+        @pl.when((t > a) & (a > 0))
+        def _():
+            by_z(t, 0, to_right).wait_recv()
+            add(s, rz.at[t, 0])
+
+        @pl.when(t < a)
+        def _():
+            by_z(t, 1, to_left).start()
+
+        @pl.when(t > a)
+        def _():
+            by_z(t, 0, to_right).start()
+
+    def finish():
+        for t in (0, LINES - 1, 1, LINES - 2):
+            along_z(t)
+        total[...] = gb[slot(m, d)].astype(f32)
+
+        @pl.when(a < LINES - 1)
+        def _():
+            by_z(a, 1, to_left).wait_recv()
+            total[...] += rz[a, 1].astype(f32)
+
+        @pl.when(a > 0)
+        def _():
+            by_z(a, 0, to_right).wait_recv()
+            total[...] += rz[a, 0].astype(f32)
+
+    def drain():
+        for j in range(2):
+            lax.fori_loop(0, MPS, lambda row, _: (by_core(j, row).wait_send(), 0)[1], 0)
+        lax.fori_loop(0, MPS, lambda row, _: (by_x(row).wait_send(), 0)[1], 0)
+        lax.fori_loop(0, LINES, lambda t, _: (by_y(t).wait_send(), 0)[1], 0)
+        for t in range(LINES):
+
+            @pl.when(t != a)
+            def _(t=t):
+                by_z(t, 0, to_right).wait_send()
+
+    start_core()
+    lax.fori_loop(0, MPS, over_x, 0)
+    lax.fori_loop(0, MPS, keep, 0)
+    lax.fori_loop(0, LINES, over_y, 0)
+    lax.fori_loop(0, LINES, own_y, 0)
+    finish()
+    drain()
+
+
+def smalls_in(gsm, got, part, got2, total, ssem, rsem, rsem2):
+    d, m, *_ = place()
+
+    def over_mp(k):
+        dst = (m + k) % MPS
+        return remote(gsm.at[dst], got.at[k], ssem.at[k], rsem.at[k], {"dp": d, "mp": dst})
+
+    def over_dp(k):
+        return remote(part, got2.at[k], ssem.at[0], rsem2.at[k], {"dp": DPS - 1, "mp": m})
+
+    for k in range(1, MPS):
+        over_mp(k).start()
+    value = gsm[m]
+    for k in range(1, MPS):
+        over_mp(k).wait_recv()
+        value = value + got[k]
+    part[...] = value
+    for k in range(DPS - 1):
+
+        @pl.when(d == k)
+        def _(k=k):
+            over_dp(k).start()
+
+    @pl.when(d == DPS - 1)
+    def _():
+        total[...] = part[...]
+        for k in range(DPS - 1):
+            over_dp(k).wait_recv()
+            total[...] += got2[k]
+
+    for k in range(DPS - 1):
+
+        @pl.when(d == k)
+        def _(k=k):
+            over_dp(k).wait_send()
+
+    for k in range(1, MPS):
+        over_mp(k).wait_send()
+
+
+def flat_grads(total, smalls, fl, roll, head, head_sem, wide, tall, gflat):
+    d, m, *_ = place()
+    fl[768:792, :] = jnp.zeros((24, 128), f32)
+
+    def put(start, size, step, val):
+        fl[pl.ds(start, size, stride=step), :] = val
+
+    @pl.when(d == 0)
+    def _():
+        tall[192:256, :] = jnp.zeros((64, C), f32)
+        for half in range(2):
+            for kind in range(3):
+                for i in range(2):
+                    frm = half * 192 + kind * 64 + i * 32
+                    to = i * 96 + kind * 32
+                    tall[to : to + 32, HALVES[half]] = total[frm : frm + 32, :]
+        wide[0:C, :] = tall[0:128, :].T
+        wide[C : 2 * C, :] = tall[128:256, :].T
+        low = iota((256, 128), 1) < 64
+
+        def every(start):
+            return wide[pl.ds(start, 256, stride=2), :]
+
+        one, two = pltpu.roll(every(1), 64, 1), pltpu.roll(every(C + 1), 64, 1)
+        put(0, 256, 3, every(0))
+        put(1, 256, 3, jnp.where(low, every(C), one))
+        put(2, 256, 3, jnp.where(low, one, two))
+
+    @pl.when(d == 1)
+    def _():
+        for j in range(2):
+            js = slice(j * 128, (j + 1) * 128)
+            for half in range(2):
+                put(2 * half + j, 64, 4, total[half * 64 : half * 64 + 64, js])
+            put(256 + j, 256, 2, total[128:384, js])
+
+    @pl.when(d == 2)
+    def _():
+        for j in range(2):
+            js = slice(j * 128, (j + 1) * 128)
+            put(j, 256, 2, total[0:256, js])
+            for half in range(2):
+                at = 256 + half * 64
+                put(512 + 2 * half + j, 64, 4, total[at : at + 64, js])
+
+    @pl.when(d == 3)
+    def _():
+        for j in range(2):
+            js = slice(j * 128, (j + 1) * 128)
+            for half in range(2):
+                put(2 * half + j, 192, 4, total[half * 192 : half * 192 + 192, js])
+        fl[768:784, :] = smalls[...]
+
+    back = remote(fl.at[0:8], head.at[1, 0:8], head_sem.at[2], head_sem.at[3], {"dp": (d + DPS - 1) % DPS, "mp": m})
+
+    @pl.when(d > 0)
+    def _():
+        back.start()
+
+    @pl.when(d < DPS - 1)
+    def _():
+        back.wait_recv()
+        fl[768:776, :] = head[1, 0:8, :]
+
+    lane = iota((FLAT, 128), 1)
+    for k in range(DPS):
+
+        @pl.when(d == k)
+        def _(k=k):
+            lanes, down = OFFSET * k % 128, OFFSET * k // 128
+            if k == 0:
+                gflat[...] = fl[0:FLAT, :]
+            else:
+                roll[0:784, :] = pltpu.roll(fl[0:784, :], 128 - lanes, 1)
+                roll[784:792, :] = jnp.zeros((8, 128), f32)
+                gflat[...] = jnp.where(lane < 128 - lanes, roll[down : down + FLAT, :], roll[down + 1 : down + 1 + FLAT, :])
+
+    @pl.when(d > 0)
+    def _():
+        back.wait_send()
+
+
+def step_kernel(images, rows, block, length, *refs):
+    (nlive, x, cot, pf, sel, mask) = refs[:6]
+    (out, gin, gflat) = refs[6:9]
+    (
+        fl, roll, head, wide, tall, wb, sm, vecs, b1, tabs, tabs2, bias, gvec, gb1, acc, gb, gsm, got, part, got2,
+        stotal, rc, rx, ry, rz, total,
+        head_sem, sm_s, sm_r, ag_s, ag_r, rsm_s, rsm_r, rsm_r2, s_core, r_core, s_x, r_x, s_y, r_y, s_z, r_z,
+    ) = refs[9:51]
+    sc = refs[51:]
+    greet()
+    flatten_params(pf, fl, roll, head, head_sem, wide, wb, sm)
+    steps, drain = blocks_out(wb, ag_s, ag_r)
+    steps[0]()
+    finish_sm, drain_sm = smalls_out(sm, sm_s, sm_r)
+    for step in steps[1:]:
+        step()
+    finish_sm()
+    gather_smalls(sm, vecs, b1, tabs, bias, mask)
+    mega_compute(images, rows, block, length, nlive[0], x, cot, wb, vecs, b1, bias, sel, out, gin, gb, gvec, gb1, acc, sc)
+    scatter_smalls(gvec, gb1, acc, gsm, tabs2)
+    blocks_in(gb, rc, rx, ry, rz, total, s_core, r_core, s_x, r_x, s_y, r_y, s_z, r_z)
+    smalls_in(gsm, got, part, got2, stotal, rsm_s, rsm_r, rsm_r2)
+    flat_grads(total, stotal, fl, roll, head, head_sem, wide, tall, gflat)
+    drain()
+    drain_sm()
+
+
+def step_call(x, cot, nlive, pf):
+    rows = x.shape[0]
+    images = rows // PIX
+    block = block_size(rows)
+    length = image_frames(images)[2]
+    sel = jnp.asarray(placement(images), bf16)
+    mask = jnp.asarray(score_masks(), f32)
+    vmem = pl.BlockSpec(memory_space=pltpu.VMEM)
+    smem = pl.BlockSpec(memory_space=pltpu.SMEM)
+    s = jax.ShapeDtypeStruct
+    dma = pltpu.SemaphoreType.DMA
+    nb = MPS * DPS
+    return pl.pallas_call(
+        functools.partial(step_kernel, images, rows, block, length),
+        out_shape=(s((rows, C), bf16), s((rows, C), bf16), s((FLAT, 128), f32)),
+        in_specs=[smem] + [vmem] * 5,
+        out_specs=(vmem,) * 3,
+        scratch_shapes=[
+            pltpu.VMEM((792, 128), f32),
+            pltpu.VMEM((792, 128), f32),
+            pltpu.VMEM((2, 16, 128), f32),
+            pltpu.VMEM((2 * C, 128), f32),
+            pltpu.VMEM((256, C), f32),
+            pltpu.VMEM((nb, QROWS, 256), bf16),
+            pltpu.VMEM((MPS, 16, 128), bf16),
+            pltpu.VMEM((8, C), f32),
+            pltpu.VMEM((1, FF), f32),
+            pltpu.VMEM((MPS, 384), f32),
+            pltpu.VMEM((MPS, 512), f32),
+            pltpu.VMEM((NW * NG, SEG, GH * SEG), f32),
+            pltpu.VMEM((8, C), f32),
+            pltpu.VMEM((1, FF), f32),
+            pltpu.VMEM((NG, SEG, GH * SEG), f32),
+            pltpu.VMEM((nb, QROWS, 256), bf16),
+            pltpu.VMEM((MPS, 16, 128), f32),
+            pltpu.VMEM((MPS, 16, 128), f32),
+            pltpu.VMEM((16, 128), f32),
+            pltpu.VMEM((DPS, 16, 128), f32),
+            pltpu.VMEM((16, 128), f32),
+            pltpu.VMEM((2 * MPS, QROWS, 256), bf16),
+            pltpu.VMEM((MPS, QROWS, 256), bf16),
+            pltpu.VMEM((LINES, QROWS, 256), bf16),
+            pltpu.VMEM((LINES, 2, QROWS, 256), bf16),
+            pltpu.VMEM((QROWS, 256), f32),
+            dma((4,)),
+            dma((3 + MPS,)),
+            dma((MPS,)),
+            dma((nb, 5)),
+            dma((nb,)),
+            dma((MPS,)),
+            dma((MPS,)),
+            dma((DPS,)),
+            dma((2 * MPS,)),
+            dma((2 * MPS,)),
+            dma((MPS,)),
+            dma((MPS,)),
+            dma((LINES,)),
+            dma((LINES,)),
+            dma((LINES,)),
+            dma((LINES, 2)),
+        ]
+        + mega_scratch(images, rows),
+        compiler_params=pltpu.CompilerParams(
+            vmem_limit_bytes=62 * 1024 * 1024, collective_id=0, has_side_effects=True
+        ),
+    )(nlive, x, cot, pf, sel, mask)
+
 
 VEC_LABELS = [
     "norm1_gain",
@@ -416,7 +1379,23 @@
     return pieces
 
 
-def local(tokens, cotangent, image_counts, params, moment_one, moment_two):
+def finish(output, grad_input, grad_shard, params, moment_one, moment_two):
+    group = lax.axis_index("dp")
+    shard_length = params.shape[1]
+    weights_rank = (4 * C * C + 2 * C * FF) // lax.axis_size("mp")
+    position = group * shard_length + jnp.arange(shard_length, dtype=jnp.int32)[None, :]
+    decays = (position < weights_rank).astype(jnp.float32)
+    new_one = beta_one * moment_one + (1.0 - beta_one) * grad_shard
+    new_two = second_decay_rate * moment_two + (1.0 - second_decay_rate) * grad_shard * grad_shard
+    corrected_one = new_one / (1.0 - beta_one**adam_step)
+    corrected_two = new_two / (1.0 - second_decay_rate**adam_step)
+    new_params = params - learn_rate * (
+        corrected_one / (jnp.sqrt(corrected_two) + adam_eps) + weight_decay * decays * params
+    )
+    return (output, grad_input, grad_shard, new_params, new_one, new_two)
+
+
+def local_xla(tokens, cotangent, image_counts, params, moment_one, moment_two):
     ranks = lax.axis_size("mp")
     rank = lax.axis_index("mp")
     group = lax.axis_index("dp")
@@ -459,17 +1438,32 @@
     flat = jnp.concatenate(pieces, axis=1)
     flat = lax.psum_scatter(flat, "mp", scatter_dimension=0, tiled=True)
     grad_shard = lax.psum_scatter(flat, "dp", scatter_dimension=1, tiled=True).astype(f32)
-    weights_rank = (4 * C * C + 2 * C * FF) // ranks
-    position = group * shard_length + jnp.arange(shard_length, dtype=jnp.int32)[None, :]
-    decays = (position < weights_rank).astype(jnp.float32)
-    new_one = beta_one * moment_one + (1.0 - beta_one) * grad_shard
-    new_two = second_decay_rate * moment_two + (1.0 - second_decay_rate) * grad_shard * grad_shard
-    corrected_one = new_one / (1.0 - beta_one**adam_step)
-    corrected_two = new_two / (1.0 - second_decay_rate**adam_step)
-    new_params = params - learn_rate * (
-        corrected_one / (jnp.sqrt(corrected_two) + adam_eps) + weight_decay * decays * params
+    return finish(output, grad_input, grad_shard, params, moment_one, moment_two)
+
+
+def local(tokens, cotangent, image_counts, params, moment_one, moment_two):
+    ranks = lax.axis_size("mp")
+    rows = tokens.shape[0]
+    shard = params.shape[1]
+    fits = (
+        ranks == MPS
+        and lax.axis_size("dp") == DPS
+        and rows % 16 == 0
+        and image_frames(rows // PIX)[0][-1] + image_frames(rows // PIX)[2] <= rows
+        and shard == QUART + OFFSET
     )
-    return (output, grad_input, grad_shard, new_params, new_one, new_two)
+    if not fits:
+        return local_xla(tokens, cotangent, image_counts, params, moment_one, moment_two)
+    rank = lax.axis_index("mp")
+    group = lax.axis_index("dp")
+    limit = jnp.sum(
+        jnp.where(jnp.arange(image_counts.shape[0], dtype=jnp.int32) == group, image_counts, 0)
+    )
+    nlive = jnp.clip(limit * PIX - rank * rows, 0, rows).reshape(1)
+    pf = jnp.pad(params, ((0, 0), (0, FLAT * 128 - shard))).reshape(FLAT, 128)
+    output, grad_input, gflat = step_call(tokens, cotangent, nlive, pf)
+    grad_shard = gflat.reshape(1, -1)[:, :shard]
+    return finish(output, grad_input, grad_shard, params, moment_one, moment_two)
 
 
 def solution(mesh):

time: 643 us -> 226 us (0.35); the launches traced: 631 us -> 226 us
  waiting for transfers between devices: 361 us -> 0 us
  local copies, waits for them, and re-layouts: 159 us -> 4.99 us
  Pallas kernels: 83.6 us -> 214 us
  between operations: 15.5 us -> 1.35 us
    unnamed x6 -> x0, waiting for transfers between devices: 253 us -> none
    pallas_call x1, Pallas kernels: 83.6 us -> 214 us  [step_call(): pl.pallas_call(functools.partial(step_kernel, images, rows, block, length...]
    all_gather x2 -> x0, waiting for transfers between devices: 108 us -> none  [the longest x1 64.4 us: local(): owned = lax.all_gather(params.astype(bf16), 'mp', axis=0, tiled=True)]
    unnamed x47 -> x14, local copies, waits for them, and re-layouts: 84.1 us -> 2.97 us
    reshape x8 -> x0, local copies, waits for them, and re-layouts: 22.2 us -> none  [the longest x2 15.5 us: local(): gqkv.reshape(3, ranks, heads, HD, C).transpose(1, 4, 2, 0, 3)]
    another operation x13 -> x0, local copies, waits for them, and re-layouts: 20.9 us -> none  [the longest x1 15.3 us: local(): op['qkv_weight'].reshape(ranks, C, heads, 3, HD).transpose(3, 0, 2, 4, 1)]
    transpose x3 -> x0, local copies, waits for them, and re-layouts: 15.9 us -> none  [the longest x1 11.8 us: local(): op['qkv_weight'].reshape(ranks, C, heads, 3, HD).transpose(3, 0, 2, 4, 1)]
    all_gather x1 -> x0, local copies, waits for them, and re-layouts: 7.89 us -> none  [local(): owned = lax.all_gather(owned, 'dp', axis=1, tiled=True)]
  transfers between devices with their start and end apart: 4 -> 0, of which waited for: 4 -> 0; matrix products, arithmetic and copies ran while one was open for 0% -> 0% of each run, Pallas kernels for 0% -> 0%
where the time goes in v2:
time: 226 us
  Pallas kernels  214 us (95%)
  other arithmetic  5.39 us (2%)
  local copies, waits for them, and re-layouts  4.99 us (2%)
    pallas_call x1, Pallas kernels, step_call(): pl.pallas_call(functools.partial(step_kernel, images, rows, block, length...  214 us
    sub x1, other arithmetic, finish(): params - learn_rate * (corrected_one / (jnp.sqrt(corrected_two) + adam_ep...  4.75 us

profile of v2, /device:TPU:0, one launch (start us, length us, event | category | flops | bytes accessed | tf_op | source)
XLA Modules:
  0.0 225.7 jit_solution(13592497592155364833)
XLA Ops:
  0.6 0.0 copy-start.5
  0.6 0.6 copy-done.5
  1.3 0.6 fusion.3
  2.6 2.0 pad.4
  4.6 0.0 copy-start
  4.6 0.0 copy-start.3
  4.6 0.0 copy-start.4
  4.6 213.9 %shard_map.127 = (bf16[784,512]{1,0:T(8,128)(2,1)}, bf16[784,512]{1,0:T(8,128)(2,1)}, f32[776,128]{1,0:T(8,128)}) custom-call(s32[1]{0:T(128)} %bitcast.refs_0_, bf16[784,512]{1,0:T(8,128)(2,1)} %refs_1_.1, bf16[784,512]{1,0:T(8,128)(2,1)} %refs_2_.1, f32[776,128]{1,0:T(8,128)} %bitcast.3, bf16[4,256,208]{2,1,0:T(8,128)(2,1)} %constant.43.clone.refs_4_, ...), custom_call_target="tpu_custom_call" | custom-call | tf_op jit(solution)/shard_map/pallas_call | solution.py:1285
  218.6 0.0 copy-done
  218.6 0.0 copy-done.3
  218.6 0.0 copy-done.4
  218.6 0.0 copy-start.2
  218.6 4.8 %multiply_subtract_fusion = (f32[1,98581]{1,0:T(1,128)}, f32[1,98581]{1,0:T(1,128)}, f32[1,98581]{1,0:T(1,128)}, f32[1,98581]{1,0:T(1,128)}) fusion(f32[1,98581]{1,0:T(1,128)S(1)} %copy-done, s32[]{:T(128)S(6)} %mul.56, f32[1,98581]{1,0:T(1,128)S(1)} %copy-done.3, f32[1,98581]{1,0:T(1,128)S(1)} %copy-done.4, f32[1,99328]{1,0:T(1,128)} %bitcast.4), kind=kLoop, calls=%fused_computation.5 | loop fusion | flops 1774458 | bytes 3154596 | tf_op jit(solution)/shard_map/sub | solution.py:1392
  223.4 0.0 copy-done.2
  223.4 0.0 copy-start.1
  223.4 0.9 copy.16
  224.3 0.5 copy-done.1
  224.8 0.9 copy.17
Async XLA Ops:
  0.6 0.7 copy-start.5
  4.6 214.0 %copy-start = (f32[1,98581]{1,0:T(1,128)S(1)}, f32[1,98581]{1,0:T(1,128)}, u32[]{:S(2)}) copy-start(f32[1,98581]{1,0:T(1,128)} %param.11) | copy-start | bytes 1182976
  4.6 214.0 %copy-start.3 = (f32[1,98581]{1,0:T(1,128)S(1)}, f32[1,98581]{1,0:T(1,128)}, u32[]{:S(2)}) copy-start(f32[1,98581]{1,0:T(1,128)} %param.12) | copy-start | bytes 1182976
  4.6 214.0 %copy-start.4 = (f32[1,98581]{1,0:T(1,128)S(1)}, f32[1,98581]{1,0:T(1,128)}, u32[]{:S(2)}) copy-start(f32[1,98581]{1,0:T(1,128)} %param.13) | copy-start | bytes 1182976
  218.6 4.8 %copy-start.2 = (bf16[784,512]{1,0:T(8,128)(2,1)S(1)}, bf16[784,512]{1,0:T(8,128)(2,1)}, u32[]{:S(2)}) copy-start(bf16[784,512]{1,0:T(8,128)(2,1)} %get-tuple-element.22) | copy-start | bytes 2408452
  223.4 1.4 copy-start.1

commit v3 on v2

--- a/solution.py
+++ b/solution.py
@@ -63,15 +63,7 @@
 
 
 def phi_parts(v):
-    z = jnp.abs(v) * (1.0 / math.sqrt(2.0))
-    t = 1.0 / (1.0 + 0.3275911 * z)
-    poly = t * (
-        0.254829592
-        + t * (-0.284496736 + t * (1.421413741 + t * (-1.453152027 + t * 1.061405429)))
-    )
-    e = jnp.exp(-0.5 * v * v)
-    tail = 0.5 * poly * e
-    return jnp.where(v >= 0, 1.0 - tail, tail), e
+    return 0.5 * (1.0 + lax.erf(v * (1.0 / math.sqrt(2.0)))), jnp.exp(-0.5 * v * v)
 
 
 def window_sites():
@@ -547,47 +539,37 @@
 HALVES = (slice(0, 256), slice(256, 512))
 
 
-def mega_compute(images, rows, block, length, live_rows, x, cot, wb, vecs, b1, bias, sel, out, gin, gb, gvec, gb1, acc, sc):
-    blocks = rows // block
+def first_norm(x, vecs, ln1):
+    xin = x[...].astype(f32)
+    center, scale = norm_stats(xin)
+    ln1[...] = ((xin - center) * scale * vecs[0:1, :] + vecs[1:2, :]).astype(bf16)
+
+
+def project_qkv(wb, vecs, ln1, qkv, poll):
+    for kind in range(3):
+        for quad in range(2):
+            poll(2 * kind + quad)
+            qs = HALVES[quad]
+            val = mm_t(ln1[:, HALVES[0]], w_qkv(wb, kind, quad, 0)) + mm_t(
+                ln1[:, HALVES[1]], w_qkv(wb, kind, quad, 1)
+            )
+            if kind == 0:
+                val = (val + vecs[2:3, qs]) * HD ** (-0.5)
+            if kind == 2:
+                val = val + vecs[3:4, qs]
+            qkv[:, kind * C + quad * 256 : kind * C + quad * 256 + 256] = val.astype(bf16)
+
+
+def attention_forward(images, length, sel, bias, qkv, wq, probs, mixw, mixed, poll):
+    head_of_lane = lane_head_mask()
     frame = image_frames(images)[0]
-    head_of_lane = lane_head_mask()
-    ln1, qkv, wq, probs, mixw, mixed, ln2, act, gpre, gresb, gres, gmix, gwin, goutb = sc
-
-    def vec(i):
-        return vecs[i : i + 1, :]
-
-    gvec[...] = jnp.zeros_like(gvec)
-    gb1[...] = jnp.zeros_like(gb1)
-    acc[...] = jnp.zeros_like(acc)
     mixed[...] = jnp.zeros_like(mixed)
-
-    def norm_rows(t, _):
-        sl = pl.ds(pl.multiple_of(t * block, 16), block)
-        xin = x[sl, :].astype(f32)
-        center, scale = norm_stats(xin)
-        normed = ((xin - center) * scale * vec(0) + vec(1)).astype(bf16)
-        ln1[sl, :] = normed
-        for kind in range(3):
-            for quad in range(2):
-                cols = slice(kind * C + quad * 256, kind * C + quad * 256 + 256)
-                val = mm_t(normed[:, HALVES[0]], w_qkv(wb, kind, quad, 0)) + mm_t(
-                    normed[:, HALVES[1]], w_qkv(wb, kind, quad, 1)
-                )
-                qs = slice(quad * 256, quad * 256 + 256)
-                if kind == 0:
-                    val = (val + vecs[2:3, qs]) * HD ** (-0.5)
-                if kind == 2:
-                    val = val + vecs[3:4, qs]
-                qkv[sl, cols] = val.astype(bf16)
-        return 0
-
-    lax.fori_loop(0, blocks, norm_rows, 0)
-
     for i in range(images):
         fr = pl.ds(frame[i], length)
         wq[i] = mm(sel[i], qkv[fr, :]).astype(bf16)
 
         def window(w, _):
+            poll(i, w)
             ws = pl.ds(pl.multiple_of(w * SEG, SEG), SEG)
             for g in range(NG):
                 q = wq[i, ws, g * 128 : (g + 1) * 128]
@@ -603,78 +585,81 @@
         lax.fori_loop(0, NW, window, 0)
         mixed[fr, :] = (mixed[fr, :].astype(f32) + mm_r(sel[i], mixw[...])).astype(bf16)
 
-    def middle(t, _):
-        sl = pl.ds(pl.multiple_of(t * block, 16), block)
-        xin = x[sl, :].astype(f32)
-        att = [
-            mm(mixed[sl, HALVES[0]], w_proj(wb, 0, h)) + mm(mixed[sl, HALVES[1]], w_proj(wb, 1, h)) for h in range(2)
-        ]
-        res = xin + (jnp.concatenate(att, axis=1) + vec(4))
-        center, scale = norm_stats(res)
-        unit = (res - center) * scale
-        normed = (unit * vec(5) + vec(6)).astype(bf16)
-        ln2[sl, :] = normed
-        live = (iota((block, 1), 0) + t * block < live_rows).astype(f32)
-        gout = live * cot[sl, :].astype(f32)
-        gob = gout.astype(bf16)
-        goutb[sl, :] = gob
-        feed = [jnp.zeros((block, 256), f32)] * 2
-        gln = [jnp.zeros((block, 256), f32)] * 2
-        for r in range(MPS):
-            js = slice(r * 256, (r + 1) * 256)
-            pre = mm(normed[:, HALVES[0]], w_one(wb, r, 0)) + mm(normed[:, HALVES[1]], w_one(wb, r, 1)) + b1[:, js]
-            phi, e = phi_parts(pre)
-            av = (pre * phi).astype(bf16)
-            act[sl, js] = av
-            feed = [feed[h] + mm(av, w_two(wb, r, h)) for h in range(2)]
-            ga = mm_t(gob[:, HALVES[0]], w_two(wb, r, 0)) + mm_t(gob[:, HALVES[1]], w_two(wb, r, 1))
-            gp = ga * (phi + pre * (e * (1.0 / math.sqrt(2.0 * math.pi))))
-            gb1[:, js] += jnp.sum(gp, axis=0, keepdims=True)
-            gpb = gp.astype(bf16)
-            gpre[sl, js] = gpb
-            gln = [gln[h] + mm_t(gpb, w_one(wb, r, h)) for h in range(2)]
-        feed = jnp.concatenate(feed, axis=1)
-        gln = jnp.concatenate(gln, axis=1)
-        out[sl, :] = (live * (res + feed + vec(7))).astype(bf16)
-        gr = gout + norm_back(gln * vec(5), unit, scale)
-        gres[sl, :] = gr
-        grb = gr.astype(bf16)
-        gresb[sl, :] = grb
-        for quad in range(2):
-            gmix[sl, HALVES[quad]] = (
-                mm_t(grb[:, HALVES[0]], w_proj(wb, quad, 0)) + mm_t(grb[:, HALVES[1]], w_proj(wb, quad, 1))
-            ).astype(bf16)
-        gvec[4:5, :] += jnp.sum(gr, axis=0, keepdims=True)
-        gvec[5:6, :] += jnp.sum(gln * unit, axis=0, keepdims=True)
-        gvec[6:7, :] += jnp.sum(gln, axis=0, keepdims=True)
-        gvec[7:8, :] += jnp.sum(gout, axis=0, keepdims=True)
-        return 0
-
-    lax.fori_loop(0, blocks, middle, 0)
-
-    def ff_grads(r, _):
-        js = pl.ds(pl.multiple_of(r * 256, 256), 256)
-        two = mm_r(act[:, js], goutb[...]).astype(bf16)
-        for h in range(2):
-            gb[slot(r, 2), 256 + h * 64 : 256 + h * 64 + 64, :] = two[0:64, HALVES[h]]
-            gb[slot(r, 3), h * 192 : h * 192 + 192, :] = two[64:256, HALVES[h]]
-        one = mm_r(ln2[...], gpre[:, js]).astype(bf16)
-        gb[slot(r, 1), 128:384, :] = one[0:256]
-        gb[slot(r, 2), 0:256, :] = one[256:512]
-        return 0
-
-    lax.fori_loop(0, MPS, ff_grads, 0)
+
+def feed_forward(rows, live_rows, x, cot, wb, vecs, b1, out, gvec, gb1, mixed, ln2, act, gpre, gresb, gres, gmix, goutb):
+    def vec(i):
+        return vecs[i : i + 1, :]
+
+    att = [mm(mixed[:, HALVES[0]], w_proj(wb, 0, h)) + mm(mixed[:, HALVES[1]], w_proj(wb, 1, h)) for h in range(2)]
+    res = x[...].astype(f32) + (jnp.concatenate(att, axis=1) + vec(4))
+    center, scale = norm_stats(res)
+    unit = (res - center) * scale
+    ln2[...] = (unit * vec(5) + vec(6)).astype(bf16)
+    live = (iota((rows, 1), 0) < live_rows).astype(f32)
+    gout = live * cot[...].astype(f32)
+    goutb[...] = gout.astype(bf16)
+    feed = [jnp.zeros((rows, 256), f32)] * 2
+    gln = [jnp.zeros((rows, 256), f32)] * 2
+    for r in range(MPS):
+        js = slice(r * 256, (r + 1) * 256)
+        pre = mm(ln2[:, HALVES[0]], w_one(wb, r, 0)) + mm(ln2[:, HALVES[1]], w_one(wb, r, 1)) + b1[:, js]
+        phi, e = phi_parts(pre)
+        av = (pre * phi).astype(bf16)
+        act[:, js] = av
+        feed = [feed[h] + mm(av, w_two(wb, r, h)) for h in range(2)]
+        ga = mm_t(goutb[:, HALVES[0]], w_two(wb, r, 0)) + mm_t(goutb[:, HALVES[1]], w_two(wb, r, 1))
+        gp = ga * (phi + pre * (e * (1.0 / math.sqrt(2.0 * math.pi))))
+        gb1[:, js] = jnp.sum(gp, axis=0, keepdims=True)
+        gpb = gp.astype(bf16)
+        gpre[:, js] = gpb
+        gln = [gln[h] + mm_t(gpb, w_one(wb, r, h)) for h in range(2)]
+    feed = jnp.concatenate(feed, axis=1)
+    gln = jnp.concatenate(gln, axis=1)
+    out[...] = (live * (res + feed + vec(7))).astype(bf16)
+    gr = gout + norm_back(gln * vec(5), unit, scale)
+    gres[...] = gr
+    grb = gr.astype(bf16)
+    gresb[...] = grb
+    for quad in range(2):
+        gmix[:, HALVES[quad]] = (
+            mm_t(grb[:, HALVES[0]], w_proj(wb, quad, 0)) + mm_t(grb[:, HALVES[1]], w_proj(wb, quad, 1))
+        ).astype(bf16)
+    gvec[4:5, :] = jnp.sum(gr, axis=0, keepdims=True)
+    gvec[5:6, :] = jnp.sum(gln * unit, axis=0, keepdims=True)
+    gvec[6:7, :] = jnp.sum(gln, axis=0, keepdims=True)
+    gvec[7:8, :] = jnp.sum(gout, axis=0, keepdims=True)
+
+
+def proj_grads(gb, mixed, gresb):
     gproj = mm_r(mixed[...], gresb[...]).astype(bf16)
     for r in range(MPS):
         for h in range(2):
             gb[slot(r, 1), h * 64 : h * 64 + 64, :] = gproj[r * 64 : r * 64 + 64, HALVES[h]]
 
+
+def feed_forward_grads(r, gb, act, goutb, ln2, gpre):
+    js = pl.ds(pl.multiple_of(r * 256, 256), 256)
+    two = mm_r(act[:, js], goutb[...]).astype(bf16)
+    for h in range(2):
+        gb[slot(r, 2), 256 + h * 64 : 256 + h * 64 + 64, :] = two[0:64, HALVES[h]]
+        gb[slot(r, 3), h * 192 : h * 192 + 192, :] = two[64:256, HALVES[h]]
+    one = mm_r(ln2[...], gpre[:, js]).astype(bf16)
+    gb[slot(r, 1), 128:384, :] = one[0:256]
+    gb[slot(r, 2), 0:256, :] = one[256:512]
+
+
+def attention_backward(images, length, sel, gmix, wq, probs, mixw, gwin, qkv, acc, gvec, poll):
+    head_of_lane = lane_head_mask()
+    frame = image_frames(images)[0]
     qkv[...] = jnp.zeros_like(qkv)
+    acc[...] = jnp.zeros_like(acc)
+    gvec[2:4, :] = jnp.zeros((2, C), f32)
     for i in range(images):
         fr = pl.ds(frame[i], length)
         mixw[...] = mm(sel[i], gmix[fr, :]).astype(bf16)
 
         def window(w, _):
+            poll(i, w)
             ws = pl.ds(pl.multiple_of(w * SEG, SEG), SEG)
             for g in range(NG):
                 q = wq[i, ws, g * 128 : (g + 1) * 128]
@@ -702,33 +687,33 @@
         lax.fori_loop(0, NW, window, 0)
         qkv[fr, :] = (qkv[fr, :].astype(f32) + mm_r(sel[i], gwin[...])).astype(bf16)
 
-    def last(t, _):
-        sl = pl.ds(pl.multiple_of(t * block, 16), block)
-        gln = [jnp.zeros((block, 256), f32)] * 2
-        for kind in range(3):
-            for quad in range(2):
-                part = qkv[sl, kind * C + quad * 256 : kind * C + quad * 256 + 256]
-                gln = [gln[h] + mm(part, w_qkv(wb, kind, quad, h)) for h in range(2)]
-        gln = jnp.concatenate(gln, axis=1)
-        xin = x[sl, :].astype(f32)
-        center, scale = norm_stats(xin)
-        unit = (xin - center) * scale
-        gvec[0:1, :] += jnp.sum(gln * unit, axis=0, keepdims=True)
-        gvec[1:2, :] += jnp.sum(gln, axis=0, keepdims=True)
-        gin[sl, :] = (gres[sl, :] + norm_back(gln * vec(0), unit, scale)).astype(bf16)
-        return 0
-
-    lax.fori_loop(0, blocks, last, 0)
-
+
+def qkv_grads(quad, gb, qkv, ln1):
+    for kind in range(3):
+        cols = slice(kind * C + quad * 256, kind * C + quad * 256 + 256)
+        part = mm_r(qkv[:, cols], ln1[...]).astype(bf16)
+        for r in range(4):
+            for h in range(2):
+                gb[slot(4 * quad + r, 0), h * 192 + kind * 64 : h * 192 + kind * 64 + 64, :] = part[
+                    r * 64 : r * 64 + 64, HALVES[h]
+                ]
+
+
+def first_norm_back(x, wb, vecs, qkv, gres, gin, gvec, poll):
+    rows = x.shape[0]
+    gln = [jnp.zeros((rows, 256), f32)] * 2
     for kind in range(3):
         for quad in range(2):
-            cols = slice(kind * C + quad * 256, kind * C + quad * 256 + 256)
-            part = mm_r(qkv[:, cols], ln1[...]).astype(bf16)
-            for r in range(4):
-                for h in range(2):
-                    gb[slot(4 * quad + r, 0), h * 192 + kind * 64 : h * 192 + kind * 64 + 64, :] = part[
-                        r * 64 : r * 64 + 64, HALVES[h]
-                    ]
+            poll(2 * kind + quad)
+            part = qkv[:, kind * C + quad * 256 : kind * C + quad * 256 + 256]
+            gln = [gln[h] + mm(part, w_qkv(wb, kind, quad, h)) for h in range(2)]
+    gln = jnp.concatenate(gln, axis=1)
+    xin = x[...].astype(f32)
+    center, scale = norm_stats(xin)
+    unit = (xin - center) * scale
+    gvec[0:1, :] = jnp.sum(gln * unit, axis=0, keepdims=True)
+    gvec[1:2, :] = jnp.sum(gln, axis=0, keepdims=True)
+    gin[...] = (gres[...] + norm_back(gln * vecs[0:1, :], unit, scale)).astype(bf16)
 
 
 def mega_scratch(images, rows):
@@ -922,203 +907,253 @@
 RIGHT, LEFT, SIDE_Y, SIDE_X, CORE = range(5)
 
 
-def blocks_out(wb, ssem, rsem):
-    d, m, x, c, a, b = place()
-    dev = {
-        RIGHT: {"dp": d, "mp": (m + 2) % MPS},
-        LEFT: {"dp": d, "mp": (m + MPS - 2) % MPS},
-        SIDE_Y: {"dp": d, "mp": m + 1 - 2 * b},
-        SIDE_X: {"dp": (d + 2) % DPS, "mp": m},
-        CORE: {"dp": d + 1 - 2 * c, "mp": m},
-    }
-    d_far = (d + 2) % DPS
-    d_twin = d + 1 - 2 * c
-    sends = []
-
-    def copy(s, way):
-        return remote(wb.at[s], wb.at[s], ssem.at[s, way], rsem.at[s], dev[way])
-
-    def go(s, way, cond=None):
-        sends.append((s, way, cond))
-        if cond is None:
-            copy(s, way).start()
+class BlocksOut:
+    def __init__(self, wb, ssem, rsem):
+        self.wb, self.ssem, self.rsem = wb, ssem, rsem
+        self.d, self.m, self.x, self.c, self.a, self.b = place()
+        d, m, b, c = self.d, self.m, self.b, self.c
+        self.far = (d + 2) % DPS
+        self.dev = {
+            RIGHT: {"dp": d, "mp": (m + 2) % MPS},
+            LEFT: {"dp": d, "mp": (m + MPS - 2) % MPS},
+            SIDE_Y: {"dp": d, "mp": m + 1 - 2 * b},
+            SIDE_X: {"dp": self.far, "mp": m},
+            CORE: {"dp": d + 1 - 2 * c, "mp": m},
+        }
+
+    def copy(self, s, way):
+        return remote(self.wb.at[s], self.wb.at[s], self.ssem.at[s, way], self.rsem.at[s], self.dev[way])
+
+    def arrive(self, s):
+        self.copy(s, CORE).wait_recv()
+
+    def ways_of_line(self, core, dd, j):
+        a = self.a
+        t = twin(a, j)
+        if j == 0:
+            ways = [(RIGHT, a < LINES - 1), (LEFT, a > 0)]
         else:
-            pl.when(cond)(lambda: copy(s, way).start())
-
-    def arrive(s):
-        copy(s, CORE).wait_recv()
-
-    def line_step(j):
-        far = twin(a, j)
-        s = slot(2 * far + b, d)
-        if j == 0:
-            go(s, RIGHT, a < LINES - 1)
-            go(s, LEFT, a > 0)
-        else:
-            arrive(s)
-            go(s, RIGHT, (far < a) & (a < LINES - 1))
-            go(s, LEFT, (far > a) & (a > 0))
-        go(s, SIDE_X)
-        go(s, SIDE_Y)
-        go(s, CORE)
-
-    def y_step(j):
-        s = slot(2 * twin(a, j) + 1 - b, d)
-        arrive(s)
-        go(s, SIDE_X)
-        go(s, CORE)
-
-    def x_step(j, same):
-        row = 2 * twin(a, j) + (b if same else 1 - b)
-        s = slot(row, d_far)
-        arrive(s)
-        go(s, CORE)
-
-    def core_step(row, dd):
-        arrive(slot(row, dd))
-
-    def drain():
-        for s, way, cond in sends:
+            ways = [(RIGHT, (t < a) & (a < LINES - 1)), (LEFT, (t > a) & (a > 0))]
+        if core:
+            ways.append((SIDE_X, None))
+        elif j == 0:
+            ways.insert(0, (SIDE_X, self.d == dd))
+        return slot(2 * t + self.b, dd), ways + [(SIDE_Y, None), (CORE, None)]
+
+    def ways_of_side(self, core, dd, j):
+        ways = [(SIDE_X, None)] if core else []
+        return slot(2 * twin(self.a, j) + 1 - self.b, dd), ways + [(CORE, None)]
+
+    def ways_of_cross(self, j, same):
+        return slot(2 * twin(self.a, j) + (self.b if same else 1 - self.b), self.far), [(CORE, None)]
+
+    def start(self, s, ways):
+        for way, cond in ways:
             if cond is None:
-                copy(s, way).wait_send()
+                self.copy(s, way).start()
             else:
-                pl.when(cond)(lambda: copy(s, way).wait_send())
-
-    steps = [
-        lambda: line_step(0),
-        lambda: line_step(1),
-        lambda: y_step(0),
-        lambda: x_step(0, True),
-        lambda: line_step(2),
-        lambda: y_step(1),
-        lambda: x_step(1, True),
-        lambda: line_step(3),
-        lambda: x_step(0, False),
-        lambda: y_step(2),
-        lambda: x_step(2, True),
-        lambda: y_step(3),
-        lambda: x_step(1, False),
-        lambda: x_step(3, True),
-        lambda: x_step(2, False),
-        lambda: x_step(3, False),
-    ]
-    for row in range(MPS):
-        for dd in (d_twin, (d_twin + 2) % DPS):
-            steps.append(functools.partial(core_step, row, dd))
-    return steps, drain
-
-
-def blocks_in(gb, rc, rx, ry, rz, total, s_core, r_core, s_x, r_x, s_y, r_y, s_z, r_z):
-    d, m, x, c, a, b = place()
-    d_far = (d + 2) % DPS
-    d_twin = d + 1 - 2 * c
-    to_core = {"dp": d_twin, "mp": m}
-    to_x = {"dp": d_far, "mp": m}
-    to_y = {"dp": d, "mp": m + 1 - 2 * b}
-    to_left = {"dp": d, "mp": (m + MPS - 2) % MPS}
-    to_right = {"dp": d, "mp": (m + 2) % MPS}
-
-    def by_core(j, row):
-        dd = (d_twin + 2) % DPS if j == 0 else d_twin
-        k = j * MPS + row
-        return remote(gb.at[slot(row, dd)], rc.at[k], s_core.at[k], r_core.at[k], to_core)
-
-    def by_x(row):
-        return remote(gb.at[slot(row, d_far)], rx.at[row], s_x.at[row], r_x.at[row], to_x)
-
-    def by_y(t):
-        return remote(gb.at[slot(2 * t + 1 - b, d)], ry.at[t], s_y.at[t], r_y.at[t], to_y)
-
-    def by_z(t, side, dev):
-        return remote(gb.at[slot(2 * t + b, d)], rz.at[t, side], s_z.at[t], r_z.at[t, side], dev)
-
-    def add(s, got):
-        gb[s] = (gb[s].astype(f32) + got[...].astype(f32)).astype(bf16)
-
-    def start_core():
-        for j in range(2):
-            lax.fori_loop(0, MPS, lambda row, _: (by_core(j, row).start(), 0)[1], 0)
-
-    def over_x(row, _):
-        by_core(0, row).wait_recv()
-        add(slot(row, d_far), rc.at[row])
-        by_x(row).start()
-        return 0
-
-    def keep(row, _):
-        by_core(1, row).wait_recv()
-        add(slot(row, d), rc.at[MPS + row])
-        return 0
-
-    def over_y(t, _):
-        row = 2 * t + 1 - b
-        by_x(row).wait_recv()
-        add(slot(row, d), rx.at[row])
-        by_y(t).start()
-        return 0
-
-    def own_y(t, _):
-        row = 2 * t + b
-        by_x(row).wait_recv()
-        add(slot(row, d), rx.at[row])
-        by_y(t).wait_recv()
-        add(slot(row, d), ry.at[t])
-        return 0
-
-    def along_z(t):
-        s = slot(2 * t + b, d)
+                pl.when(cond)(functools.partial(lambda way: self.copy(s, way).start(), way))
+
+    def settle(self, s, ways):
+        for way, cond in ways:
+            if cond is None:
+                self.copy(s, way).wait_send()
+            else:
+                pl.when(cond)(functools.partial(lambda way: self.copy(s, way).wait_send(), way))
+
+    def line(self, core, dd, j):
+        s, ways = self.ways_of_line(core, dd, j)
+        if j:
+            self.arrive(s)
+        elif core == 0:
+            pl.when(self.d != dd)(lambda: self.arrive(s))
+        self.start(s, ways)
+
+    def side(self, core, dd, j):
+        s, ways = self.ways_of_side(core, dd, j)
+        self.arrive(s)
+        self.start(s, ways)
+
+    def cross(self, j, same):
+        s, ways = self.ways_of_cross(j, same)
+        self.arrive(s)
+        self.start(s, ways)
+
+    def from_core(self, dd):
+        for row in range(MPS):
+            self.arrive(slot(row, dd))
+
+    def drain(self):
+        @pl.when(self.c == 0)
+        def _():
+            for dd in (0, 2):
+                for j in range(LINES):
+                    self.settle(*self.ways_of_line(0, dd, j))
+                    self.settle(*self.ways_of_side(0, dd, j))
+
+        @pl.when(self.c == 1)
+        def _():
+            for j in range(LINES):
+                self.settle(*self.ways_of_line(1, self.d, j))
+                self.settle(*self.ways_of_side(1, self.d, j))
+                self.settle(*self.ways_of_cross(j, True))
+                self.settle(*self.ways_of_cross(j, False))
+
+
+def in_turn(n):
+    return (3 * n) % LINES
+
+
+class BlocksIn:
+    def __init__(self, gb, rc, rx, ry, rz, total, spare, sems):
+        self.gb, self.rc, self.rx, self.ry, self.rz = gb, rc, rx, ry, rz
+        self.total, self.spare = total, spare
+        self.sems = sems
+        self.d, self.m, self.x, self.c, self.a, self.b = place()
+        d, m, b, c = self.d, self.m, self.b, self.c
+        self.far = (d + 2) % DPS
+        self.twin = d + 1 - 2 * c
+        self.to_core = {"dp": self.twin, "mp": m}
+        self.to_x = {"dp": self.far, "mp": m}
+        self.to_y = {"dp": d, "mp": m + 1 - 2 * b}
+        self.to_left = {"dp": d, "mp": (m + MPS - 2) % MPS}
+        self.to_right = {"dp": d, "mp": (m + 2) % MPS}
+
+    def move(self, s, dst, name, k, part, dev):
+        ss, rs = self.sems[name]
+        rows = pl.ds(*part[1:])
+        return remote(self.gb.at[s, rows], dst.at[rows], ss.at[k, part[0]], rs.at[k, part[0]], dev)
+
+    def by_core(self, row, dd, part):
+        k = dd // 2 * MPS + row
+        return self.move(slot(row, dd), self.rc.at[k], "core", k, part, self.to_core)
+
+    def by_x(self, k, s, part):
+        return self.move(s, self.rx.at[k], "x", k, part, self.to_x)
+
+    def by_y(self, k, t, dd, part):
+        return self.move(slot(2 * t + 1 - self.b, dd), self.ry.at[k * LINES + t], "y", k * LINES + t, part, self.to_y)
+
+    def by_z(self, k, t, dd, side, part, dev):
+        n = (k * LINES + t) * 2 + side
+        return self.move(slot(2 * t + self.b, dd), self.rz.at[n], "z", n, part, dev)
+
+    def add(self, s, part, *got):
+        rows = pl.ds(*part[1:])
+        value = self.gb[s, rows].astype(f32)
+        for ref in got:
+            value = value + ref[rows].astype(f32)
+        self.gb[s, rows] = value.astype(bf16)
+
+    def along_z(self, k, t, dd, part):
+        a = self.a
+        s = slot(2 * t + self.b, dd)
 
         @pl.when((t < a) & (a < LINES - 1))
         def _():
-            by_z(t, 1, to_left).wait_recv()
-            add(s, rz.at[t, 1])
+            self.by_z(k, t, dd, 1, part, self.to_left).wait_recv()
+            self.add(s, part, self.rz.at[(k * LINES + t) * 2 + 1])
 
         @pl.when((t > a) & (a > 0))
         def _():
-            by_z(t, 0, to_right).wait_recv()
-            add(s, rz.at[t, 0])
-
-        @pl.when(t < a)
-        def _():
-            by_z(t, 1, to_left).start()
-
-        @pl.when(t > a)
-        def _():
-            by_z(t, 0, to_right).start()
-
-    def finish():
-        for t in (0, LINES - 1, 1, LINES - 2):
-            along_z(t)
-        total[...] = gb[slot(m, d)].astype(f32)
+            self.by_z(k, t, dd, 0, part, self.to_right).wait_recv()
+            self.add(s, part, self.rz.at[(k * LINES + t) * 2])
+
+        pl.when(t < a)(lambda: self.by_z(k, t, dd, 1, part, self.to_left).start())
+        pl.when(t > a)(lambda: self.by_z(k, t, dd, 0, part, self.to_right).start())
+
+    def end_z(self, k, dd, part, to):
+        a = self.a
+        rows = pl.ds(*part[1:])
+        to[rows, :] = self.gb[slot(self.m, dd), rows].astype(f32)
 
         @pl.when(a < LINES - 1)
         def _():
-            by_z(a, 1, to_left).wait_recv()
-            total[...] += rz[a, 1].astype(f32)
+            self.by_z(k, a, dd, 1, part, self.to_left).wait_recv()
+            to[rows, :] += self.rz[(k * LINES + a) * 2 + 1, rows].astype(f32)
 
         @pl.when(a > 0)
         def _():
-            by_z(a, 0, to_right).wait_recv()
-            total[...] += rz[a, 0].astype(f32)
-
-    def drain():
-        for j in range(2):
-            lax.fori_loop(0, MPS, lambda row, _: (by_core(j, row).wait_send(), 0)[1], 0)
-        lax.fori_loop(0, MPS, lambda row, _: (by_x(row).wait_send(), 0)[1], 0)
-        lax.fori_loop(0, LINES, lambda t, _: (by_y(t).wait_send(), 0)[1], 0)
+            self.by_z(k, a, dd, 0, part, self.to_right).wait_recv()
+            to[rows, :] += self.rz[(k * LINES + a) * 2, rows].astype(f32)
+
+    def zero_over(self, dd, t, part):
+        row = 2 * t + 1 - self.b
+        self.by_core(row, dd, part).wait_recv()
+        self.add(slot(row, dd), part, self.rc.at[dd // 2 * MPS + row])
+        self.by_y(dd // 2, t, dd, part).start()
+
+    def zero_own(self, dd, t, part):
+        row = 2 * t + self.b
+        k = dd // 2
+        self.by_core(row, dd, part).wait_recv()
+        self.by_y(k, t, dd, part).wait_recv()
+        self.add(slot(row, dd), part, self.rc.at[k * MPS + row], self.ry.at[k * LINES + t])
+        self.along_z(k, t, dd, part)
+
+    def zero_end(self, dd, part):
+        k = dd // 2
+        s = slot(self.m, dd)
+        rows = pl.ds(*part[1:])
+        self.end_z(k, dd, part, self.spare)
+
+        @pl.when(self.d != dd)
+        def _():
+            self.gb[s, rows] = self.spare[rows, :].astype(bf16)
+            self.by_x(k, s, part).start()
+
+        @pl.when(self.d == dd)
+        def _():
+            self.by_x(k, s, part).wait_recv()
+            self.total[rows, :] = self.spare[rows, :] + self.rx[k, rows].astype(f32)
+
+    def one_end(self, part):
+        self.end_z(0, self.d, part, self.total)
+
+    def one_far(self, n, part):
+        t = in_turn(n)
+        row = 2 * t + self.b + (1 - 2 * self.b) * (1 - n // LINES)
+        dd = self.far
+        self.by_core(row, dd, part).wait_recv()
+        self.add(slot(row, dd), part, self.rc.at[dd // 2 * MPS + row])
+        self.by_x(row, slot(row, dd), part).start()
+
+    def one_over(self, t, part):
+        row = 2 * t + 1 - self.b
+        dd = self.d
+        self.by_core(row, dd, part).wait_recv()
+        self.by_x(row, slot(row, dd), part).wait_recv()
+        self.add(slot(row, dd), part, self.rc.at[dd // 2 * MPS + row], self.rx.at[row])
+        self.by_y(0, t, dd, part).start()
+
+    def one_own(self, t, part):
+        row = 2 * t + self.b
+        dd = self.d
+        self.by_core(row, dd, part).wait_recv()
+        self.by_x(row, slot(row, dd), part).wait_recv()
+        self.by_y(0, t, dd, part).wait_recv()
+        self.add(slot(row, dd), part, self.rc.at[dd // 2 * MPS + row], self.rx.at[row], self.ry.at[t])
+        self.along_z(0, t, dd, part)
+
+    def drain_tree(self, core, dd, part):
+        k = dd // 2 if core == 0 else 0
+        a = self.a
         for t in range(LINES):
-
-            @pl.when(t != a)
-            def _(t=t):
-                by_z(t, 0, to_right).wait_send()
-
-    start_core()
-    lax.fori_loop(0, MPS, over_x, 0)
-    lax.fori_loop(0, MPS, keep, 0)
-    lax.fori_loop(0, LINES, over_y, 0)
-    lax.fori_loop(0, LINES, own_y, 0)
-    finish()
-    drain()
+            self.by_y(k, t, dd, part).wait_send()
+            pl.when(t < a)(functools.partial(self.wait_z, k, t, dd, 1, part))
+            pl.when(t > a)(functools.partial(self.wait_z, k, t, dd, 0, part))
+        if core == 0:
+            pl.when(self.d != dd)(lambda: self.by_x(k, slot(self.m, dd), part).wait_send())
+        else:
+            for row in range(MPS):
+                self.by_x(row, slot(row, self.far), part).wait_send()
+
+    def wait_z(self, k, t, dd, side, part):
+        self.by_z(k, t, dd, side, part, self.to_left if side else self.to_right).wait_send()
+
+
+WHOLE = ((0, 0, QROWS),)
+PARTS = ((0, 0, QROWS // 2), (1, QROWS // 2, QROWS // 2))
 
 
 def smalls_in(gsm, got, part, got2, total, ssem, rsem, rsem2):
@@ -1133,32 +1168,31 @@
 
     for k in range(1, MPS):
         over_mp(k).start()
-    value = gsm[m]
-    for k in range(1, MPS):
-        over_mp(k).wait_recv()
-        value = value + got[k]
-    part[...] = value
-    for k in range(DPS - 1):
-
-        @pl.when(d == k)
-        def _(k=k):
-            over_dp(k).start()
-
-    @pl.when(d == DPS - 1)
-    def _():
-        total[...] = part[...]
+
+    def middle():
+        value = gsm[m]
+        for k in range(1, MPS):
+            over_mp(k).wait_recv()
+            value = value + got[k]
+        part[...] = value
         for k in range(DPS - 1):
-            over_dp(k).wait_recv()
-            total[...] += got2[k]
-
-    for k in range(DPS - 1):
-
-        @pl.when(d == k)
-        def _(k=k):
-            over_dp(k).wait_send()
-
-    for k in range(1, MPS):
-        over_mp(k).wait_send()
+            pl.when(d == k)(lambda k=k: over_dp(k).start())
+
+    def end():
+        @pl.when(d == DPS - 1)
+        def _():
+            total[...] = part[...]
+            for k in range(DPS - 1):
+                over_dp(k).wait_recv()
+                total[...] += got2[k]
+
+    def drain():
+        for k in range(DPS - 1):
+            pl.when(d == k)(lambda k=k: over_dp(k).wait_send())
+        for k in range(1, MPS):
+            over_mp(k).wait_send()
+
+    return middle, end, drain
 
 
 def flat_grads(total, smalls, fl, roll, head, head_sem, wide, tall, gflat):
@@ -1243,37 +1277,248 @@
         back.wait_send()
 
 
-def step_kernel(images, rows, block, length, *refs):
+def step_kernel(images, rows, length, *refs):
     (nlive, x, cot, pf, sel, mask) = refs[:6]
     (out, gin, gflat) = refs[6:9]
     (
         fl, roll, head, wide, tall, wb, sm, vecs, b1, tabs, tabs2, bias, gvec, gb1, acc, gb, gsm, got, part, got2,
-        stotal, rc, rx, ry, rz, total,
+        stotal, rc, rx, ry, rz, total, spare,
         head_sem, sm_s, sm_r, ag_s, ag_r, rsm_s, rsm_r, rsm_r2, s_core, r_core, s_x, r_x, s_y, r_y, s_z, r_z,
-    ) = refs[9:51]
-    sc = refs[51:]
+    ) = refs[9:52]
+    ln1, qkv, wq, probs, mixw, mixed, ln2, act, gpre, gresb, gres, gmix, gwin, goutb = refs[52:]
     greet()
     flatten_params(pf, fl, roll, head, head_sem, wide, wb, sm)
-    steps, drain = blocks_out(wb, ag_s, ag_r)
-    steps[0]()
+    outs = BlocksOut(wb, ag_s, ag_r)
+    c = outs.c
+    zero, one = c == 0, c == 1
+    pl.when(zero)(lambda: outs.line(0, 0, 0))
     finish_sm, drain_sm = smalls_out(sm, sm_s, sm_r)
-    for step in steps[1:]:
-        step()
+
+    @pl.when(zero)
+    def _():
+        outs.line(0, 0, 1)
+        outs.side(0, 0, 0)
+
     finish_sm()
     gather_smalls(sm, vecs, b1, tabs, bias, mask)
-    mega_compute(images, rows, block, length, nlive[0], x, cot, wb, vecs, b1, bias, sel, out, gin, gb, gvec, gb1, acc, sc)
+
+    @pl.when(zero)
+    def _():
+        outs.line(0, 0, 2)
+        outs.side(0, 0, 1)
+
+    first_norm(x, vecs, ln1)
+
+    @pl.when(zero)
+    def _():
+        outs.line(0, 0, 3)
+        outs.side(0, 0, 2)
+        outs.side(0, 0, 3)
+
+    @pl.when(one)
+    def _():
+        outs.from_core(0)
+        outs.line(1, outs.d, 0)
+
+    def two(fn, *args):
+        return functools.partial(fn, 0, 2, *args)
+
+    def mine(fn, *args):
+        return functools.partial(fn, 1, outs.d, *args)
+
+    def cross(j, same):
+        return functools.partial(outs.cross, j, same)
+
+    zero_at = {
+        1: [two(outs.line, 0)],
+        4: [two(outs.line, 1)],
+        5: [two(outs.side, 0)],
+        8: [two(outs.line, 2)],
+        9: [two(outs.side, 1)],
+        12: [two(outs.line, 3)],
+        13: [two(outs.side, 2)],
+        17: [two(outs.side, 3)],
+    }
+    one_at = {
+        4: [mine(outs.line, 1)],
+        5: [mine(outs.side, 0)],
+        6: [cross(0, True)],
+        8: [mine(outs.line, 2)],
+        9: [mine(outs.side, 1)],
+        10: [cross(1, True), cross(0, False)],
+        12: [mine(outs.line, 3), mine(outs.side, 2)],
+        14: [cross(2, True), cross(1, False)],
+        17: [mine(outs.side, 3)],
+        19: [cross(3, True), cross(2, False)],
+        21: [cross(3, False)],
+    }
+
+    def run(zeros, ones):
+        if zeros:
+            pl.when(zero)(lambda: [fn() for fn in zeros] and None)
+        if ones:
+            pl.when(one)(lambda: [fn() for fn in ones] and None)
+
+    def at_point(zero_table, one_table, point):
+        run(zero_table.get(point), one_table.get(point))
+
+    def poll_project(n):
+        at_point(zero_at, one_at, n)
+
+    def poll_forward(i, w):
+        for k in range(NW):
+            point = 6 + NW * i + k
+            if point in zero_at or point in one_at:
+                pl.when(w == k)(functools.partial(at_point, zero_at, one_at, point))
+
+    project_qkv(wb, vecs, ln1, qkv, poll_project)
+    attention_forward(images, length, sel, bias, qkv, wq, probs, mixw, mixed, poll_forward)
+
+    @pl.when(zero)
+    def _():
+        outs.from_core(1)
+        outs.from_core(3)
+
+    pl.when(one)(lambda: outs.from_core(2))
+
+    feed_forward(
+        rows, nlive[0], x, cot, wb, vecs, b1, out, gvec, gb1, mixed, ln2, act, gpre, gresb, gres, gmix, goutb
+    )
+    proj_grads(gb, mixed, gresb)
+    ins = BlocksIn(
+        gb, rc, rx, ry, rz, total, spare, {"core": (s_core, r_core), "x": (s_x, r_x), "y": (s_y, r_y), "z": (s_z, r_z)}
+    )
+    whole = WHOLE[0]
+
+    def hand_over(row):
+        @pl.when(zero)
+        def _():
+            for dd in (1, 3):
+                ins.by_core(row, dd, whole).start()
+
+        pl.when(one)(lambda: ins.by_core(row, 2, whole).start())
+
+    def grads(n, _):
+        t = in_turn(n)
+        row = 2 * t + ins.b + (1 - 2 * ins.b) * (1 - n // LINES)
+        feed_forward_grads(row, gb, act, goutb, ln2, gpre)
+        hand_over(row)
+
+        @pl.when((n >= 1) & one)
+        def _():
+            ins.one_far(n - 1, whole)
+
+        @pl.when((n >= 1) & (n <= LINES) & zero)
+        def _():
+            ins.zero_over(2, in_turn(n - 1), whole)
+
+        return 0
+
+    lax.fori_loop(0, MPS, grads, 0)
+
+    turn = [in_turn(n) for n in range(LINES)]
+    zero_at = {
+        3: [functools.partial(ins.zero_own, 2, turn[0], whole)],
+        5: [functools.partial(ins.zero_own, 2, turn[1], whole)],
+        7: [functools.partial(ins.zero_own, 2, turn[2], whole)],
+        9: [functools.partial(ins.zero_own, 2, turn[3], whole)],
+        13: [functools.partial(ins.zero_end, 2, whole)],
+    }
+    one_at = {
+        0: [functools.partial(ins.one_far, MPS - 1, whole)],
+        1: [functools.partial(ins.one_over, turn[0], whole)],
+        2: [functools.partial(ins.one_over, turn[1], whole)],
+        4: [functools.partial(ins.one_over, turn[2], whole)],
+        5: [functools.partial(ins.one_over, turn[3], whole)],
+        8: [functools.partial(ins.one_own, turn[0], whole)],
+        10: [functools.partial(ins.one_own, turn[1], whole)],
+        12: [functools.partial(ins.one_own, turn[2], whole)],
+        14: [functools.partial(ins.one_own, turn[3], whole)],
+    }
+
+    def poll_backward(i, w):
+        for k in range(NW):
+            point = NW * i + k
+            if point in zero_at or point in one_at:
+                pl.when(w == k)(functools.partial(at_point, zero_at, one_at, point))
+
+    attention_backward(images, length, sel, gmix, wq, probs, mixw, gwin, qkv, acc, gvec, poll_backward)
+
+    order = (0, 1, 3, 2)
+
+    def hand_first(rows_of):
+        @pl.when(one)
+        def _():
+            for row in rows_of:
+                for part in PARTS:
+                    ins.by_core(row, 0, part).start()
+
+    qkv_grads(0, gb, qkv, ln1)
+    hand_first(range(MPS // 2))
+    qkv_grads(1, gb, qkv, ln1)
+    hand_first(range(MPS // 2, MPS))
+    def both_parts(fn, t):
+        return [functools.partial(fn, 0, t, part) for part in PARTS]
+
+    zero_at = {
+        0: both_parts(ins.zero_over, order[0]),
+        1: both_parts(ins.zero_over, order[1]),
+        2: both_parts(ins.zero_over, order[2]),
+        3: both_parts(ins.zero_over, order[3]),
+        5: both_parts(ins.zero_own, order[0]),
+    }
+    one_at = {0: [functools.partial(ins.one_end, whole)]}
+    first_norm_back(x, wb, vecs, qkv, gres, gin, gvec, functools.partial(at_point, zero_at, one_at))
     scatter_smalls(gvec, gb1, acc, gsm, tabs2)
-    blocks_in(gb, rc, rx, ry, rz, total, s_core, r_core, s_x, r_x, s_y, r_y, s_z, r_z)
-    smalls_in(gsm, got, part, got2, stotal, rsm_s, rsm_r, rsm_r2)
+    mid_sm, end_sm, drain_in = smalls_in(gsm, got, part, got2, stotal, rsm_s, rsm_r, rsm_r2)
+
+    @pl.when(zero)
+    def _():
+        for fn in both_parts(ins.zero_own, order[1]):
+            fn()
+
+    mid_sm()
+
+    @pl.when(zero)
+    def _():
+        for t in order[2:]:
+            for fn in both_parts(ins.zero_own, t):
+                fn()
+
+    end_sm()
+
+    @pl.when(zero)
+    def _():
+        for part in PARTS:
+            ins.zero_end(0, part)
+
     flat_grads(total, stotal, fl, roll, head, head_sem, wide, tall, gflat)
-    drain()
+
+    @pl.when(zero)
+    def _():
+        for row in range(MPS):
+            for dd in (1, 3):
+                ins.by_core(row, dd, whole).wait_send()
+        ins.drain_tree(0, 2, whole)
+        for part in PARTS:
+            ins.drain_tree(0, 0, part)
+
+    @pl.when(one)
+    def _():
+        for row in range(MPS):
+            ins.by_core(row, 2, whole).wait_send()
+            for part in PARTS:
+                ins.by_core(row, 0, part).wait_send()
+        ins.drain_tree(1, ins.d, whole)
+
+    drain_in()
+    outs.drain()
     drain_sm()
 
 
 def step_call(x, cot, nlive, pf):
     rows = x.shape[0]
     images = rows // PIX
-    block = block_size(rows)
     length = image_frames(images)[2]
     sel = jnp.asarray(placement(images), bf16)
     mask = jnp.asarray(score_masks(), f32)
@@ -1283,7 +1528,7 @@
     dma = pltpu.SemaphoreType.DMA
     nb = MPS * DPS
     return pl.pallas_call(
-        functools.partial(step_kernel, images, rows, block, length),
+        functools.partial(step_kernel, images, rows, length),
         out_shape=(s((rows, C), bf16), s((rows, C), bf16), s((FLAT, 128), f32)),
         in_specs=[smem] + [vmem] * 5,
         out_specs=(vmem,) * 3,
@@ -1311,8 +1556,9 @@
             pltpu.VMEM((16, 128), f32),
             pltpu.VMEM((2 * MPS, QROWS, 256), bf16),
             pltpu.VMEM((MPS, QROWS, 256), bf16),
-            pltpu.VMEM((LINES, QROWS, 256), bf16),
-            pltpu.VMEM((LINES, 2, QROWS, 256), bf16),
+            pltpu.VMEM((2 * LINES, QROWS, 256), bf16),
+            pltpu.VMEM((4 * LINES, QROWS, 256), bf16),
+            pltpu.VMEM((QROWS, 256), f32),
             pltpu.VMEM((QROWS, 256), f32),
             dma((4,)),
             dma((3 + MPS,)),
@@ -1322,14 +1568,14 @@
             dma((MPS,)),
             dma((MPS,)),
             dma((DPS,)),
-            dma((2 * MPS,)),
-            dma((2 * MPS,)),
-            dma((MPS,)),
-            dma((MPS,)),
-            dma((LINES,)),
-            dma((LINES,)),
-            dma((LINES,)),
-            dma((LINES, 2)),
+            dma((2 * MPS, 2)),
+            dma((2 * MPS, 2)),
+            dma((MPS, 2)),
+            dma((MPS, 2)),
+            dma((2 * LINES, 2)),
+            dma((2 * LINES, 2)),
+            dma((4 * LINES, 2)),
+            dma((4 * LINES, 2)),
         ]
         + mega_scratch(images, rows),
         compiler_params=pltpu.CompilerParams(

time: 226 us -> 180 us (0.80)
  the two profiles are of different devices: /device:TPU:0 before, /device:TPU:25 now
where the time goes in v3:
time: 180 us
  Pallas kernels  168 us (93%)
  other arithmetic  5.39 us (3%)
  local copies, waits for them, and re-layouts  4.99 us (3%)
    pallas_call x1, Pallas kernels, step_call(): pl.pallas_call(functools.partial(step_kernel, images, rows, length), out_...  168 us
    sub x1, other arithmetic, finish(): params - learn_rate * (corrected_one / (jnp.sqrt(corrected_two) + adam_ep...  4.75 us

profile of v3, /device:TPU:25, one launch (start us, length us, event | category | flops | bytes accessed | tf_op | source)
XLA Modules:
  0.0 180.0 jit_solution(13011141572050540856)
XLA Ops:
  0.6 0.0 copy-start.5
  0.6 0.6 copy-done.5
  1.3 0.6 fusion.3
  2.6 2.0 %pad.4 = f32[1,99328]{1,0:T(1,128)} pad(f32[1,98581]{1,0:T(1,128)} %param.11, f32[]{:T(128)} %constant.14.clone.1), padding=0_0x0_747 | pad | bytes 791640 | tf_op jit(solution)/shard_map/jit(_pad)/pad | solution.py:1709
  4.6 0.0 copy-start
  4.6 0.0 copy-start.3
  4.6 0.0 copy-start.4
  4.6 168.3 %shard_map.127 = (bf16[784,512]{1,0:T(8,128)(2,1)}, bf16[784,512]{1,0:T(8,128)(2,1)}, f32[776,128]{1,0:T(8,128)}) custom-call(s32[1]{0:T(128)} %bitcast.refs_0_, bf16[784,512]{1,0:T(8,128)(2,1)} %refs_1_.1, bf16[784,512]{1,0:T(8,128)(2,1)} %refs_2_.1, f32[776,128]{1,0:T(8,128)} %bitcast.3, bf16[4,256,208]{2,1,0:T(8,128)(2,1)} %constant.43.clone.refs_4_, ...), custom_call_target="tpu_custom_call" | custom-call | tf_op jit(solution)/shard_map/pallas_call | solution.py:1530
  172.9 0.0 copy-done
  172.9 0.0 copy-done.3
  172.9 0.0 copy-done.4
  172.9 0.0 copy-start.2
  172.9 4.8 %multiply_subtract_fusion = (f32[1,98581]{1,0:T(1,128)}, f32[1,98581]{1,0:T(1,128)}, f32[1,98581]{1,0:T(1,128)}, f32[1,98581]{1,0:T(1,128)}) fusion(f32[1,98581]{1,0:T(1,128)S(1)} %copy-done, s32[]{:T(128)S(6)} %mul.56, f32[1,98581]{1,0:T(1,128)S(1)} %copy-done.3, f32[1,98581]{1,0:T(1,128)S(1)} %copy-done.4, f32[1,99328]{1,0:T(1,128)} %bitcast.4), kind=kLoop, calls=%fused_computation.5 | loop fusion | flops 1774458 | bytes 3154596 | tf_op jit(solution)/shard_map/sub | solution.py:1638
  177.7 0.0 copy-done.2
  177.7 0.0 copy-start.1
  177.7 0.9 copy.16
  178.6 0.5 copy-done.1
  179.1 0.9 copy.17
Async XLA Ops:
  0.6 0.7 copy-start.5
  4.6 168.3 %copy-start = (f32[1,98581]{1,0:T(1,128)S(1)}, f32[1,98581]{1,0:T(1,128)}, u32[]{:S(2)}) copy-start(f32[1,98581]{1,0:T(1,128)} %param.11) | copy-start | bytes 1182976
  4.6 168.3 %copy-start.3 = (f32[1,98581]{1,0:T(1,128)S(1)}, f32[1,98581]{1,0:T(1,128)}, u32[]{:S(2)}) copy-start(f32[1,98581]{1,0:T(1,128)} %param.12) | copy-start | bytes 1182976
  4.6 168.3 %copy-start.4 = (f32[1,98581]{1,0:T(1,128)S(1)}, f32[1,98581]{1,0:T(1,128)}, u32[]{:S(2)}) copy-start(f32[1,98581]{1,0:T(1,128)} %param.13) | copy-start | bytes 1182976
  172.9 4.8 %copy-start.2 = (bf16[784,512]{1,0:T(8,128)(2,1)S(1)}, bf16[784,512]{1,0:T(8,128)(2,1)}, u32[]{:S(2)}) copy-start(bf16[784,512]{1,0:T(8,128)(2,1)} %get-tuple-element.22) | copy-start | bytes 2408452
  177.7 1.4 copy-start.1

commit v4 on v3

--- a/solution.py
+++ b/solution.py
@@ -463,6 +463,19 @@
             bias[w * NG + g] = bt + mask[w]
 
 
+def row_half(gvec, i, r):
+    g, k = divmod(r, 2)
+    v = gvec[i : i + 1, g * 128 : (g + 1) * 128]
+    turned = pltpu.roll(v, 64, 1)
+    return (v, turned) if k == 0 else (turned, v)
+
+
+def scatter_first(gvec, gsm):
+    low = iota((1, 128), 1) < 64
+    for r in range(MPS):
+        gsm[r, 0:1, :] = jnp.where(low, row_half(gvec, 0, r)[0], row_half(gvec, 1, r)[1])
+
+
 def scatter_smalls(gvec, gb1, acc, gsm, tabs):
     lane = iota((1, 128), 1)
     low = lane < 64
@@ -481,19 +494,13 @@
             tabs[r : r + 1, i * 256 : (i + 1) * 256] = jnp.sum(total, axis=0, keepdims=True)
     flat = split_mm_left(mm_t, tabs[...], table_lanes())
 
-    def half(i, r):
-        g, k = divmod(r, 2)
-        v = gvec[i : i + 1, g * 128 : (g + 1) * 128]
-        turned = pltpu.roll(v, 64, 1)
-        return (v, turned) if k == 0 else (turned, v)
-
+    half = functools.partial(row_half, gvec)
     zero = jnp.zeros((1, 128), f32)
     for r in range(MPS):
         fb0 = gb1[:, r * 256 : r * 256 + 128]
         fb1 = gb1[:, r * 256 + 128 : r * 256 + 256]
         t0, t1 = pltpu.roll(fb0, 64, 1), pltpu.roll(fb1, 64, 1)
         rows = [
-            jnp.where(low, half(0, r)[0], half(1, r)[1]),
             jnp.where(low, half(2, r)[0], half(3, r)[1]),
             jnp.where(low, half(4, r)[0], half(5, r)[1]),
             jnp.where(low, half(6, r)[0], t0),
@@ -501,7 +508,7 @@
             jnp.where(low, t1, half(7, r)[1]),
         ]
         for j, row in enumerate(rows):
-            gsm[r, j : j + 1, :] = row
+            gsm[r, 1 + j : 2 + j, :] = row
         for j in range(3):
             gsm[r, 6 + j : 7 + j, :] = flat[r : r + 1, j * 128 : (j + 1) * 128]
         for j in range(9, 16):
@@ -545,45 +552,91 @@
     ln1[...] = ((xin - center) * scale * vecs[0:1, :] + vecs[1:2, :]).astype(bf16)
 
 
-def project_qkv(wb, vecs, ln1, qkv, poll):
+def group_lanes(g):
+    return pl.ds(pl.multiple_of(g * 128, 128), 128)
+
+
+def group_qkv(wb, g, half):
+    return jnp.concatenate(
+        [
+            wb[slot(2 * g + r, 0), half * 192 + kind * 64 : half * 192 + kind * 64 + 64, :]
+            for kind in range(3)
+            for r in range(2)
+        ],
+        axis=0,
+    )
+
+
+def project_group(g, wb, vecs, ln1, qkv):
+    val = mm_t(ln1[:, HALVES[0]], group_qkv(wb, g, 0)) + mm_t(ln1[:, HALVES[1]], group_qkv(wb, g, 1))
+    gl = group_lanes(g)
+    qkv[:, 0:128] = ((val[:, 0:128] + vecs[2:3, gl]) * HD ** (-0.5)).astype(bf16)
+    qkv[:, 128:256] = val[:, 128:256].astype(bf16)
+    qkv[:, 256:384] = (val[:, 256:384] + vecs[3:4, gl]).astype(bf16)
+
+
+def frame_rows(i, length):
+    return pl.ds(pl.multiple_of(PIX * i // 16 * 16, 16), length)
+
+
+def attend(i, g, length, sel, bias, qkv, wq, probs, mixed):
+    head_of_lane = lane_head_mask()
+    fr = frame_rows(i, length)
+    wq[g, i] = mm(sel[i], qkv[fr, :]).astype(bf16)
+    outs = []
+    for w in range(NW):
+        ws = slice(w * SEG, (w + 1) * SEG)
+        q, k, v = (wq[g, i, ws, n * 128 : (n + 1) * 128] for n in range(3))
+        st = mm_t(k, block_diag(q, head_of_lane)) + bias[w * NG + g]
+        e = jnp.exp(st - jnp.max(st, axis=0, keepdims=True))
+        pt = (e * (1.0 / jnp.sum(e, axis=0, keepdims=True))).astype(bf16)
+        probs[g, i, w] = pt
+        outs.append(diag_pick(mm_r(pt, v), head_of_lane).astype(bf16))
+    gl = group_lanes(g)
+    back = mm_r(sel[i], jnp.concatenate(outs, axis=0))
+    mixed[fr, gl] = (mixed[fr, gl].astype(f32) + back).astype(bf16)
+
+
+def attend_back(i, g, length, sel, gmix, wq, probs, gqkv, acc, gvec):
+    head_of_lane = lane_head_mask()
+    fr = frame_rows(i, length)
+    gl = group_lanes(g)
+    gwin = mm(sel[i], gmix[fr, gl]).astype(bf16)
+    outs = []
+    for w in range(NW):
+        ws = slice(w * SEG, (w + 1) * SEG)
+        q, k, v = (wq[g, i, ws, n * 128 : (n + 1) * 128] for n in range(3))
+        pt = probs[g, i, w]
+        dod = block_diag(gwin[ws, :], head_of_lane)
+        gv = mm(pt, dod)
+        dpt = mm_t(v, dod)
+        ptf = pt.astype(f32)
+        prod = ptf * dpt
+        dst = prod - ptf * jnp.sum(prod, axis=0, keepdims=True)
+        acc[g] += dst
+        dsb = dst.astype(bf16)
+        gk = mm(dsb, block_diag(q, head_of_lane))
+        gq = diag_pick(mm_r(dsb, k), head_of_lane) * HD ** (-0.5)
+        gvec[2:3, gl] += jnp.sum(gq, axis=0, keepdims=True)
+        gvec[3:4, gl] += jnp.sum(gv, axis=0, keepdims=True)
+        outs.append(jnp.concatenate([gq.astype(bf16), gk.astype(bf16), gv.astype(bf16)], axis=1))
+    back = mm_r(sel[i], jnp.concatenate(outs, axis=0))
+    gqkv[fr, :] = (gqkv[fr, :].astype(f32) + back).astype(bf16)
+
+
+def group_grads(g, gb, gqkv, ln1):
+    part = mm_r(gqkv[...], ln1[...]).astype(bf16)
     for kind in range(3):
-        for quad in range(2):
-            poll(2 * kind + quad)
-            qs = HALVES[quad]
-            val = mm_t(ln1[:, HALVES[0]], w_qkv(wb, kind, quad, 0)) + mm_t(
-                ln1[:, HALVES[1]], w_qkv(wb, kind, quad, 1)
-            )
-            if kind == 0:
-                val = (val + vecs[2:3, qs]) * HD ** (-0.5)
-            if kind == 2:
-                val = val + vecs[3:4, qs]
-            qkv[:, kind * C + quad * 256 : kind * C + quad * 256 + 256] = val.astype(bf16)
-
-
-def attention_forward(images, length, sel, bias, qkv, wq, probs, mixw, mixed, poll):
-    head_of_lane = lane_head_mask()
-    frame = image_frames(images)[0]
-    mixed[...] = jnp.zeros_like(mixed)
-    for i in range(images):
-        fr = pl.ds(frame[i], length)
-        wq[i] = mm(sel[i], qkv[fr, :]).astype(bf16)
-
-        def window(w, _):
-            poll(i, w)
-            ws = pl.ds(pl.multiple_of(w * SEG, SEG), SEG)
-            for g in range(NG):
-                q = wq[i, ws, g * 128 : (g + 1) * 128]
-                k = wq[i, ws, C + g * 128 : C + (g + 1) * 128]
-                v = wq[i, ws, 2 * C + g * 128 : 2 * C + (g + 1) * 128]
-                st = mm_t(k, block_diag(q, head_of_lane)) + bias[w * NG + g]
-                e = jnp.exp(st - jnp.max(st, axis=0, keepdims=True))
-                pt = (e * (1.0 / jnp.sum(e, axis=0, keepdims=True))).astype(bf16)
-                probs[i, w * NG + g] = pt
-                mixw[ws, g * 128 : (g + 1) * 128] = diag_pick(mm_r(pt, v), head_of_lane).astype(bf16)
-            return 0
-
-        lax.fori_loop(0, NW, window, 0)
-        mixed[fr, :] = (mixed[fr, :].astype(f32) + mm_r(sel[i], mixw[...])).astype(bf16)
+        for r in range(2):
+            at = kind * 128 + r * 64
+            for h in range(2):
+                to = h * 192 + kind * 64
+                gb[slot(2 * g + r, 0), to : to + 64, :] = part[at : at + 64, HALVES[h]]
+
+
+def group_norm_grad(g, wb, gqkv, gl1):
+    for h in range(2):
+        gl1[:, HALVES[h]] += mm(gqkv[...], group_qkv(wb, g, h))
 
 
 def feed_forward(rows, live_rows, x, cot, wb, vecs, b1, out, gvec, gb1, mixed, ln2, act, gpre, gresb, gres, gmix, goutb):
@@ -648,81 +701,28 @@
     gb[slot(r, 2), 0:256, :] = one[256:512]
 
 
-def attention_backward(images, length, sel, gmix, wq, probs, mixw, gwin, qkv, acc, gvec, poll):
-    head_of_lane = lane_head_mask()
-    frame = image_frames(images)[0]
-    qkv[...] = jnp.zeros_like(qkv)
-    acc[...] = jnp.zeros_like(acc)
-    gvec[2:4, :] = jnp.zeros((2, C), f32)
-    for i in range(images):
-        fr = pl.ds(frame[i], length)
-        mixw[...] = mm(sel[i], gmix[fr, :]).astype(bf16)
-
-        def window(w, _):
-            poll(i, w)
-            ws = pl.ds(pl.multiple_of(w * SEG, SEG), SEG)
-            for g in range(NG):
-                q = wq[i, ws, g * 128 : (g + 1) * 128]
-                k = wq[i, ws, C + g * 128 : C + (g + 1) * 128]
-                v = wq[i, ws, 2 * C + g * 128 : 2 * C + (g + 1) * 128]
-                pt = probs[i, w * NG + g]
-                dod = block_diag(mixw[ws, g * 128 : (g + 1) * 128], head_of_lane)
-                gv = mm(pt, dod)
-                dpt = mm_t(v, dod)
-                ptf = pt.astype(f32)
-                prod = ptf * dpt
-                dst = prod - ptf * jnp.sum(prod, axis=0, keepdims=True)
-                acc[g] += dst
-                dsb = dst.astype(bf16)
-                gk = mm(dsb, block_diag(q, head_of_lane))
-                gq = diag_pick(mm_r(dsb, k), head_of_lane) * HD ** (-0.5)
-                gl = slice(g * 128, (g + 1) * 128)
-                gvec[2:3, gl] += jnp.sum(gq, axis=0, keepdims=True)
-                gvec[3:4, gl] += jnp.sum(gv, axis=0, keepdims=True)
-                gwin[ws, g * 128 : (g + 1) * 128] = gq.astype(bf16)
-                gwin[ws, C + g * 128 : C + (g + 1) * 128] = gk.astype(bf16)
-                gwin[ws, 2 * C + g * 128 : 2 * C + (g + 1) * 128] = gv.astype(bf16)
-            return 0
-
-        lax.fori_loop(0, NW, window, 0)
-        qkv[fr, :] = (qkv[fr, :].astype(f32) + mm_r(sel[i], gwin[...])).astype(bf16)
-
-
-def qkv_grads(quad, gb, qkv, ln1):
-    for kind in range(3):
-        cols = slice(kind * C + quad * 256, kind * C + quad * 256 + 256)
-        part = mm_r(qkv[:, cols], ln1[...]).astype(bf16)
-        for r in range(4):
-            for h in range(2):
-                gb[slot(4 * quad + r, 0), h * 192 + kind * 64 : h * 192 + kind * 64 + 64, :] = part[
-                    r * 64 : r * 64 + 64, HALVES[h]
-                ]
-
-
-def first_norm_back(x, wb, vecs, qkv, gres, gin, gvec, poll):
-    rows = x.shape[0]
-    gln = [jnp.zeros((rows, 256), f32)] * 2
-    for kind in range(3):
-        for quad in range(2):
-            poll(2 * kind + quad)
-            part = qkv[:, kind * C + quad * 256 : kind * C + quad * 256 + 256]
-            gln = [gln[h] + mm(part, w_qkv(wb, kind, quad, h)) for h in range(2)]
-    gln = jnp.concatenate(gln, axis=1)
+def first_norm_sums(x, gl1, gvec):
     xin = x[...].astype(f32)
     center, scale = norm_stats(xin)
     unit = (xin - center) * scale
+    gln = gl1[...]
     gvec[0:1, :] = jnp.sum(gln * unit, axis=0, keepdims=True)
     gvec[1:2, :] = jnp.sum(gln, axis=0, keepdims=True)
-    gin[...] = (gres[...] + norm_back(gln * vecs[0:1, :], unit, scale)).astype(bf16)
+
+
+def first_norm_back(x, vecs, gl1, gres, gin):
+    xin = x[...].astype(f32)
+    center, scale = norm_stats(xin)
+    unit = (xin - center) * scale
+    gin[...] = (gres[...] + norm_back(gl1[...] * vecs[0:1, :], unit, scale)).astype(bf16)
 
 
 def mega_scratch(images, rows):
     return [
         pltpu.VMEM((rows, C), bf16),
-        pltpu.VMEM((rows, 3 * C), bf16),
-        pltpu.VMEM((images, NW * SEG, 3 * C), bf16),
-        pltpu.VMEM((images, NW * NG, SEG, GH * SEG), bf16),
-        pltpu.VMEM((NW * SEG, C), bf16),
+        pltpu.VMEM((rows, 384), bf16),
+        pltpu.VMEM((NG, images, NW * SEG, 384), bf16),
+        pltpu.VMEM((NG, images, NW, SEG, GH * SEG), bf16),
         pltpu.VMEM((rows, C), bf16),
         pltpu.VMEM((rows, C), bf16),
         pltpu.VMEM((rows, FF), bf16),
@@ -730,7 +730,7 @@
         pltpu.VMEM((rows, C), bf16),
         pltpu.VMEM((rows, C), f32),
         pltpu.VMEM((rows, C), bf16),
-        pltpu.VMEM((NW * SEG, 3 * C), bf16),
+        pltpu.VMEM((rows, C), f32),
         pltpu.VMEM((rows, C), bf16),
     ]
 
@@ -750,13 +750,7 @@
 
 
 def twin(a, j):
-    if j == 0:
-        return a
-    if j == 1:
-        return a + 1 - 2 * (a % 2)
-    if j == 2:
-        return (a + 2) % LINES
-    return LINES - 1 - a
+    return 2 * ((a // 2 + j // 2) % 2) + (a + j) % 2
 
 
 def remote(src, dst, send, recv, dev):
@@ -774,10 +768,12 @@
 
 def greet():
     barrier = pltpu.get_barrier_semaphore()
-    group = peers()
-    for dev in group:
+    for dev in peers():
         pl.semaphore_signal(barrier, inc=1, device_id=dev, device_id_type=MESH)
-    pl.semaphore_wait(barrier, len(group))
+
+
+def greeted():
+    pl.semaphore_wait(pltpu.get_barrier_semaphore(), DPS - 1 + MPS - 1)
 
 
 OFFSET = 277
@@ -801,6 +797,7 @@
                     lane >= lanes, roll[8 : 8 + FLAT, :], roll[7 : 7 + FLAT, :]
                 )
 
+    greeted()
     over = remote(fl.at[768:784], head.at[0], head_sem.at[0], head_sem.at[1], {"dp": (d + 1) % DPS, "mp": m})
 
     @pl.when(d < DPS - 1)
@@ -904,7 +901,7 @@
     return finish, drain
 
 
-RIGHT, LEFT, SIDE_Y, SIDE_X, CORE = range(5)
+SIDE_Z, SIDE_Y, SIDE_X, CORE = 0, 3, 4, 5
 
 
 class BlocksOut:
@@ -914,12 +911,12 @@
         d, m, b, c = self.d, self.m, self.b, self.c
         self.far = (d + 2) % DPS
         self.dev = {
-            RIGHT: {"dp": d, "mp": (m + 2) % MPS},
-            LEFT: {"dp": d, "mp": (m + MPS - 2) % MPS},
             SIDE_Y: {"dp": d, "mp": m + 1 - 2 * b},
             SIDE_X: {"dp": self.far, "mp": m},
             CORE: {"dp": d + 1 - 2 * c, "mp": m},
         }
+        for j in range(1, LINES):
+            self.dev[SIDE_Z + j - 1] = {"dp": d, "mp": 2 * twin(self.a, j) + b}
 
     def copy(self, s, way):
         return remote(self.wb.at[s], self.wb.at[s], self.ssem.at[s, way], self.rsem.at[s], self.dev[way])
@@ -927,81 +924,84 @@
     def arrive(self, s):
         self.copy(s, CORE).wait_recv()
 
-    def ways_of_line(self, core, dd, j):
-        a = self.a
-        t = twin(a, j)
-        if j == 0:
-            ways = [(RIGHT, a < LINES - 1), (LEFT, a > 0)]
-        else:
-            ways = [(RIGHT, (t < a) & (a < LINES - 1)), (LEFT, (t > a) & (a > 0))]
-        if core:
-            ways.append((SIDE_X, None))
-        elif j == 0:
-            ways.insert(0, (SIDE_X, self.d == dd))
-        return slot(2 * t + self.b, dd), ways + [(SIDE_Y, None), (CORE, None)]
-
-    def ways_of_side(self, core, dd, j):
-        ways = [(SIDE_X, None)] if core else []
-        return slot(2 * twin(self.a, j) + 1 - self.b, dd), ways + [(CORE, None)]
-
-    def ways_of_cross(self, j, same):
-        return slot(2 * twin(self.a, j) + (self.b if same else 1 - self.b), self.far), [(CORE, None)]
+    def row(self, j, same):
+        return 2 * twin(self.a, j) + (self.b if same else 1 - self.b)
+
+    def own_ways(self, core):
+        return [SIDE_Z, SIDE_Z + 1, SIDE_Z + 2, SIDE_Y] + ([SIDE_X] if core else []) + [CORE]
 
     def start(self, s, ways):
-        for way, cond in ways:
-            if cond is None:
-                self.copy(s, way).start()
-            else:
-                pl.when(cond)(functools.partial(lambda way: self.copy(s, way).start(), way))
+        for way in ways:
+            self.copy(s, way).start()
 
     def settle(self, s, ways):
-        for way, cond in ways:
-            if cond is None:
-                self.copy(s, way).wait_send()
-            else:
-                pl.when(cond)(functools.partial(lambda way: self.copy(s, way).wait_send(), way))
+        for way in ways:
+            self.copy(s, way).wait_send()
+
+    def origin_out(self, dd):
+        @pl.when(self.d == dd)
+        def _():
+            self.start(slot(self.m, dd), [SIDE_X] + self.own_ways(0))
+
+    def origin_in(self, dd):
+        @pl.when(self.d != dd)
+        def _():
+            s = slot(self.m, dd)
+            self.arrive(s)
+            self.start(s, self.own_ways(0))
+
+    def own(self):
+        self.start(slot(self.m, self.d), self.own_ways(1))
+
+    def line_ways(self, core):
+        return [SIDE_Y] + ([SIDE_X] if core else []) + [CORE]
+
+    def side_ways(self, core):
+        return ([SIDE_X] if core else []) + [CORE]
 
     def line(self, core, dd, j):
-        s, ways = self.ways_of_line(core, dd, j)
-        if j:
-            self.arrive(s)
-        elif core == 0:
-            pl.when(self.d != dd)(lambda: self.arrive(s))
-        self.start(s, ways)
+        s = slot(self.row(j, True), dd)
+        self.arrive(s)
+        self.start(s, self.line_ways(core))
 
     def side(self, core, dd, j):
-        s, ways = self.ways_of_side(core, dd, j)
+        s = slot(self.row(j, False), dd)
         self.arrive(s)
-        self.start(s, ways)
+        self.start(s, self.side_ways(core))
 
     def cross(self, j, same):
-        s, ways = self.ways_of_cross(j, same)
+        s = slot(self.row(j, same), self.far)
         self.arrive(s)
-        self.start(s, ways)
+        self.start(s, [CORE])
 
     def from_core(self, dd):
         for row in range(MPS):
             self.arrive(slot(row, dd))
+
+    def group_from_core(self, dd, j):
+        self.arrive(slot(self.row(j, True), dd))
+        self.arrive(slot(self.row(j, False), dd))
 
     def drain(self):
         @pl.when(self.c == 0)
         def _():
             for dd in (0, 2):
+                pl.when(self.d == dd)(lambda: self.copy(slot(self.m, dd), SIDE_X).wait_send())
+                self.settle(slot(self.m, dd), self.own_ways(0))
                 for j in range(LINES):
-                    self.settle(*self.ways_of_line(0, dd, j))
-                    self.settle(*self.ways_of_side(0, dd, j))
+                    if j:
+                        self.settle(slot(self.row(j, True), dd), self.line_ways(0))
+                    self.settle(slot(self.row(j, False), dd), self.side_ways(0))
 
         @pl.when(self.c == 1)
         def _():
+            self.settle(slot(self.m, self.d), self.own_ways(1))
             for j in range(LINES):
-                self.settle(*self.ways_of_line(1, self.d, j))
-                self.settle(*self.ways_of_side(1, self.d, j))
-                self.settle(*self.ways_of_cross(j, True))
-                self.settle(*self.ways_of_cross(j, False))
-
-
-def in_turn(n):
-    return (3 * n) % LINES
+                if j:
+                    self.settle(slot(self.row(j, True), self.d), self.line_ways(1))
+                self.settle(slot(self.row(j, False), self.d), self.side_ways(1))
+                for same in (True, False):
+                    self.settle(slot(self.row(j, same), self.far), [CORE])
 
 
 class BlocksIn:
@@ -1016,8 +1016,6 @@
         self.to_core = {"dp": self.twin, "mp": m}
         self.to_x = {"dp": self.far, "mp": m}
         self.to_y = {"dp": d, "mp": m + 1 - 2 * b}
-        self.to_left = {"dp": d, "mp": (m + MPS - 2) % MPS}
-        self.to_right = {"dp": d, "mp": (m + 2) % MPS}
 
     def move(self, s, dst, name, k, part, dev):
         ss, rs = self.sems[name]
@@ -1034,9 +1032,22 @@
     def by_y(self, k, t, dd, part):
         return self.move(slot(2 * t + 1 - self.b, dd), self.ry.at[k * LINES + t], "y", k * LINES + t, part, self.to_y)
 
-    def by_z(self, k, t, dd, side, part, dev):
-        n = (k * LINES + t) * 2 + side
-        return self.move(slot(2 * t + self.b, dd), self.rz.at[n], "z", n, part, dev)
+    def by_z(self, k, t, dd, part):
+        ss, rs = self.sems["z"]
+        rows = pl.ds(*part[1:])
+        n = k * LINES + self.a
+        return remote(
+            self.gb.at[slot(2 * t + self.b, dd), rows],
+            self.rz.at[n].at[rows],
+            ss.at[k * LINES + t, part[0]],
+            rs.at[n, part[0]],
+            {"dp": self.d, "mp": 2 * t + self.b},
+        )
+
+    def from_z(self, k, t, part):
+        _, rs = self.sems["z"]
+        ref = self.rz.at[k * LINES + t].at[pl.ds(*part[1:])]
+        remote(ref, ref, rs.at[k * LINES + t, part[0]], rs.at[k * LINES + t, part[0]], self.to_y).wait_recv()
 
     def add(self, s, part, *got):
         rows = pl.ds(*part[1:])
@@ -1046,36 +1057,18 @@
         self.gb[s, rows] = value.astype(bf16)
 
     def along_z(self, k, t, dd, part):
-        a = self.a
-        s = slot(2 * t + self.b, dd)
-
-        @pl.when((t < a) & (a < LINES - 1))
-        def _():
-            self.by_z(k, t, dd, 1, part, self.to_left).wait_recv()
-            self.add(s, part, self.rz.at[(k * LINES + t) * 2 + 1])
-
-        @pl.when((t > a) & (a > 0))
-        def _():
-            self.by_z(k, t, dd, 0, part, self.to_right).wait_recv()
-            self.add(s, part, self.rz.at[(k * LINES + t) * 2])
-
-        pl.when(t < a)(lambda: self.by_z(k, t, dd, 1, part, self.to_left).start())
-        pl.when(t > a)(lambda: self.by_z(k, t, dd, 0, part, self.to_right).start())
+        pl.when(t != self.a)(lambda: self.by_z(k, t, dd, part).start())
+
+    def line_here(self, k):
+        for j in range(1, LINES):
+            self.from_z(k, twin(self.a, j), WHOLE[0])
 
     def end_z(self, k, dd, part, to):
-        a = self.a
         rows = pl.ds(*part[1:])
-        to[rows, :] = self.gb[slot(self.m, dd), rows].astype(f32)
-
-        @pl.when(a < LINES - 1)
-        def _():
-            self.by_z(k, a, dd, 1, part, self.to_left).wait_recv()
-            to[rows, :] += self.rz[(k * LINES + a) * 2 + 1, rows].astype(f32)
-
-        @pl.when(a > 0)
-        def _():
-            self.by_z(k, a, dd, 0, part, self.to_right).wait_recv()
-            to[rows, :] += self.rz[(k * LINES + a) * 2, rows].astype(f32)
+        value = self.gb[slot(self.m, dd), rows].astype(f32)
+        for j in range(1, LINES):
+            value = value + self.rz[k * LINES + twin(self.a, j), rows].astype(f32)
+        to[rows, :] = value
 
     def zero_over(self, dd, t, part):
         row = 2 * t + 1 - self.b
@@ -1108,11 +1101,17 @@
             self.total[rows, :] = self.spare[rows, :] + self.rx[k, rows].astype(f32)
 
     def one_end(self, part):
+        self.line_here(0)
         self.end_z(0, self.d, part, self.total)
 
+    def turn(self, n):
+        return twin(self.a, LINES - 1 - n % LINES)
+
+    def row_turn(self, n):
+        return 2 * self.turn(n) + self.b + (1 - 2 * self.b) * (1 - n // LINES)
+
     def one_far(self, n, part):
-        t = in_turn(n)
-        row = 2 * t + self.b + (1 - 2 * self.b) * (1 - n // LINES)
+        row = self.row_turn(n)
         dd = self.far
         self.by_core(row, dd, part).wait_recv()
         self.add(slot(row, dd), part, self.rc.at[dd // 2 * MPS + row])
@@ -1137,19 +1136,20 @@
 
     def drain_tree(self, core, dd, part):
         k = dd // 2 if core == 0 else 0
-        a = self.a
-        for t in range(LINES):
-            self.by_y(k, t, dd, part).wait_send()
-            pl.when(t < a)(functools.partial(self.wait_z, k, t, dd, 1, part))
-            pl.when(t > a)(functools.partial(self.wait_z, k, t, dd, 0, part))
+        for n in range(LINES):
+            self.drain_place(k, self.turn(n), dd, part)
         if core == 0:
-            pl.when(self.d != dd)(lambda: self.by_x(k, slot(self.m, dd), part).wait_send())
+            self.drain_end(dd, part)
         else:
             for row in range(MPS):
                 self.by_x(row, slot(row, self.far), part).wait_send()
 
-    def wait_z(self, k, t, dd, side, part):
-        self.by_z(k, t, dd, side, part, self.to_left if side else self.to_right).wait_send()
+    def drain_place(self, k, t, dd, part):
+        self.by_y(k, t, dd, part).wait_send()
+        pl.when(t != self.a)(lambda: self.by_z(k, t, dd, part).wait_send())
+
+    def drain_end(self, dd, part):
+        pl.when(self.d != dd)(lambda: self.by_x(dd // 2, slot(self.m, dd), part).wait_send())
 
 
 WHOLE = ((0, 0, QROWS),)
@@ -1197,182 +1197,180 @@
 
 def flat_grads(total, smalls, fl, roll, head, head_sem, wide, tall, gflat):
     d, m, *_ = place()
-    fl[768:792, :] = jnp.zeros((24, 128), f32)
+    back = remote(fl.at[0:8], head.at[1, 0:8], head_sem.at[2], head_sem.at[3], {"dp": (d + DPS - 1) % DPS, "mp": m})
 
     def put(start, size, step, val):
         fl[pl.ds(start, size, stride=step), :] = val
 
-    @pl.when(d == 0)
-    def _():
-        tall[192:256, :] = jnp.zeros((64, C), f32)
-        for half in range(2):
-            for kind in range(3):
-                for i in range(2):
-                    frm = half * 192 + kind * 64 + i * 32
-                    to = i * 96 + kind * 32
-                    tall[to : to + 32, HALVES[half]] = total[frm : frm + 32, :]
-        wide[0:C, :] = tall[0:128, :].T
-        wide[C : 2 * C, :] = tall[128:256, :].T
-        low = iota((256, 128), 1) < 64
-
-        def every(start):
-            return wide[pl.ds(start, 256, stride=2), :]
-
-        one, two = pltpu.roll(every(1), 64, 1), pltpu.roll(every(C + 1), 64, 1)
-        put(0, 256, 3, every(0))
-        put(1, 256, 3, jnp.where(low, every(C), one))
-        put(2, 256, 3, jnp.where(low, one, two))
-
-    @pl.when(d == 1)
-    def _():
-        for j in range(2):
-            js = slice(j * 128, (j + 1) * 128)
+    def rest():
+        fl[768:792, :] = jnp.zeros((24, 128), f32)
+
+        @pl.when(d == 1)
+        def _():
+            for j in range(2):
+                js = slice(j * 128, (j + 1) * 128)
+                for half in range(2):
+                    put(2 * half + j, 64, 4, total[half * 64 : half * 64 + 64, js])
+                put(256 + j, 256, 2, total[128:384, js])
+
+        @pl.when(d == 2)
+        def _():
+            for j in range(2):
+                js = slice(j * 128, (j + 1) * 128)
+                put(j, 256, 2, total[0:256, js])
+                for half in range(2):
+                    at = 256 + half * 64
+                    put(512 + 2 * half + j, 64, 4, total[at : at + 64, js])
+
+        @pl.when(d == 3)
+        def _():
+            for j in range(2):
+                js = slice(j * 128, (j + 1) * 128)
+                for half in range(2):
+                    put(2 * half + j, 192, 4, total[half * 192 : half * 192 + 192, js])
+
+        pl.when(d > 0)(lambda: back.start())
+
+    def first():
+        @pl.when(d == 0)
+        def _():
+            tall[192:256, :] = jnp.zeros((64, C), f32)
             for half in range(2):
-                put(2 * half + j, 64, 4, total[half * 64 : half * 64 + 64, js])
-            put(256 + j, 256, 2, total[128:384, js])
-
-    @pl.when(d == 2)
-    def _():
-        for j in range(2):
-            js = slice(j * 128, (j + 1) * 128)
-            put(j, 256, 2, total[0:256, js])
-            for half in range(2):
-                at = 256 + half * 64
-                put(512 + 2 * half + j, 64, 4, total[at : at + 64, js])
-
-    @pl.when(d == 3)
-    def _():
-        for j in range(2):
-            js = slice(j * 128, (j + 1) * 128)
-            for half in range(2):
-                put(2 * half + j, 192, 4, total[half * 192 : half * 192 + 192, js])
-        fl[768:784, :] = smalls[...]
-
-    back = remote(fl.at[0:8], head.at[1, 0:8], head_sem.at[2], head_sem.at[3], {"dp": (d + DPS - 1) % DPS, "mp": m})
-
-    @pl.when(d > 0)
-    def _():
-        back.start()
-
-    @pl.when(d < DPS - 1)
-    def _():
-        back.wait_recv()
-        fl[768:776, :] = head[1, 0:8, :]
-
-    lane = iota((FLAT, 128), 1)
-    for k in range(DPS):
-
-        @pl.when(d == k)
-        def _(k=k):
-            lanes, down = OFFSET * k % 128, OFFSET * k // 128
-            if k == 0:
-                gflat[...] = fl[0:FLAT, :]
-            else:
-                roll[0:784, :] = pltpu.roll(fl[0:784, :], 128 - lanes, 1)
-                roll[784:792, :] = jnp.zeros((8, 128), f32)
-                gflat[...] = jnp.where(lane < 128 - lanes, roll[down : down + FLAT, :], roll[down + 1 : down + 1 + FLAT, :])
-
-    @pl.when(d > 0)
-    def _():
-        back.wait_send()
+                for kind in range(3):
+                    for i in range(2):
+                        frm = half * 192 + kind * 64 + i * 32
+                        to = i * 96 + kind * 32
+                        tall[to : to + 32, HALVES[half]] = total[frm : frm + 32, :]
+            wide[0:C, :] = tall[0:128, :].T
+            wide[C : 2 * C, :] = tall[128:256, :].T
+            low = iota((256, 128), 1) < 64
+
+            def every(start):
+                return wide[pl.ds(start, 256, stride=2), :]
+
+            one, two = pltpu.roll(every(1), 64, 1), pltpu.roll(every(C + 1), 64, 1)
+            put(0, 256, 3, every(0))
+            put(1, 256, 3, jnp.where(low, every(C), one))
+            put(2, 256, 3, jnp.where(low, one, two))
+
+    def end():
+        @pl.when(d == DPS - 1)
+        def _():
+            fl[768:784, :] = smalls[...]
+
+        @pl.when(d < DPS - 1)
+        def _():
+            back.wait_recv()
+            fl[768:776, :] = head[1, 0:8, :]
+
+        lane = iota((FLAT, 128), 1)
+        for k in range(DPS):
+
+            @pl.when(d == k)
+            def _(k=k):
+                lanes, down = OFFSET * k % 128, OFFSET * k // 128
+                if k == 0:
+                    gflat[...] = fl[0:FLAT, :]
+                else:
+                    roll[0:784, :] = pltpu.roll(fl[0:784, :], 128 - lanes, 1)
+                    roll[784:792, :] = jnp.zeros((8, 128), f32)
+                    gflat[...] = jnp.where(lane < 128 - lanes, roll[down : down + FLAT, :], roll[down + 1 : down + 1 + FLAT, :])
+
+    def drain():
+        pl.when(d > 0)(lambda: back.wait_send())
+
+    return rest, first, end, drain
 
 
 def step_kernel(images, rows, length, *refs):
     (nlive, x, cot, pf, sel, mask) = refs[:6]
     (out, gin, gflat) = refs[6:9]
     (
-        fl, roll, head, wide, tall, wb, sm, vecs, b1, tabs, tabs2, bias, gvec, gb1, acc, gb, gsm, got, part, got2,
+        fl, roll, head, wide, tall, wb, sm, vecs, b1, tabs, tabs2, bias, gvec, gb1, acc, gb, gsm, got, part_sm, got2,
         stotal, rc, rx, ry, rz, total, spare,
         head_sem, sm_s, sm_r, ag_s, ag_r, rsm_s, rsm_r, rsm_r2, s_core, r_core, s_x, r_x, s_y, r_y, s_z, r_z,
     ) = refs[9:52]
-    ln1, qkv, wq, probs, mixw, mixed, ln2, act, gpre, gresb, gres, gmix, gwin, goutb = refs[52:]
+    ln1, qkv, wq, probs, mixed, ln2, act, gpre, gresb, gres, gmix, gl1, goutb = refs[52:]
     greet()
     flatten_params(pf, fl, roll, head, head_sem, wide, wb, sm)
     outs = BlocksOut(wb, ag_s, ag_r)
-    c = outs.c
-    zero, one = c == 0, c == 1
-    pl.when(zero)(lambda: outs.line(0, 0, 0))
+    zero, one = outs.c == 0, outs.c == 1
+    pl.when(zero)(lambda: outs.origin_out(0))
     finish_sm, drain_sm = smalls_out(sm, sm_s, sm_r)
-
-    @pl.when(zero)
-    def _():
-        outs.line(0, 0, 1)
-        outs.side(0, 0, 0)
-
+    pl.when(zero)(lambda: outs.origin_in(0))
     finish_sm()
     gather_smalls(sm, vecs, b1, tabs, bias, mask)
-
-    @pl.when(zero)
-    def _():
-        outs.line(0, 0, 2)
-        outs.side(0, 0, 1)
-
     first_norm(x, vecs, ln1)
-
-    @pl.when(zero)
-    def _():
-        outs.line(0, 0, 3)
-        outs.side(0, 0, 2)
-        outs.side(0, 0, 3)
-
-    @pl.when(one)
-    def _():
-        outs.from_core(0)
-        outs.line(1, outs.d, 0)
 
     def two(fn, *args):
         return functools.partial(fn, 0, 2, *args)
 
+    def qk(fn, j):
+        return functools.partial(fn, 0, 0, j)
+
     def mine(fn, *args):
         return functools.partial(fn, 1, outs.d, *args)
 
     def cross(j, same):
         return functools.partial(outs.cross, j, same)
 
+    def run(fns):
+        for fn in fns:
+            fn()
+
+    def at_point(zeros, ones, point):
+        if point in zeros:
+            pl.when(zero)(lambda: run(zeros[point]))
+        if point in ones:
+            pl.when(one)(lambda: run(ones[point]))
+
+    def poll(zeros, ones, point, now):
+        for k in sorted(set(zeros) | set(ones)):
+            if 0 <= k < 4 * images:
+                pl.when(now == k)(functools.partial(at_point, zeros, ones, k))
+
     zero_at = {
-        1: [two(outs.line, 0)],
-        4: [two(outs.line, 1)],
-        5: [two(outs.side, 0)],
-        8: [two(outs.line, 2)],
-        9: [two(outs.side, 1)],
-        12: [two(outs.line, 3)],
-        13: [two(outs.side, 2)],
-        17: [two(outs.side, 3)],
+        0: [qk(outs.line, 1), qk(outs.side, 0)],
+        1: [qk(outs.line, 2)],
+        2: [qk(outs.line, 3), functools.partial(outs.origin_out, 2)],
+        4: [qk(outs.side, 1)],
+        7: [functools.partial(outs.origin_in, 2)],
+        8: [qk(outs.side, 2)],
+        10: [two(outs.line, 1)],
+        11: [two(outs.side, 0)],
+        12: [qk(outs.side, 3), two(outs.line, 2)],
+        14: [two(outs.line, 3)],
+        15: [two(outs.side, 1)],
+        16: [two(outs.side, 2), two(outs.side, 3)],
     }
     one_at = {
-        4: [mine(outs.line, 1)],
-        5: [mine(outs.side, 0)],
-        6: [cross(0, True)],
-        8: [mine(outs.line, 2)],
-        9: [mine(outs.side, 1)],
-        10: [cross(1, True), cross(0, False)],
-        12: [mine(outs.line, 3), mine(outs.side, 2)],
-        14: [cross(2, True), cross(1, False)],
-        17: [mine(outs.side, 3)],
-        19: [cross(3, True), cross(2, False)],
-        21: [cross(3, False)],
+        0: [functools.partial(outs.group_from_core, 0, 0)],
+        1: [outs.own],
+        4: [functools.partial(outs.group_from_core, 0, 1)],
+        6: [mine(outs.line, 1)],
+        7: [mine(outs.side, 0)],
+        8: [functools.partial(outs.group_from_core, 0, 2), cross(0, True)],
+        9: [mine(outs.line, 2)],
+        10: [mine(outs.side, 1)],
+        11: [mine(outs.line, 3)],
+        12: [functools.partial(outs.group_from_core, 0, 3), cross(1, True), cross(0, False)],
+        13: [mine(outs.side, 2)],
+        14: [cross(1, False)],
+        15: [mine(outs.side, 3), cross(2, True)],
+        16: [cross(3, True), cross(2, False), cross(3, False)],
     }
-
-    def run(zeros, ones):
-        if zeros:
-            pl.when(zero)(lambda: [fn() for fn in zeros] and None)
-        if ones:
-            pl.when(one)(lambda: [fn() for fn in ones] and None)
-
-    def at_point(zero_table, one_table, point):
-        run(zero_table.get(point), one_table.get(point))
-
-    def poll_project(n):
-        at_point(zero_at, one_at, n)
-
-    def poll_forward(i, w):
-        for k in range(NW):
-            point = 6 + NW * i + k
-            if point in zero_at or point in one_at:
-                pl.when(w == k)(functools.partial(at_point, zero_at, one_at, point))
-
-    project_qkv(wb, vecs, ln1, qkv, poll_project)
-    attention_forward(images, length, sel, bias, qkv, wq, probs, mixw, mixed, poll_forward)
+    mixed[...] = jnp.zeros_like(mixed)
+
+    def forward(n, _):
+        j, i = n // images, n % images
+        g = twin(outs.a, j)
+        poll(zero_at, one_at, None, n)
+        pl.when(i == 0)(lambda: project_group(g, wb, vecs, ln1, qkv))
+        attend(i, g, length, sel, bias, qkv, wq, probs, mixed)
+        return 0
+
+    lax.fori_loop(0, NG * images, forward, 0)
+    at_point(zero_at, one_at, 16)
 
     @pl.when(zero)
     def _():
@@ -1390,109 +1388,115 @@
     )
     whole = WHOLE[0]
 
-    def hand_over(row):
+    def grads(n, _):
+        row = ins.row_turn(n)
+        feed_forward_grads(row, gb, act, goutb, ln2, gpre)
+
         @pl.when(zero)
         def _():
             for dd in (1, 3):
                 ins.by_core(row, dd, whole).start()
 
         pl.when(one)(lambda: ins.by_core(row, 2, whole).start())
-
-    def grads(n, _):
-        t = in_turn(n)
-        row = 2 * t + ins.b + (1 - 2 * ins.b) * (1 - n // LINES)
-        feed_forward_grads(row, gb, act, goutb, ln2, gpre)
-        hand_over(row)
-
-        @pl.when((n >= 1) & one)
-        def _():
-            ins.one_far(n - 1, whole)
-
-        @pl.when((n >= 1) & (n <= LINES) & zero)
-        def _():
-            ins.zero_over(2, in_turn(n - 1), whole)
-
+        pl.when((n >= 1) & one)(lambda: ins.one_far(n - 1, whole))
+        pl.when((n >= 1) & (n <= LINES) & zero)(lambda: ins.zero_over(2, ins.turn(n - 1), whole))
         return 0
 
     lax.fori_loop(0, MPS, grads, 0)
-
-    turn = [in_turn(n) for n in range(LINES)]
+    turn = [ins.turn(n) for n in range(LINES)]
+
+    def step(fn, *args):
+        return functools.partial(fn, *args, whole)
+
+    lay_rest, lay_first, lay_end, drain_lay = flat_grads(
+        total, stotal, fl, roll, head, head_sem, wide, tall, gflat
+    )
     zero_at = {
-        3: [functools.partial(ins.zero_own, 2, turn[0], whole)],
-        5: [functools.partial(ins.zero_own, 2, turn[1], whole)],
-        7: [functools.partial(ins.zero_own, 2, turn[2], whole)],
-        9: [functools.partial(ins.zero_own, 2, turn[3], whole)],
-        13: [functools.partial(ins.zero_end, 2, whole)],
+        1: [step(ins.zero_own, 2, turn[0])],
+        2: [step(ins.zero_own, 2, turn[1])],
+        3: [step(ins.zero_own, 2, turn[2])],
+        4: [step(ins.zero_own, 2, turn[3])],
+        5: [step(ins.zero_over, 0, turn[0])],
+        9: [step(ins.zero_own, 0, turn[0]), step(ins.zero_over, 0, turn[1])],
+        11: [functools.partial(ins.line_here, 1), step(ins.zero_end, 2)],
+        13: [step(ins.zero_own, 0, turn[1]), step(ins.zero_over, 0, turn[2])],
     }
     one_at = {
-        0: [functools.partial(ins.one_far, MPS - 1, whole)],
-        1: [functools.partial(ins.one_over, turn[0], whole)],
-        2: [functools.partial(ins.one_over, turn[1], whole)],
-        4: [functools.partial(ins.one_over, turn[2], whole)],
-        5: [functools.partial(ins.one_over, turn[3], whole)],
-        8: [functools.partial(ins.one_own, turn[0], whole)],
-        10: [functools.partial(ins.one_own, turn[1], whole)],
-        12: [functools.partial(ins.one_own, turn[2], whole)],
-        14: [functools.partial(ins.one_own, turn[3], whole)],
+        0: [step(ins.one_far, MPS - 1)],
+        1: [step(ins.one_over, turn[0])],
+        2: [step(ins.one_over, turn[1])],
+        3: [step(ins.one_over, turn[2])],
+        4: [step(ins.one_over, turn[3])],
+        7: [step(ins.one_own, turn[0])],
+        9: [step(ins.one_own, turn[1])],
+        10: [step(ins.one_own, turn[2])],
+        11: [step(ins.one_own, turn[3])],
     }
-
-    def poll_backward(i, w):
-        for k in range(NW):
-            point = NW * i + k
-            if point in zero_at or point in one_at:
-                pl.when(w == k)(functools.partial(at_point, zero_at, one_at, point))
-
-    attention_backward(images, length, sel, gmix, wq, probs, mixw, gwin, qkv, acc, gvec, poll_backward)
-
-    order = (0, 1, 3, 2)
-
-    def hand_first(rows_of):
-        @pl.when(one)
+    acc[...] = jnp.zeros_like(acc)
+    gvec[2:4, :] = jnp.zeros((2, C), f32)
+    gl1[...] = jnp.zeros_like(gl1)
+
+    def backward(n, _):
+        j, i = n // images, n % images
+        g = ins.turn(j)
+        poll(zero_at, one_at, None, n)
+
+        @pl.when(i == 0)
         def _():
-            for row in rows_of:
-                for part in PARTS:
-                    ins.by_core(row, 0, part).start()
-
-    qkv_grads(0, gb, qkv, ln1)
-    hand_first(range(MPS // 2))
-    qkv_grads(1, gb, qkv, ln1)
-    hand_first(range(MPS // 2, MPS))
-    def both_parts(fn, t):
-        return [functools.partial(fn, 0, t, part) for part in PARTS]
-
-    zero_at = {
-        0: both_parts(ins.zero_over, order[0]),
-        1: both_parts(ins.zero_over, order[1]),
-        2: both_parts(ins.zero_over, order[2]),
-        3: both_parts(ins.zero_over, order[3]),
-        5: both_parts(ins.zero_own, order[0]),
-    }
-    one_at = {0: [functools.partial(ins.one_end, whole)]}
-    first_norm_back(x, wb, vecs, qkv, gres, gin, gvec, functools.partial(at_point, zero_at, one_at))
+            qkv[...] = jnp.zeros_like(qkv)
+
+        attend_back(i, g, length, sel, gmix, wq, probs, qkv, acc, gvec)
+
+        @pl.when((i == images - 1) & (j < NG - 1))
+        def _():
+            group_grads(g, gb, qkv, ln1)
+
+            @pl.when(one)
+            def _():
+                for r in range(2):
+                    ins.by_core(2 * g + r, 0, whole).start()
+
+            group_norm_grad(g, wb, qkv, gl1)
+
+        return 0
+
+    lax.fori_loop(0, NG * images, backward, 0)
+    own = ins.a
+    group_grads(own, gb, qkv, ln1)
+
+    @pl.when(one)
+    def _():
+        for same in (0, 1):
+            for part in PARTS:
+                ins.by_core(2 * own + (1 - ins.b if same == 0 else ins.b), 0, part).start()
+
+    pl.when(zero)(lambda: ins.zero_own(0, turn[2], whole))
     scatter_smalls(gvec, gb1, acc, gsm, tabs2)
-    mid_sm, end_sm, drain_in = smalls_in(gsm, got, part, got2, stotal, rsm_s, rsm_r, rsm_r2)
-
-    @pl.when(zero)
-    def _():
-        for fn in both_parts(ins.zero_own, order[1]):
-            fn()
-
-    mid_sm()
-
-    @pl.when(zero)
-    def _():
-        for t in order[2:]:
-            for fn in both_parts(ins.zero_own, t):
-                fn()
-
-    end_sm()
 
     @pl.when(zero)
     def _():
         for part in PARTS:
+            ins.zero_over(0, own, part)
+
+    group_norm_grad(own, wb, qkv, gl1)
+    first_norm_sums(x, gl1, gvec)
+    scatter_first(gvec, gsm)
+    mid_sm, end_sm, drain_in = smalls_in(gsm, got, part_sm, got2, stotal, rsm_s, rsm_r, rsm_r2)
+    pl.when(one)(lambda: ins.one_end(whole))
+    lay_rest()
+    first_norm_back(x, vecs, gl1, gres, gin)
+
+    @pl.when(zero)
+    def _():
+        ins.line_here(0)
+        for part in PARTS:
+            ins.zero_own(0, own, part)
             ins.zero_end(0, part)
 
-    flat_grads(total, stotal, fl, roll, head, head_sem, wide, tall, gflat)
+    mid_sm()
+    lay_first()
+    end_sm()
+    lay_end()
 
     @pl.when(zero)
     def _():
@@ -1500,17 +1504,25 @@
             for dd in (1, 3):
                 ins.by_core(row, dd, whole).wait_send()
         ins.drain_tree(0, 2, whole)
+        for n in range(LINES - 1):
+            ins.drain_place(0, turn[n], 0, whole)
         for part in PARTS:
-            ins.drain_tree(0, 0, part)
+            ins.drain_place(0, own, 0, part)
+            ins.drain_end(0, part)
 
     @pl.when(one)
     def _():
         for row in range(MPS):
             ins.by_core(row, 2, whole).wait_send()
+        for n in range(LINES - 1):
+            for r in range(2):
+                ins.by_core(2 * turn[n] + r, 0, whole).wait_send()
+        for r in range(2):
             for part in PARTS:
-                ins.by_core(row, 0, part).wait_send()
+                ins.by_core(2 * own + r, 0, part).wait_send()
         ins.drain_tree(1, ins.d, whole)
 
+    drain_lay()
     drain_in()
     outs.drain()
     drain_sm()
@@ -1557,13 +1569,13 @@
             pltpu.VMEM((2 * MPS, QROWS, 256), bf16),
             pltpu.VMEM((MPS, QROWS, 256), bf16),
             pltpu.VMEM((2 * LINES, QROWS, 256), bf16),
-            pltpu.VMEM((4 * LINES, QROWS, 256), bf16),
+            pltpu.VMEM((2 * LINES, QROWS, 256), bf16),
             pltpu.VMEM((QROWS, 256), f32),
             pltpu.VMEM((QROWS, 256), f32),
             dma((4,)),
             dma((3 + MPS,)),
             dma((MPS,)),
-            dma((nb, 5)),
+            dma((nb, 6)),
             dma((nb,)),
             dma((MPS,)),
             dma((MPS,)),
@@ -1574,8 +1586,8 @@
             dma((MPS, 2)),
             dma((2 * LINES, 2)),
             dma((2 * LINES, 2)),
-            dma((4 * LINES, 2)),
-            dma((4 * LINES, 2)),
+            dma((2 * LINES, 2)),
+            dma((2 * LINES, 2)),
         ]
         + mega_scratch(images, rows),
         compiler_params=pltpu.CompilerParams(

time: 180 us -> 134 us (0.74)
  the two profiles are of different devices: /device:TPU:25 before, /device:TPU:0 now
where the time goes in v4:
time: 134 us
  Pallas kernels  122 us (91%)
  other arithmetic  5.39 us (4%)
  local copies, waits for them, and re-layouts  4.99 us (4%)
  between operations  1.35 us (1%)
    pallas_call x1, Pallas kernels, step_call(): pl.pallas_call(functools.partial(step_kernel, images, rows, length), out_...  122 us
    sub x1, other arithmetic, finish(): params - learn_rate * (corrected_one / (jnp.sqrt(corrected_two) + adam_ep...  4.75 us
    unnamed x14, local copies, waits for them, and re-layouts  2.97 us

profile of v4, /device:TPU:0, one launch (start us, length us, event | category | flops | bytes accessed | tf_op | source)
XLA Modules:
  0.0 134.0 jit_solution(14939757696302635354)
XLA Ops:
  0.6 0.0 copy-start.5
  0.6 0.6 copy-done.5
  1.3 0.6 fusion.3
  2.6 2.0 %pad.4 = f32[1,99328]{1,0:T(1,128)} pad(f32[1,98581]{1,0:T(1,128)} %param.11, f32[]{:T(128)} %constant.14.clone.1), padding=0_0x0_747 | pad | bytes 791640 | tf_op jit(solution)/shard_map/jit(_pad)/pad | solution.py:1721
  4.6 0.0 copy-start
  4.6 0.0 copy-start.3
  4.6 0.0 copy-start.4
  4.6 122.2 %shard_map.127 = (bf16[784,512]{1,0:T(8,128)(2,1)}, bf16[784,512]{1,0:T(8,128)(2,1)}, f32[776,128]{1,0:T(8,128)}) custom-call(s32[1]{0:T(128)} %bitcast.refs_0_, bf16[784,512]{1,0:T(8,128)(2,1)} %refs_1_.1, bf16[784,512]{1,0:T(8,128)(2,1)} %refs_2_.1, f32[776,128]{1,0:T(8,128)} %bitcast.3, bf16[4,256,208]{2,1,0:T(8,128)(2,1)} %constant.43.clone.refs_4_, ...), custom_call_target="tpu_custom_call" | custom-call | tf_op jit(solution)/shard_map/pallas_call | solution.py:1542
  126.8 0.0 copy-done
  126.9 0.0 copy-done.3
  126.9 0.0 copy-done.4
  126.9 0.0 copy-start.2
  126.9 4.8 %multiply_subtract_fusion = (f32[1,98581]{1,0:T(1,128)}, f32[1,98581]{1,0:T(1,128)}, f32[1,98581]{1,0:T(1,128)}, f32[1,98581]{1,0:T(1,128)}) fusion(f32[1,98581]{1,0:T(1,128)S(1)} %copy-done, s32[]{:T(128)S(6)} %mul.56, f32[1,98581]{1,0:T(1,128)S(1)} %copy-done.3, f32[1,98581]{1,0:T(1,128)S(1)} %copy-done.4, f32[1,99328]{1,0:T(1,128)} %bitcast.4), kind=kLoop, calls=%fused_computation.5 | loop fusion | flops 1774458 | bytes 3154596 | tf_op jit(solution)/shard_map/sub | solution.py:1650
  131.6 0.0 copy-done.2
  131.6 0.0 copy-start.1
  131.6 0.9 copy.16
  132.5 0.5 copy-done.1
  133.1 0.9 copy.17
Async XLA Ops:
  0.6 0.7 copy-start.5
  4.6 122.2 %copy-start = (f32[1,98581]{1,0:T(1,128)S(1)}, f32[1,98581]{1,0:T(1,128)}, u32[]{:S(2)}) copy-start(f32[1,98581]{1,0:T(1,128)} %param.11) | copy-start | bytes 1182976
  4.6 122.2 %copy-start.3 = (f32[1,98581]{1,0:T(1,128)S(1)}, f32[1,98581]{1,0:T(1,128)}, u32[]{:S(2)}) copy-start(f32[1,98581]{1,0:T(1,128)} %param.12) | copy-start | bytes 1182976
  4.6 122.3 %copy-start.4 = (f32[1,98581]{1,0:T(1,128)S(1)}, f32[1,98581]{1,0:T(1,128)}, u32[]{:S(2)}) copy-start(f32[1,98581]{1,0:T(1,128)} %param.13) | copy-start | bytes 1182976
  126.9 4.8 %copy-start.2 = (bf16[784,512]{1,0:T(8,128)(2,1)S(1)}, bf16[784,512]{1,0:T(8,128)(2,1)}, u32[]{:S(2)}) copy-start(bf16[784,512]{1,0:T(8,128)(2,1)} %get-tuple-element.22) | copy-start | bytes 2408452
  131.6 1.4 %copy-start.1 = (bf16[784,512]{1,0:T(8,128)(2,1)S(1)}, bf16[784,512]{1,0:T(8,128)(2,1)}, u32[]{:S(2)}) copy-start(bf16[784,512]{1,0:T(8,128)(2,1)} %get-tuple-element.23) | copy-start | bytes 2408452

commit v5 on v4

--- a/solution.py
+++ b/solution.py
@@ -797,19 +797,6 @@
                     lane >= lanes, roll[8 : 8 + FLAT, :], roll[7 : 7 + FLAT, :]
                 )
 
-    greeted()
-    over = remote(fl.at[768:784], head.at[0], head_sem.at[0], head_sem.at[1], {"dp": (d + 1) % DPS, "mp": m})
-
-    @pl.when(d < DPS - 1)
-    def _():
-        over.start()
-
-    @pl.when(d > 0)
-    def _():
-        over.wait_recv()
-        pos = iota((8, 128), 0) * 128 + iota((8, 128), 1)
-        fl[0:8, :] = jnp.where(pos < OFFSET * d, head[0, 0:8, :], fl[0:8, :])
-
     def cut(start, size, step):
         return fl[pl.ds(start, size, stride=step), :]
 
@@ -830,75 +817,87 @@
                     frm = i * 96 + kind * 32
                     wb[s, to : to + 32, :] = turned[frm : frm + 32, HALVES[half]]
 
-    @pl.when(d == 1)
+    @pl.when(d == DPS - 1)
     def _():
-        s = slot(m, 1)
-        for j in range(2):
-            js = slice(j * 128, (j + 1) * 128)
-            for half in range(2):
-                wb[s, half * 64 : half * 64 + 64, js] = cut(2 * half + j, 64, 4).astype(bf16)
-            wb[s, 128:384, js] = cut(256 + j, 256, 2).astype(bf16)
-
-    @pl.when(d == 2)
-    def _():
-        s = slot(m, 2)
-        for j in range(2):
-            js = slice(j * 128, (j + 1) * 128)
-            wb[s, 0:256, js] = cut(j, 256, 2).astype(bf16)
-            for half in range(2):
-                at = 256 + half * 64
-                wb[s, at : at + 64, js] = cut(512 + 2 * half + j, 64, 4).astype(bf16)
-
-    @pl.when(d == 3)
-    def _():
-        s = slot(m, 3)
-        for j in range(2):
-            js = slice(j * 128, (j + 1) * 128)
-            for half in range(2):
-                wb[s, half * 192 : half * 192 + 192, js] = cut(2 * half + j, 192, 4).astype(bf16)
         sm[m] = fl[768:784, :].astype(bf16)
 
-    @pl.when(d < DPS - 1)
-    def _():
-        over.wait_send()
+    over = remote(fl.at[768:784], head.at[0], head_sem.at[0], head_sem.at[1], {"dp": (d + 1) % DPS, "mp": m})
+
+    def rest():
+        @pl.when(d > 0)
+        def _():
+            over.wait_recv()
+            pos = iota((8, 128), 0) * 128 + iota((8, 128), 1)
+            fl[0:8, :] = jnp.where(pos < OFFSET * d, head[0, 0:8, :], fl[0:8, :])
+
+        @pl.when(d == 1)
+        def _():
+            s = slot(m, 1)
+            for j in range(2):
+                js = slice(j * 128, (j + 1) * 128)
+                for half in range(2):
+                    wb[s, half * 64 : half * 64 + 64, js] = cut(2 * half + j, 64, 4).astype(bf16)
+                wb[s, 128:384, js] = cut(256 + j, 256, 2).astype(bf16)
+
+        @pl.when(d == 2)
+        def _():
+            s = slot(m, 2)
+            for j in range(2):
+                js = slice(j * 128, (j + 1) * 128)
+                wb[s, 0:256, js] = cut(j, 256, 2).astype(bf16)
+                for half in range(2):
+                    at = 256 + half * 64
+                    wb[s, at : at + 64, js] = cut(512 + 2 * half + j, 64, 4).astype(bf16)
+
+        @pl.when(d == 3)
+        def _():
+            s = slot(m, 3)
+            for j in range(2):
+                js = slice(j * 128, (j + 1) * 128)
+                for half in range(2):
+                    wb[s, half * 192 : half * 192 + 192, js] = cut(2 * half + j, 192, 4).astype(bf16)
+
+        pl.when(d < DPS - 1)(lambda: over.wait_send())
+
+    return lambda: pl.when(d < DPS - 1)(lambda: over.start()), rest
 
 
 def smalls_out(sm, ssem, rsem):
     d, m, *_ = place()
+    last = d == DPS - 1
+
+    def over_mp(k):
+        return remote(sm.at[m], sm.at[m], ssem.at[k], rsem.at[m], {"dp": d, "mp": (m + k) % MPS})
 
     def over_dp(k):
-        return remote(sm.at[m], sm.at[m], ssem.at[k], rsem.at[m], {"dp": k, "mp": m})
-
-    def over_mp(k):
-        return remote(sm.at[m], sm.at[m], ssem.at[3 + k], rsem.at[m], {"dp": d, "mp": (m + k) % MPS})
-
-    @pl.when(d == DPS - 1)
-    def _():
-        for k in range(DPS - 1):
-            over_dp(k).start()
-
-    @pl.when(d < DPS - 1)
-    def _():
-        over_dp(0).wait_recv()
-
-    for k in range(1, MPS):
-        over_mp(k).start()
+        return remote(sm, sm, ssem.at[MPS + k], rsem.at[MPS], {"dp": k, "mp": m})
+
+    def begin():
+        @pl.when(last)
+        def _():
+            for k in range(1, MPS):
+                over_mp(k).start()
 
     def finish():
-        for k in range(1, MPS):
-            src = (m + k) % MPS
-            remote(sm.at[src], sm.at[src], ssem.at[0], rsem.at[src], {"dp": d, "mp": src}).wait_recv()
+        @pl.when(last)
+        def _():
+            for k in range(1, MPS):
+                src = (m + k) % MPS
+                remote(sm.at[src], sm.at[src], ssem.at[0], rsem.at[src], {"dp": d, "mp": src}).wait_recv()
+            for k in range(DPS - 1):
+                over_dp(k).start()
+
+        pl.when(d < DPS - 1)(lambda: over_dp(0).wait_recv())
 
     def drain():
-        @pl.when(d == DPS - 1)
-        def _():
+        @pl.when(last)
+        def _():
+            for k in range(1, MPS):
+                over_mp(k).wait_send()
             for k in range(DPS - 1):
                 over_dp(k).wait_send()
 
-        for k in range(1, MPS):
-            over_mp(k).wait_send()
-
-    return finish, drain
+    return begin, finish, drain
 
 
 SIDE_Z, SIDE_Y, SIDE_X, CORE = 0, 3, 4, 5
@@ -919,7 +918,7 @@
             self.dev[SIDE_Z + j - 1] = {"dp": d, "mp": 2 * twin(self.a, j) + b}
 
     def copy(self, s, way):
-        return remote(self.wb.at[s], self.wb.at[s], self.ssem.at[s, way], self.rsem.at[s], self.dev[way])
+        return remote(self.wb.at[s], self.wb.at[s], self.ssem.at[0], self.rsem.at[s], self.dev[way])
 
     def arrive(self, s):
         self.copy(s, CORE).wait_recv()
@@ -934,14 +933,11 @@
         for way in ways:
             self.copy(s, way).start()
 
-    def settle(self, s, ways):
-        for way in ways:
-            self.copy(s, way).wait_send()
+    def origin_x(self, dd):
+        pl.when(self.d == dd)(lambda: self.start(slot(self.m, dd), [SIDE_X]))
 
     def origin_out(self, dd):
-        @pl.when(self.d == dd)
-        def _():
-            self.start(slot(self.m, dd), [SIDE_X] + self.own_ways(0))
+        pl.when(self.d == dd)(lambda: self.start(slot(self.m, dd), self.own_ways(0)))
 
     def origin_in(self, dd):
         @pl.when(self.d != dd)
@@ -983,32 +979,19 @@
         self.arrive(slot(self.row(j, False), dd))
 
     def drain(self):
-        @pl.when(self.c == 0)
-        def _():
-            for dd in (0, 2):
-                pl.when(self.d == dd)(lambda: self.copy(slot(self.m, dd), SIDE_X).wait_send())
-                self.settle(slot(self.m, dd), self.own_ways(0))
-                for j in range(LINES):
-                    if j:
-                        self.settle(slot(self.row(j, True), dd), self.line_ways(0))
-                    self.settle(slot(self.row(j, False), dd), self.side_ways(0))
-
-        @pl.when(self.c == 1)
-        def _():
-            self.settle(slot(self.m, self.d), self.own_ways(1))
-            for j in range(LINES):
-                if j:
-                    self.settle(slot(self.row(j, True), self.d), self.line_ways(1))
-                self.settle(slot(self.row(j, False), self.d), self.side_ways(1))
-                for same in (True, False):
-                    self.settle(slot(self.row(j, same), self.far), [CORE])
+        sent_all(self.wb, self.ssem, self.dev[CORE])
+
+
+def sent_all(blocks, sem, dev):
+    span = blocks.at[pl.ds(0, MPS * DPS - 1)]
+    remote(span, span, sem.at[0], sem.at[0], dev).wait_send()
 
 
 class BlocksIn:
-    def __init__(self, gb, rc, rx, ry, rz, total, spare, sems):
+    def __init__(self, gb, rc, rx, ry, rz, total, spare, sent, sems):
         self.gb, self.rc, self.rx, self.ry, self.rz = gb, rc, rx, ry, rz
         self.total, self.spare = total, spare
-        self.sems = sems
+        self.sent, self.sems = sent, sems
         self.d, self.m, self.x, self.c, self.a, self.b = place()
         d, m, b, c = self.d, self.m, self.b, self.c
         self.far = (d + 2) % DPS
@@ -1018,9 +1001,8 @@
         self.to_y = {"dp": d, "mp": m + 1 - 2 * b}
 
     def move(self, s, dst, name, k, part, dev):
-        ss, rs = self.sems[name]
         rows = pl.ds(*part[1:])
-        return remote(self.gb.at[s, rows], dst.at[rows], ss.at[k, part[0]], rs.at[k, part[0]], dev)
+        return remote(self.gb.at[s, rows], dst.at[rows], self.sent.at[0], self.sems[name].at[k, part[0]], dev)
 
     def by_core(self, row, dd, part):
         k = dd // 2 * MPS + row
@@ -1033,19 +1015,18 @@
         return self.move(slot(2 * t + 1 - self.b, dd), self.ry.at[k * LINES + t], "y", k * LINES + t, part, self.to_y)
 
     def by_z(self, k, t, dd, part):
-        ss, rs = self.sems["z"]
         rows = pl.ds(*part[1:])
         n = k * LINES + self.a
         return remote(
             self.gb.at[slot(2 * t + self.b, dd), rows],
             self.rz.at[n].at[rows],
-            ss.at[k * LINES + t, part[0]],
-            rs.at[n, part[0]],
+            self.sent.at[0],
+            self.sems["z"].at[n, part[0]],
             {"dp": self.d, "mp": 2 * t + self.b},
         )
 
     def from_z(self, k, t, part):
-        _, rs = self.sems["z"]
+        rs = self.sems["z"]
         ref = self.rz.at[k * LINES + t].at[pl.ds(*part[1:])]
         remote(ref, ref, rs.at[k * LINES + t, part[0]], rs.at[k * LINES + t, part[0]], self.to_y).wait_recv()
 
@@ -1097,8 +1078,15 @@
 
         @pl.when(self.d == dd)
         def _():
-            self.by_x(k, s, part).wait_recv()
-            self.total[rows, :] = self.spare[rows, :] + self.rx[k, rows].astype(f32)
+            self.total[rows, :] = self.spare[rows, :]
+
+    def zero_take(self, dd, part):
+        rows = pl.ds(*part[1:])
+
+        @pl.when(self.d == dd)
+        def _():
+            self.by_x(dd // 2, slot(self.m, dd), part).wait_recv()
+            self.total[rows, :] += self.rx[dd // 2, rows].astype(f32)
 
     def one_end(self, part):
         self.line_here(0)
@@ -1134,22 +1122,8 @@
         self.add(slot(row, dd), part, self.rc.at[dd // 2 * MPS + row], self.rx.at[row], self.ry.at[t])
         self.along_z(0, t, dd, part)
 
-    def drain_tree(self, core, dd, part):
-        k = dd // 2 if core == 0 else 0
-        for n in range(LINES):
-            self.drain_place(k, self.turn(n), dd, part)
-        if core == 0:
-            self.drain_end(dd, part)
-        else:
-            for row in range(MPS):
-                self.by_x(row, slot(row, self.far), part).wait_send()
-
-    def drain_place(self, k, t, dd, part):
-        self.by_y(k, t, dd, part).wait_send()
-        pl.when(t != self.a)(lambda: self.by_z(k, t, dd, part).wait_send())
-
-    def drain_end(self, dd, part):
-        pl.when(self.d != dd)(lambda: self.by_x(dd // 2, slot(self.m, dd), part).wait_send())
+    def drain(self):
+        sent_all(self.gb, self.sent, self.to_core)
 
 
 WHOLE = ((0, 0, QROWS),)
@@ -1283,24 +1257,51 @@
 
 
 def step_kernel(images, rows, length, *refs):
-    (nlive, x, cot, pf, sel, mask) = refs[:6]
-    (out, gin, gflat) = refs[6:9]
+    (counts, *far_in) = refs[:6]
+    (*far_out, gflat) = refs[6:9]
     (
         fl, roll, head, wide, tall, wb, sm, vecs, b1, tabs, tabs2, bias, gvec, gb1, acc, gb, gsm, got, part_sm, got2,
         stotal, rc, rx, ry, rz, total, spare,
-        head_sem, sm_s, sm_r, ag_s, ag_r, rsm_s, rsm_r, rsm_r2, s_core, r_core, s_x, r_x, s_y, r_y, s_z, r_z,
-    ) = refs[9:52]
-    ln1, qkv, wq, probs, mixed, ln2, act, gpre, gresb, gres, gmix, gl1, goutb = refs[52:]
+        head_sem, sm_s, sm_r, ag_s, ag_r, rsm_s, rsm_r, rsm_r2, sent, r_core, r_x, r_y, r_z,
+    ) = refs[9:49]
+    (x, cot, pf, sel, mask, out, gin, near_sem) = refs[49:57]
+    ln1, qkv, wq, probs, mixed, ln2, act, gpre, gresb, gres, gmix, gl1, goutb = refs[57:]
+    x_in, cot_in, pf_in, sel_in, mask_in = (
+        pltpu.make_async_copy(src, dst, near_sem.at[n]) for n, (src, dst) in enumerate(zip(far_in, (x, cot, pf, sel, mask)))
+    )
+    out_back = pltpu.make_async_copy(out, far_out[0], near_sem.at[5])
+    gin_back = pltpu.make_async_copy(gin, far_out[1], near_sem.at[6])
     greet()
-    flatten_params(pf, fl, roll, head, head_sem, wide, wb, sm)
+    for copy in (pf_in, mask_in, x_in, sel_in, cot_in):
+        copy.start()
+    pf_in.wait()
+    hand_tail, flatten_rest = flatten_params(pf, fl, roll, head, head_sem, wide, wb, sm)
     outs = BlocksOut(wb, ag_s, ag_r)
     zero, one = outs.c == 0, outs.c == 1
-    pl.when(zero)(lambda: outs.origin_out(0))
-    finish_sm, drain_sm = smalls_out(sm, sm_s, sm_r)
-    pl.when(zero)(lambda: outs.origin_in(0))
+    begin_sm, finish_sm, drain_sm = smalls_out(sm, sm_s, sm_r)
+    greeted()
+    hand_tail()
+    begin_sm()
+
+    @pl.when(zero)
+    def _():
+        outs.origin_x(0)
+        outs.origin_out(0)
+
+    flatten_rest()
+    pl.when(one)(lambda: outs.own())
+
+    @pl.when(zero)
+    def _():
+        outs.origin_x(2)
+        outs.origin_in(0)
+
     finish_sm()
+    mask_in.wait()
     gather_smalls(sm, vecs, b1, tabs, bias, mask)
+    x_in.wait()
     first_norm(x, vecs, ln1)
+    sel_in.wait()
 
     def two(fn, *args):
         return functools.partial(fn, 0, 2, *args)
@@ -1324,47 +1325,51 @@
         if point in ones:
             pl.when(one)(lambda: run(ones[point]))
 
-    def poll(zeros, ones, point, now):
-        for k in sorted(set(zeros) | set(ones)):
-            if 0 <= k < 4 * images:
-                pl.when(now == k)(functools.partial(at_point, zeros, ones, k))
+    def poll(zeros, ones, j, i):
+        points = set(zeros) | set(ones)
+
+        def group(jj):
+            for ii in range(images):
+                if images * jj + ii in points:
+                    pl.when(i == ii)(functools.partial(at_point, zeros, ones, images * jj + ii))
+
+        for jj in range(NG):
+            if points & set(range(images * jj, images * jj + images)):
+                pl.when(j == jj)(functools.partial(group, jj))
 
     zero_at = {
-        0: [qk(outs.line, 1), qk(outs.side, 0)],
-        1: [qk(outs.line, 2)],
-        2: [qk(outs.line, 3), functools.partial(outs.origin_out, 2)],
+        0: [functools.partial(outs.origin_out, 2), qk(outs.line, 1), qk(outs.side, 0)],
+        1: [qk(outs.line, 2), functools.partial(outs.origin_in, 2)],
+        2: [qk(outs.line, 3)],
         4: [qk(outs.side, 1)],
-        7: [functools.partial(outs.origin_in, 2)],
+        5: [two(outs.line, 1)],
+        6: [two(outs.side, 0)],
+        7: [two(outs.line, 2)],
         8: [qk(outs.side, 2)],
-        10: [two(outs.line, 1)],
-        11: [two(outs.side, 0)],
-        12: [qk(outs.side, 3), two(outs.line, 2)],
-        14: [two(outs.line, 3)],
-        15: [two(outs.side, 1)],
-        16: [two(outs.side, 2), two(outs.side, 3)],
+        9: [two(outs.line, 3)],
+        10: [two(outs.side, 1)],
+        12: [qk(outs.side, 3), two(outs.side, 2)],
+        14: [two(outs.side, 3)],
     }
     one_at = {
-        0: [functools.partial(outs.group_from_core, 0, 0)],
-        1: [outs.own],
-        4: [functools.partial(outs.group_from_core, 0, 1)],
-        6: [mine(outs.line, 1)],
-        7: [mine(outs.side, 0)],
-        8: [functools.partial(outs.group_from_core, 0, 2), cross(0, True)],
-        9: [mine(outs.line, 2)],
-        10: [mine(outs.side, 1)],
-        11: [mine(outs.line, 3)],
-        12: [functools.partial(outs.group_from_core, 0, 3), cross(1, True), cross(0, False)],
-        13: [mine(outs.side, 2)],
-        14: [cross(1, False)],
-        15: [mine(outs.side, 3), cross(2, True)],
-        16: [cross(3, True), cross(2, False), cross(3, False)],
+        0: [mine(outs.line, 1), mine(outs.side, 0), functools.partial(outs.group_from_core, 0, 0)],
+        1: [cross(0, True)],
+        2: [mine(outs.line, 2)],
+        4: [functools.partial(outs.group_from_core, 0, 1), mine(outs.side, 1)],
+        5: [mine(outs.line, 3)],
+        6: [cross(1, True), cross(0, False)],
+        7: [mine(outs.side, 2)],
+        8: [functools.partial(outs.group_from_core, 0, 2), cross(2, True), cross(1, False)],
+        10: [mine(outs.side, 3), cross(3, True)],
+        12: [functools.partial(outs.group_from_core, 0, 3), cross(2, False)],
+        14: [cross(3, False)],
     }
     mixed[...] = jnp.zeros_like(mixed)
 
     def forward(n, _):
         j, i = n // images, n % images
         g = twin(outs.a, j)
-        poll(zero_at, one_at, None, n)
+        poll(zero_at, one_at, j, i)
         pl.when(i == 0)(lambda: project_group(g, wb, vecs, ln1, qkv))
         attend(i, g, length, sel, bias, qkv, wq, probs, mixed)
         return 0
@@ -1379,12 +1384,14 @@
 
     pl.when(one)(lambda: outs.from_core(2))
 
+    cot_in.wait()
     feed_forward(
-        rows, nlive[0], x, cot, wb, vecs, b1, out, gvec, gb1, mixed, ln2, act, gpre, gresb, gres, gmix, goutb
+        rows, counts[outs.d] * PIX - outs.m * rows, x, cot, wb, vecs, b1, out, gvec, gb1, mixed, ln2, act, gpre, gresb, gres, gmix, goutb
     )
+    out_back.start()
     proj_grads(gb, mixed, gresb)
     ins = BlocksIn(
-        gb, rc, rx, ry, rz, total, spare, {"core": (s_core, r_core), "x": (s_x, r_x), "y": (s_y, r_y), "z": (s_z, r_z)}
+        gb, rc, rx, ry, rz, total, spare, sent, {"core": r_core, "x": r_x, "y": r_y, "z": r_z}
     )
     whole = WHOLE[0]
 
@@ -1417,9 +1424,12 @@
         3: [step(ins.zero_own, 2, turn[2])],
         4: [step(ins.zero_own, 2, turn[3])],
         5: [step(ins.zero_over, 0, turn[0])],
-        9: [step(ins.zero_own, 0, turn[0]), step(ins.zero_over, 0, turn[1])],
-        11: [functools.partial(ins.line_here, 1), step(ins.zero_end, 2)],
-        13: [step(ins.zero_own, 0, turn[1]), step(ins.zero_over, 0, turn[2])],
+        8: [step(ins.zero_own, 0, turn[0])],
+        9: [step(ins.zero_over, 0, turn[1])],
+        14: [functools.partial(ins.line_here, 1), step(ins.zero_end, 2)],
+        12: [step(ins.zero_own, 0, turn[1])],
+        13: [step(ins.zero_over, 0, turn[2])],
+        15: [step(ins.zero_own, 0, turn[2])],
     }
     one_at = {
         0: [step(ins.one_far, MPS - 1)],
@@ -1439,7 +1449,7 @@
     def backward(n, _):
         j, i = n // images, n % images
         g = ins.turn(j)
-        poll(zero_at, one_at, None, n)
+        poll(zero_at, one_at, j, i)
 
         @pl.when(i == 0)
         def _():
@@ -1470,7 +1480,6 @@
             for part in PARTS:
                 ins.by_core(2 * own + (1 - ins.b if same == 0 else ins.b), 0, part).start()
 
-    pl.when(zero)(lambda: ins.zero_own(0, turn[2], whole))
     scatter_smalls(gvec, gb1, acc, gsm, tabs2)
 
     @pl.when(zero)
@@ -1483,8 +1492,10 @@
     scatter_first(gvec, gsm)
     mid_sm, end_sm, drain_in = smalls_in(gsm, got, part_sm, got2, stotal, rsm_s, rsm_r, rsm_r2)
     pl.when(one)(lambda: ins.one_end(whole))
+    pl.when(zero)(lambda: ins.zero_take(2, whole))
     lay_rest()
     first_norm_back(x, vecs, gl1, gres, gin)
+    gin_back.start()
 
     @pl.when(zero)
     def _():
@@ -1494,41 +1505,26 @@
             ins.zero_end(0, part)
 
     mid_sm()
+
+    @pl.when(zero)
+    def _():
+        for part in PARTS:
+            ins.zero_take(0, part)
+
     lay_first()
     end_sm()
     lay_end()
 
-    @pl.when(zero)
-    def _():
-        for row in range(MPS):
-            for dd in (1, 3):
-                ins.by_core(row, dd, whole).wait_send()
-        ins.drain_tree(0, 2, whole)
-        for n in range(LINES - 1):
-            ins.drain_place(0, turn[n], 0, whole)
-        for part in PARTS:
-            ins.drain_place(0, own, 0, part)
-            ins.drain_end(0, part)
-
-    @pl.when(one)
-    def _():
-        for row in range(MPS):
-            ins.by_core(row, 2, whole).wait_send()
-        for n in range(LINES - 1):
-            for r in range(2):
-                ins.by_core(2 * turn[n] + r, 0, whole).wait_send()
-        for r in range(2):
-            for part in PARTS:
-                ins.by_core(2 * own + r, 0, part).wait_send()
-        ins.drain_tree(1, ins.d, whole)
-
+    ins.drain()
+    out_back.wait()
+    gin_back.wait()
     drain_lay()
     drain_in()
     outs.drain()
     drain_sm()
 
 
-def step_call(x, cot, nlive, pf):
+def step_call(x, cot, counts, pf):
     rows = x.shape[0]
     images = rows // PIX
     length = image_frames(images)[2]
@@ -1536,14 +1532,15 @@
     mask = jnp.asarray(score_masks(), f32)
     vmem = pl.BlockSpec(memory_space=pltpu.VMEM)
     smem = pl.BlockSpec(memory_space=pltpu.SMEM)
+    far = pl.BlockSpec(memory_space=pl.ANY)
     s = jax.ShapeDtypeStruct
     dma = pltpu.SemaphoreType.DMA
     nb = MPS * DPS
     return pl.pallas_call(
         functools.partial(step_kernel, images, rows, length),
         out_shape=(s((rows, C), bf16), s((rows, C), bf16), s((FLAT, 128), f32)),
-        in_specs=[smem] + [vmem] * 5,
-        out_specs=(vmem,) * 3,
+        in_specs=[smem] + [far] * 5,
+        out_specs=(far, far, vmem),
         scratch_shapes=[
             pltpu.VMEM((792, 128), f32),
             pltpu.VMEM((792, 128), f32),
@@ -1573,27 +1570,32 @@
             pltpu.VMEM((QROWS, 256), f32),
             pltpu.VMEM((QROWS, 256), f32),
             dma((4,)),
-            dma((3 + MPS,)),
-            dma((MPS,)),
-            dma((nb, 6)),
+            dma((MPS + DPS - 1,)),
+            dma((MPS + 1,)),
+            dma((1,)),
             dma((nb,)),
             dma((MPS,)),
             dma((MPS,)),
             dma((DPS,)),
+            dma((1,)),
             dma((2 * MPS, 2)),
-            dma((2 * MPS, 2)),
-            dma((MPS, 2)),
             dma((MPS, 2)),
             dma((2 * LINES, 2)),
             dma((2 * LINES, 2)),
-            dma((2 * LINES, 2)),
-            dma((2 * LINES, 2)),
+            pltpu.VMEM((rows, C), bf16),
+            pltpu.VMEM((rows, C), bf16),
+            pltpu.VMEM((FLAT, 128), f32),
+            pltpu.VMEM((images, NW * SEG, length), bf16),
+            pltpu.VMEM((NW, SEG, GH * SEG), f32),
+            pltpu.VMEM((rows, C), bf16),
+            pltpu.VMEM((rows, C), bf16),
+            dma((7,)),
         ]
         + mega_scratch(images, rows),
         compiler_params=pltpu.CompilerParams(
             vmem_limit_bytes=62 * 1024 * 1024, collective_id=0, has_side_effects=True
         ),
-    )(nlive, x, cot, pf, sel, mask)
+    )(counts, x, cot, pf, sel, mask)
 
 
 VEC_LABELS = [
@@ -1712,14 +1714,8 @@
     )
     if not fits:
         return local_xla(tokens, cotangent, image_counts, params, moment_one, moment_two)
-    rank = lax.axis_index("mp")
-    group = lax.axis_index("dp")
-    limit = jnp.sum(
-        jnp.where(jnp.arange(image_counts.shape[0], dtype=jnp.int32) == group, image_counts, 0)
-    )
-    nlive = jnp.clip(limit * PIX - rank * rows, 0, rows).reshape(1)
     pf = jnp.pad(params, ((0, 0), (0, FLAT * 128 - shard))).reshape(FLAT, 128)
-    output, grad_input, gflat = step_call(tokens, cotangent, nlive, pf)
+    output, grad_input, gflat = step_call(tokens, cotangent, image_counts, pf)
     grad_shard = gflat.reshape(1, -1)[:, :shard]
     return finish(output, grad_input, grad_shard, params, moment_one, moment_two)
 

time: 134 us -> 120 us (0.90)
  Pallas kernels: 122 us -> 109 us
    pallas_call x1, Pallas kernels: 122 us -> 109 us  [step_call(): pl.pallas_call(functools.partial(step_kernel, images, rows, length), out_...]
    unnamed x14 -> x12, local copies, waits for them, and re-layouts: 2.97 us -> 2.33 us
where the time goes in v5:
time: 120 us; the launch traced here: 119 us
  Pallas kernels  109 us (91%)
  other arithmetic  4.75 us (4%)
  local copies, waits for them, and re-layouts  4.34 us (4%)
    pallas_call x1, Pallas kernels, step_call(): pl.pallas_call(functools.partial(step_kernel, images, rows, length), out_...  109 us
    sub x1, other arithmetic, finish(): params - learn_rate * (corrected_one / (jnp.sqrt(corrected_two) + adam_ep...  4.75 us

profile of v5, /device:TPU:0, one launch (start us, length us, event | category | flops | bytes accessed | tf_op | source)
XLA Modules:
  0.0 118.8 jit_solution(16517257054293427964)
XLA Ops:
  0.6 2.0 %pad.4 = f32[1,99328]{1,0:T(1,128)} pad(f32[1,98581]{1,0:T(1,128)} %param.11, f32[]{:T(128)} %constant.14.clone.1), padding=0_0x0_747 | pad | bytes 791640 | tf_op jit(solution)/shard_map/jit(_pad)/pad | solution.py:1717
  2.7 0.0 copy-start
  2.7 0.0 copy-start.3
  2.7 0.0 copy-start.4
  2.7 109.0 %shard_map.127 = (bf16[784,512]{1,0:T(8,128)(2,1)}, bf16[784,512]{1,0:T(8,128)(2,1)}, f32[776,128]{1,0:T(8,128)}) custom-call(s32[4]{0:T(128)} %refs_0_.1, bf16[784,512]{1,0:T(8,128)(2,1)} %refs_1_.1, bf16[784,512]{1,0:T(8,128)(2,1)} %refs_2_.1, f32[776,128]{1,0:T(8,128)} %bitcast.2, bf16[4,256,208]{2,1,0:T(8,128)(2,1)} %constant.35.clone.refs_4_, ...), custom_call_target="tpu_custom_call" | custom-call | tf_op jit(solution)/shard_map/pallas_call | solution.py:1539
  111.7 0.0 copy-done
  111.7 0.0 copy-done.3
  111.7 0.0 copy-done.4
  111.7 0.0 copy-start.2
  111.7 4.8 %multiply_subtract_fusion = (f32[1,98581]{1,0:T(1,128)}, f32[1,98581]{1,0:T(1,128)}, f32[1,98581]{1,0:T(1,128)}, f32[1,98581]{1,0:T(1,128)}) fusion(f32[1,98581]{1,0:T(1,128)S(1)} %copy-done, s32[]{:T(128)S(6)} %mul.48, f32[1,98581]{1,0:T(1,128)S(1)} %copy-done.3, f32[1,98581]{1,0:T(1,128)S(1)} %copy-done.4, f32[1,99328]{1,0:T(1,128)} %bitcast.3), kind=kLoop, calls=%fused_computation.5 | loop fusion | flops 1774458 | bytes 3154596 | tf_op jit(solution)/shard_map/sub | solution.py:1652
  116.5 0.0 copy-done.2
  116.5 0.0 copy-start.1
  116.5 0.9 copy.16
  117.4 0.5 copy-done.1
  117.9 0.9 copy.17
Async XLA Ops:
  2.7 109.0 %copy-start = (f32[1,98581]{1,0:T(1,128)S(1)}, f32[1,98581]{1,0:T(1,128)}, u32[]{:S(2)}) copy-start(f32[1,98581]{1,0:T(1,128)} %param.11) | copy-start | bytes 1182976
  2.7 109.0 %copy-start.3 = (f32[1,98581]{1,0:T(1,128)S(1)}, f32[1,98581]{1,0:T(1,128)}, u32[]{:S(2)}) copy-start(f32[1,98581]{1,0:T(1,128)} %param.12) | copy-start | bytes 1182976
  2.7 109.0 %copy-start.4 = (f32[1,98581]{1,0:T(1,128)S(1)}, f32[1,98581]{1,0:T(1,128)}, u32[]{:S(2)}) copy-start(f32[1,98581]{1,0:T(1,128)} %param.13) | copy-start | bytes 1182976
  111.7 4.8 %copy-start.2 = (bf16[784,512]{1,0:T(8,128)(2,1)S(1)}, bf16[784,512]{1,0:T(8,128)(2,1)}, u32[]{:S(2)}) copy-start(bf16[784,512]{1,0:T(8,128)(2,1)} %get-tuple-element.22) | copy-start | bytes 2408452
  116.5 1.4 %copy-start.1 = (bf16[784,512]{1,0:T(8,128)(2,1)S(1)}, bf16[784,512]{1,0:T(8,128)(2,1)}, u32[]{:S(2)}) copy-start(bf16[784,512]{1,0:T(8,128)(2,1)} %get-tuple-element.23) | copy-start | bytes 2408452
